TPU v7x, 256 devices: a whole 4x4x8 slice. The times are simulated.
256 devices in a mesh: patch: 128 (over y, z, x), pix: 2 (over core).
Axes of the slice: x: 4, y: 4, z: 8, core: 2. Of those that a mesh axis runs over, the one named last changes fastest.
Arguments:
- pixel_pos: float32 [2, 24576], P(None, ('patch', 'pix')), may hold values from -4 to 4
- pixel_view: float32 [3, 24576], P(None, ('patch', 'pix')), may hold values from -1 to 1
- observed: float32 [24576], P(('patch', 'pix')), may hold values from -6 to 6
- noise_scale: float32 [24576], P(('patch', 'pix')), may hold values from 0.5 to 2
- valid_mask: int32 [24576], P(('patch', 'pix')), may hold values 0 or 1
- patch_pos: float32 [2, 6144], P(None, 'patch'), may hold values from -4 to 4
- patch_depth: float32 [6144], P('patch'), may hold values from 0.3 to 1.5
- segment_ids: int32 [6144], P('patch'), may hold values from 0 to 15, never falling along the last dimension, each value on 1 to 1536 neighbouring positions
- seg_strike: float32 [16], replicated, may hold values from -3.140625 to 3.140625
- seg_dip: float32 [16], replicated, may hold values from 0.35 to 1.4
- slip_models: bfloat16 [6144, 3, 128], P('patch'), may hold values from -0.8984375 to 0.8984375
Outputs:
- residual: float32 [24576, 128], P(('patch', 'pix'))
- misfit: float32 [128], replicated
Inputs may be any that keep to these rules, and one draw needn't show every extreme that they name: `segment_ids`: segment ids never fall along the patches.
All inputs are finite; a program needn't handle non-finite values. No bound on the sum of `valid_mask` on one device may be relied on, other than what follows from the above.
Results may differ from a plain program's by a relative error of at most 0.0003.
Values may be sent and summed in bfloat16 or wider, within the bound.
No kernel may reach another device: no remote copies, remote signals or barrier semaphores. Data moves between devices by JAX's collectives and lax.ppermute only.
A program may use at most 64 MiB of HBM per device.

v0:
```python
import functools
import math

import jax
import jax.numpy as jnp
from jax import lax
from jax.sharding import Mesh
from jax.sharding import PartitionSpec as P

PATCH = ("patch_0", "patch_1", "patch_2")
PATCH_PIX = ("patch_0", "patch_1", "patch_2", "pix")


two_pi = 2.0 * math.pi
mu_ratio = 0.5


def partner(value, axis, distance):
    mask = 2**distance
    pairs = [(source, source ^ mask) for source in range(lax.axis_size(axis))]
    return lax.ppermute(value, axis, pairs)


def one_axis_at_a_time(value, axes):
    return functools.reduce(lax.psum, axes, value)


def point_green(pixel_pos, pixel_view, frame_rows):
    src_east = frame_rows[0][:, None]
    src_north = frame_rows[1][:, None]
    src_depth = frame_rows[2][:, None]
    sin_strike = frame_rows[3][:, None]
    cos_strike = frame_rows[4][:, None]
    sin_dip = frame_rows[5][:, None]
    cos_dip = frame_rows[6][:, None]
    east_gap = pixel_pos[0][None, :] - src_east
    north_gap = pixel_pos[1][None, :] - src_north
    along_x = east_gap * sin_strike + north_gap * cos_strike
    across = north_gap * sin_strike - east_gap * cos_strike
    depth_term = across * cos_dip + src_depth * sin_dip
    plane_term = across * sin_dip - src_depth * cos_dip
    radius = jnp.sqrt(along_x * along_x + across * across + src_depth * src_depth)
    over_r = 1.0 / radius
    over_r3 = over_r * over_r * over_r
    over_r5 = over_r3 * over_r * over_r
    over_rd = 1.0 / (radius + src_depth)
    base_term = over_r * over_rd * over_rd
    cubic_term = (3.0 * radius + src_depth) * over_r3 * over_rd * over_rd * over_rd
    square_term = (2.0 * radius + src_depth) * over_r3 * over_rd * over_rd
    term_one = mu_ratio * across * (base_term - along_x * along_x * cubic_term)
    term_two = mu_ratio * along_x * (base_term - across * across * cubic_term)
    term_three = mu_ratio * along_x * over_r3 - term_two
    term_four = -mu_ratio * along_x * across * square_term
    term_five = mu_ratio * (over_r * over_rd - along_x * along_x * square_term)
    scaled_q = 3.0 * plane_term * over_r5
    dip_mixed = sin_dip * cos_dip
    dip_square = sin_dip * sin_dip
    strike_x = -(scaled_q * along_x * along_x + term_one * sin_dip)
    strike_y = -(scaled_q * along_x * across + term_two * sin_dip)
    strike_z = -(scaled_q * along_x * src_depth + term_four * sin_dip)
    dip_x = -(scaled_q * along_x * depth_term - term_three * dip_mixed)
    dip_y = -(scaled_q * across * depth_term - term_one * dip_mixed)
    dip_z = -(scaled_q * src_depth * depth_term - term_five * dip_mixed)
    open_x = scaled_q * along_x * plane_term - term_three * dip_square
    open_y = scaled_q * across * plane_term - term_one * dip_square
    open_z = scaled_q * src_depth * plane_term - term_five * dip_square

    def project(comp_x, comp_y, comp_z):
        east_move = comp_x * sin_strike - comp_y * cos_strike
        north_move = comp_x * cos_strike + comp_y * sin_strike
        return (
            pixel_view[0][None, :] * east_move
            + pixel_view[1][None, :] * north_move
            + pixel_view[2][None, :] * comp_z
        ) / two_pi

    return jnp.stack(
        [
            project(strike_x, strike_y, strike_z),
            project(dip_x, dip_y, dip_z),
            project(open_x, open_y, open_z),
        ],
        axis=1,
    )


def local_frames(patch_pos, patch_depth, segment_ids, seg_strike, seg_dip):
    segment_count = seg_strike.shape[0]
    matches = segment_ids[:, None] == jnp.arange(segment_count, dtype=jnp.int32)[None, :]
    strike = jnp.sum(jnp.where(matches, seg_strike[None, :], 0.0), axis=1)
    dip_angle = jnp.sum(jnp.where(matches, seg_dip[None, :], 0.0), axis=1)
    return jnp.stack(
        [
            patch_pos[0],
            patch_pos[1],
            patch_depth,
            jnp.sin(strike),
            jnp.cos(strike),
            jnp.sin(dip_angle),
            jnp.cos(dip_angle),
        ],
        axis=0,
    )


def tile_product(site_pos, site_view, frame_rows, slip_table):
    pixel_count = site_pos.shape[1]
    green_tile = point_green(site_pos, site_view, frame_rows).astype(jnp.bfloat16)
    green_tile = green_tile.reshape(frame_rows.shape[1] * 3, pixel_count)
    return lax.dot_general(
        green_tile, slip_table, (((0,), (0,)), ((), ())), preferred_element_type=jnp.float32
    )


def patch_blocks(pixel_pos, pixel_view, frame_rows, slip_piece, running):
    patch_count = slip_piece.shape[0]
    samples = slip_piece.shape[2]
    block_len = min(patch_count, 640)
    full_blocks = patch_count // block_len
    remainder = patch_count - full_blocks * block_len
    head = full_blocks * block_len
    head_frames = frame_rows[:, :head].reshape(7, full_blocks, block_len).transpose(1, 0, 2)
    head_slip = slip_piece[:head].reshape(full_blocks, block_len * 3, samples)

    def add_tile(accum, block_items):
        return (accum + tile_product(pixel_pos, pixel_view, block_items[0], block_items[1]), None)

    running, _ = lax.scan(add_tile, running, (head_frames, head_slip))
    tail_slip = slip_piece[head:].reshape(remainder * 3, samples)
    running = running + tile_product(pixel_pos, pixel_view, frame_rows[:, head:], tail_slip)
    return running


def index_bit(level):
    return lax.axis_index(PATCH) // 2**level % 2 == 1


def join_pair(mine, other, upper, axis_dim):
    first = jnp.where(upper, other, mine)
    second = jnp.where(upper, mine, other)
    return jnp.concatenate([first, second], axis=axis_dim)


def per_device(
    pixel_pos,
    pixel_view,
    observed,
    noise_scale,
    valid_mask,
    patch_pos,
    patch_depth,
    segment_ids,
    seg_strike,
    seg_dip,
    slip_models,
):
    own_pixels = pixel_pos.shape[1]
    samples = slip_models.shape[2]
    frames = local_frames(patch_pos, patch_depth, segment_ids, seg_strike, seg_dip)
    total_bits = lax.axis_size(PATCH).bit_length() - 1
    low_count = (total_bits + 1) // 2
    group_slip = slip_models
    group_frames = frames
    for level in range(low_count):
        upper = index_bit(level)
        other_slip = partner(group_slip, PATCH, level)
        other_frames = partner(group_frames, PATCH, level)
        group_slip = join_pair(group_slip, other_slip, upper, 0)
        group_frames = join_pair(group_frames, other_frames, upper, 1)
    group_sites = jnp.concatenate([pixel_pos, pixel_view], axis=0)
    for level in range(low_count, total_bits):
        upper = index_bit(level)
        other_sites = partner(group_sites, PATCH, level)
        group_sites = join_pair(group_sites, other_sites, upper, 1)
    site_groups = group_sites.shape[1] // own_pixels
    stacked = group_sites.reshape(5, site_groups, own_pixels).transpose(1, 0, 2)

    def one_group(block_sites):
        start = jnp.zeros((own_pixels, samples), jnp.float32)
        return patch_blocks(block_sites[:2], block_sites[2:], group_frames, group_slip, start)

    partial_value = lax.map(one_group, stacked).reshape(site_groups * own_pixels, samples)
    for level in range(total_bits - 1, low_count - 1, -1):
        upper = index_bit(level)
        half = partial_value.shape[0] // 2
        keep = jnp.where(upper, partial_value[half:], partial_value[:half])
        send = jnp.where(upper, partial_value[:half], partial_value[half:])
        partial_value = keep + partner(send, PATCH, level)
    residual = (
        valid_mask.astype(jnp.float32)[:, None]
        * (partial_value - observed[:, None])
        / noise_scale[:, None]
    )
    own_sum = jnp.sum(residual * residual, axis=0)
    pixels = own_pixels * lax.axis_size(PATCH) * lax.axis_size("pix")
    misfit = one_axis_at_a_time(own_sum, PATCH_PIX) / pixels
    return (residual, misfit)


def solution(mesh):
    finer = Mesh(
        mesh.devices.reshape(4, 8, 4, mesh.shape["pix"]), ("patch_0", "patch_1", "patch_2", "pix")
    )
    placed = (
        P(None, PATCH_PIX),
        P(None, PATCH_PIX),
        P(PATCH_PIX),
        P(PATCH_PIX),
        P(PATCH_PIX),
        P(None, PATCH),
        P(PATCH),
        P(PATCH),
        P(),
        P(),
        P(PATCH, None, None),
    )
    return jax.shard_map(
        per_device,
        mesh=finer,
        in_specs=placed,
        out_specs=(P(PATCH_PIX, None), P()),
        check_vma=False,
    )
```

profile of v0, /device:TPU:1, one launch (start us, length us, event | category | flops | bytes accessed | tf_op | source)
XLA Modules:
  0.0 130.1 jit_solution(3404055132361483055)
XLA Ops:
  0.6 2.1 %collective-permute-start.7 = (bf16[48,3,128]{2,0,1:T(8,128)(2,1)}, bf16[48,3,128]{2,0,1:T(8,128)(2,1)S(1)}, u32[]{:S(2)}, u32[]{:S(2)}) collective-permute-start(bf16[48,3,128]{2,0,1:T(8,128)(2,1)} %param.23), channel_id=1, source_target_pairs={{0,2},{2,0},{4,6},{6,4},{8,10},{10,8},{12,14},{14,12},{16,18},{18,... | collective-permute-start | bytes 110600 | tf_op jit(solution)/shard_map/ppermute | solution.py:21
  2.8 0.8 select_reduce_fusion
  3.6 0.7 stack.32
  4.4 0.7 pad_maximum_fusion.10
  5.1 7.1 %collective-permute-start = (f32[5,96]{1,0:T(8,128)S(1)}, f32[5,96]{1,0:T(8,128)S(1)}, u32[]{:S(2)}, u32[]{:S(2)}) collective-permute-start(f32[5,96]{1,0:T(8,128)S(1)} %pad_maximum_fusion.10), channel_id=1, source_target_pairs={{0,32},{2,34},{4,36},{6,38},{8,40},{10,42},{12,44},{14,46},{16,48}... | collective-permute-start | bytes 5768 | tf_op jit(solution)/shard_map/ppermute | solution.py:21
  12.3 2.8 %collective-permute-start.4 = (f32[7,96]{1,0:T(8,128)S(1)}, f32[7,96]{1,0:T(8,128)S(1)}, u32[]{:S(2)}, u32[]{:S(2)}) collective-permute-start(f32[7,96]{1,0:T(8,128)S(1)} %pad_maximum_fusion.11), channel_id=1, source_target_pairs={{0,4},{2,6},{4,0},{6,2},{8,12},{10,14},{12,8},{14,10},{16,20},{18,... | collective-permute-start | bytes 8072 | tf_op jit(solution)/shard_map/ppermute | solution.py:21
  15.1 0.7 broadcast_select_fusion.21
  15.9 1.3 %collective-permute-start.1 = (f32[5,192]{1,0:T(8,128)S(1)}, f32[5,192]{1,0:T(8,128)S(1)}, u32[]{:S(2)}, u32[]{:S(2)}) collective-permute-start(f32[5,192]{1,0:T(8,128)S(1)} %pad_maximum_fusion.8), channel_id=1, source_target_pairs={{0,64},{2,66},{4,68},{6,70},{8,72},{10,74},{12,76},{14,78},{16,80}... | collective-permute-start | bytes 11528 | tf_op jit(solution)/shard_map/ppermute | solution.py:21
  17.3 0.8 collective-permute-start.5
  18.1 0.5 collective-permute-done.1
  18.7 2.9 %collective-permute-start.2 = (f32[5,384]{1,0:T(8,128)S(1)}, f32[5,384]{1,0:T(8,128)S(1)}, u32[]{:S(2)}, u32[]{:S(2)}) collective-permute-start(f32[5,384]{1,0:T(8,128)S(1)} %pad_maximum_fusion.6), channel_id=1, source_target_pairs={{0,128},{2,130},{4,132},{6,134},{8,136},{10,138},{12,140},{14,142}... | collective-permute-start | bytes 23048 | tf_op jit(solution)/shard_map/ppermute | solution.py:21
  21.8 1.2 collective-permute-start.6
  23.2 2.1 %collective-permute-done.6 = f32[7,384]{1,0:T(8,128)S(1)} collective-permute-done((f32[7,384]{1,0:T(8,128)S(1)}, f32[7,384]{1,0:T(8,128)S(1)}, u32[]{:S(2)}, u32[]{:S(2)}) %collective-permute-start.6) | collective-permute-done | bytes 10784 | tf_op jit(solution)/shard_map/ppermute | solution.py:21
  25.4 1.5 %collective-permute-start.8 = (bf16[96,3,128]{2,0,1:T(8,128)(2,1)S(1)}, bf16[96,3,128]{2,0,1:T(8,128)(2,1)S(1)}, u32[]{:S(2)}, u32[]{:S(2)}) collective-permute-start(bf16[96,3,128]{2,0,1:T(8,128)(2,1)S(1)} %pad_maximum_fusion.3), channel_id=1, source_target_pairs={{0,4},{2,6},{4,0},{6,2},{8,12},{10,14},{12,8},{14,10},{16,20},{18,... | collective-permute-start | bytes 221192 | tf_op jit(solution)/shard_map/ppermute | solution.py:21
  26.9 3.3 %collective-permute-done.8 = bf16[96,3,128]{2,0,1:T(8,128)(2,1)S(1)} collective-permute-done((bf16[96,3,128]{2,0,1:T(8,128)(2,1)S(1)}, bf16[96,3,128]{2,0,1:T(8,128)(2,1)S(1)}, u32[]{:S(2)}, u32[]{:S(2)}) %collective-permute-start.8) | collective-permute-done | bytes 73760 | tf_op jit(solution)/shard_map/ppermute | solution.py:21
  30.3 0.8 collective-permute-start.9
  31.1 3.5 %collective-permute-done.9 = bf16[192,3,128]{2,0,1:T(8,128)(2,1)S(1)} collective-permute-done((bf16[192,3,128]{2,0,1:T(8,128)(2,1)S(1)}, bf16[192,3,128]{2,0,1:T(8,128)(2,1)S(1)}, u32[]{:S(2)}, u32[]{:S(2)}) %collective-permute-start.9) | collective-permute-done | bytes 147488 | tf_op jit(solution)/shard_map/ppermute | solution.py:21
  34.8 1.3 collective-permute-start.10
  36.0 8.4 %collective-permute-done.10 = bf16[384,3,128]{2,0,1:T(8,128)(2,1)S(1)} collective-permute-done((bf16[384,3,128]{2,0,1:T(8,128)(2,1)S(1)}, bf16[384,3,128]{2,0,1:T(8,128)(2,1)S(1)}, u32[]{:S(2)}, u32[]{:S(2)}) %collective-permute-start.10) | collective-permute-done | bytes 294944 | tf_op jit(solution)/shard_map/ppermute | solution.py:21
  44.6 17.5 %while.11 = (s32[]{:T(128)}, f32[8,96,128]{2,1,0:T(8,128)S(1)}, f32[8,5,96]{2,0,1:T(8,128)S(1)}, f32[7,768]{1,0:T(8,128)S(1)}, f32[640,1]{0,1:T(1,128)S(1)}, /*i...) while((s32[]{:T(128)}, f32[8,96,128]{2,1,0:T(8,128)S(1)}, ...), condition=%wide.region_3.4_spmd, body=%wide.region_2.3_spmd.sunk | while | flops 66516484 | bytes 1753905 | solution.py:182
  44.9 1.2 fusion.178
  46.1 0.3 fusion.177
  46.4 0.2 convolution_bitcast_fusion.3
  46.6 0.3 fusion.179
  47.1 1.2 fusion.178
  48.3 0.3 fusion.177
  48.6 0.2 convolution_bitcast_fusion.3
  48.8 0.3 fusion.179
  49.2 1.2 fusion.178
  50.5 0.3 fusion.177
  50.8 0.2 convolution_bitcast_fusion.3
  50.9 0.3 fusion.179
  51.4 1.2 fusion.178
  52.7 0.3 fusion.177
  53.0 0.2 convolution_bitcast_fusion.3
  53.1 0.3 fusion.179
  53.6 1.2 fusion.178
  54.8 0.3 fusion.177
  55.2 0.2 convolution_bitcast_fusion.3
  55.3 0.3 fusion.179
  55.8 1.2 fusion.178
  57.0 0.3 fusion.177
  57.3 0.2 convolution_bitcast_fusion.3
  57.5 0.3 fusion.179
  58.0 1.2 fusion.178
  59.2 0.3 fusion.177
  59.5 0.2 convolution_bitcast_fusion.3
  59.7 0.3 fusion.179
  60.2 1.2 fusion.178
  61.4 0.3 fusion.177
  61.7 0.2 convolution_bitcast_fusion.3
  61.9 0.3 fusion.179
  62.2 0.9 collective-permute-start.11
  63.1 5.2 %collective-permute-done.11 = f32[384,128]{1,0:T(8,128)S(1)} collective-permute-done((f32[384,128]{1,0:T(8,128)S(1)}, f32[384,128]{1,0:T(8,128)S(1)}, u32[]{:S(2)}, u32[]{:S(2)}) %collective-permute-start.11) | collective-permute-done | bytes 196640 | tf_op jit(solution)/shard_map/ppermute | solution.py:21
  68.4 0.5 collective-permute-start.12
  68.9 3.1 %collective-permute-done.12 = f32[192,128]{1,0:T(8,128)S(1)} collective-permute-done((f32[192,128]{1,0:T(8,128)S(1)}, f32[192,128]{1,0:T(8,128)S(1)}, u32[]{:S(2)}, u32[]{:S(2)}) %collective-permute-start.12) | collective-permute-done | bytes 98336 | tf_op jit(solution)/shard_map/ppermute | solution.py:21
  72.0 3.1 %collective-permute-start.13 = (f32[96,128]{1,0:T(8,128)S(1)}, f32[96,128]{1,0:T(8,128)S(1)}, u32[]{:S(2)}, u32[]{:S(2)}) collective-permute-start(f32[96,128]{1,0:T(8,128)S(1)} %slice_select_fusion.3), channel_id=1, source_target_pairs={{0,32},{2,34},{4,36},{6,38},{8,40},{10,42},{12,44},{14,46},{16,48}... | collective-permute-start | bytes 147464 | tf_op jit(solution)/shard_map/ppermute | solution.py:21
  75.1 4.3 %collective-permute-done.13 = f32[96,128]{1,0:T(8,128)S(1)} collective-permute-done((f32[96,128]{1,0:T(8,128)S(1)}, f32[96,128]{1,0:T(8,128)S(1)}, u32[]{:S(2)}, u32[]{:S(2)}) %collective-permute-start.13) | collective-permute-done | bytes 49184 | tf_op jit(solution)/shard_map/ppermute | solution.py:21
  79.4 0.7 multiply_reduce_fusion
  80.2 6.7 %psum.28 = f32[128]{0:T(128)S(1)} all-reduce(f32[128]{0:T(128)S(1)} %get-tuple-element.196), channel_id=1, replica_groups=mesh['patch_0'=4,'patch_1'=8,'patch_2'=4,'pix'=2] {'patch_0'}, use_global_device_ids=true, to_apply=%region_5.6 | all-reduce | flops 128 | bytes 1024 | tf_op jit(solution)/shard_map/psum | solution.py:25
  86.9 11.9 %psum.29 = f32[128]{0:T(128)S(1)} all-reduce(f32[128]{0:T(128)S(1)} %psum.28), channel_id=1, replica_groups=mesh['patch_0'=4,'patch_1'=8,'patch_2'=4,'pix'=2] {'patch_1'}, use_global_device_ids=true, to_apply=%region_6.7 | all-reduce | flops 128 | bytes 1024 | tf_op jit(solution)/shard_map/psum | solution.py:25
  98.8 8.4 %psum.30 = f32[128]{0:T(128)S(1)} all-reduce(f32[128]{0:T(128)S(1)} %psum.29), channel_id=1, replica_groups=mesh['patch_0'=4,'patch_1'=8,'patch_2'=4,'pix'=2] {'patch_2'}, use_global_device_ids=true, to_apply=%region_7.8 | all-reduce | flops 128 | bytes 1024 | tf_op jit(solution)/shard_map/psum | solution.py:25
  107.2 22.4 %psum.31 = f32[128]{0:T(128)S(1)} all-reduce(f32[128]{0:T(128)S(1)} %psum.30), channel_id=1, replica_groups=mesh['patch_0'=4,'patch_1'=8,'patch_2'=4,'pix'=2] {'pix'}, use_global_device_ids=true, to_apply=%region_8.9 | all-reduce | flops 128 | bytes 1024 | tf_op jit(solution)/shard_map/psum | solution.py:25
  129.5 0.5 broadcast_multiply_fusion.4
  (129 shorter events, 2.8 us)
Async XLA Ops:
  0.6 24.8 %copy-start = (bf16[48,3,128]{2,0,1:T(8,128)(2,1)S(1)}, bf16[48,3,128]{2,0,1:T(8,128)(2,1)}, u32[]{:S(2)}) copy-start(bf16[48,3,128]{2,0,1:T(8,128)(2,1)} %param.23) | copy-start | bytes 110596
  0.6 24.7 %collective-permute-start.7 = (bf16[48,3,128]{2,0,1:T(8,128)(2,1)}, bf16[48,3,128]{2,0,1:T(8,128)(2,1)S(1)}, u32[]{:S(2)}, u32[]{:S(2)}) collective-permute-start(bf16[48,3,128]{2,0,1:T(8,128)(2,1)} %param.23), channel_id=1, source_target_pairs={{0,2},{2,0},{4,6},{6,4},{8,10},{10,8},{12,14},{14,12},{16,18},{18,... | collective-permute-start | bytes 110600 | tf_op jit(solution)/shard_map/ppermute | solution.py:21
  4.3 8.0 %collective-permute-start.3 = (f32[7,48]{1,0:T(8,128)S(1)}, f32[7,48]{1,0:T(8,128)S(1)}, u32[]{:S(2)}, u32[]{:S(2)}) collective-permute-start(f32[7,48]{1,0:T(8,128)S(1)} %stack.32), channel_id=1, source_target_pairs={{0,2},{2,0},{4,6},{6,4},{8,10},{10,8},{12,14},{14,12},{16,18},{18,... | collective-permute-start | bytes 4040 | tf_op jit(solution)/shard_map/ppermute | solution.py:21
  5.1 10.0 %collective-permute-start = (f32[5,96]{1,0:T(8,128)S(1)}, f32[5,96]{1,0:T(8,128)S(1)}, u32[]{:S(2)}, u32[]{:S(2)}) collective-permute-start(f32[5,96]{1,0:T(8,128)S(1)} %pad_maximum_fusion.10), channel_id=1, source_target_pairs={{0,32},{2,34},{4,36},{6,38},{8,40},{10,42},{12,44},{14,46},{16,48}... | collective-permute-start | bytes 5768 | tf_op jit(solution)/shard_map/ppermute | solution.py:21
  12.3 4.9 %collective-permute-start.4 = (f32[7,96]{1,0:T(8,128)S(1)}, f32[7,96]{1,0:T(8,128)S(1)}, u32[]{:S(2)}, u32[]{:S(2)}) collective-permute-start(f32[7,96]{1,0:T(8,128)S(1)} %pad_maximum_fusion.11), channel_id=1, source_target_pairs={{0,4},{2,6},{4,0},{6,2},{8,12},{10,14},{12,8},{14,10},{16,20},{18,... | collective-permute-start | bytes 8072 | tf_op jit(solution)/shard_map/ppermute | solution.py:21
  15.9 2.7 %collective-permute-start.1 = (f32[5,192]{1,0:T(8,128)S(1)}, f32[5,192]{1,0:T(8,128)S(1)}, u32[]{:S(2)}, u32[]{:S(2)}) collective-permute-start(f32[5,192]{1,0:T(8,128)S(1)} %pad_maximum_fusion.8), channel_id=1, source_target_pairs={{0,64},{2,66},{4,68},{6,70},{8,72},{10,74},{12,76},{14,78},{16,80}... | collective-permute-start | bytes 11528 | tf_op jit(solution)/shard_map/ppermute | solution.py:21
  17.3 4.3 %collective-permute-start.5 = (f32[7,192]{1,0:T(8,128)S(1)}, f32[7,192]{1,0:T(8,128)S(1)}, u32[]{:S(2)}, u32[]{:S(2)}) collective-permute-start(f32[7,192]{1,0:T(8,128)S(1)} %pad_maximum_fusion.9), channel_id=1, source_target_pairs={{0,8},{2,10},{4,12},{6,14},{8,0},{10,2},{12,4},{14,6},{16,24},{18,... | collective-permute-start | bytes 16136 | tf_op jit(solution)/shard_map/ppermute | solution.py:21
  18.7 4.3 %collective-permute-start.2 = (f32[5,384]{1,0:T(8,128)S(1)}, f32[5,384]{1,0:T(8,128)S(1)}, u32[]{:S(2)}, u32[]{:S(2)}) collective-permute-start(f32[5,384]{1,0:T(8,128)S(1)} %pad_maximum_fusion.6), channel_id=1, source_target_pairs={{0,128},{2,130},{4,132},{6,134},{8,136},{10,138},{12,140},{14,142}... | collective-permute-start | bytes 23048 | tf_op jit(solution)/shard_map/ppermute | solution.py:21
  21.8 3.5 %collective-permute-start.6 = (f32[7,384]{1,0:T(8,128)S(1)}, f32[7,384]{1,0:T(8,128)S(1)}, u32[]{:S(2)}, u32[]{:S(2)}) collective-permute-start(f32[7,384]{1,0:T(8,128)S(1)} %pad_maximum_fusion.7), channel_id=1, source_target_pairs={{0,16},{2,18},{4,20},{6,22},{8,24},{10,26},{12,28},{14,30},{16,0},... | collective-permute-start | bytes 32264 | tf_op jit(solution)/shard_map/ppermute | solution.py:21
  25.4 4.8 %collective-permute-start.8 = (bf16[96,3,128]{2,0,1:T(8,128)(2,1)S(1)}, bf16[96,3,128]{2,0,1:T(8,128)(2,1)S(1)}, u32[]{:S(2)}, u32[]{:S(2)}) collective-permute-start(bf16[96,3,128]{2,0,1:T(8,128)(2,1)S(1)} %pad_maximum_fusion.3), channel_id=1, source_target_pairs={{0,4},{2,6},{4,0},{6,2},{8,12},{10,14},{12,8},{14,10},{16,20},{18,... | collective-permute-start | bytes 221192 | tf_op jit(solution)/shard_map/ppermute | solution.py:21
  30.3 4.4 %collective-permute-start.9 = (bf16[192,3,128]{2,0,1:T(8,128)(2,1)S(1)}, bf16[192,3,128]{2,0,1:T(8,128)(2,1)S(1)}, u32[]{:S(2)}, u32[]{:S(2)}) collective-permute-start(bf16[192,3,128]{2,0,1:T(8,128)(2,1)S(1)} %pad_maximum_fusion.2), channel_id=1, source_target_pairs={{0,8},{2,10},{4,12},{6,14},{8,0},{10,2},{12,4},{14,6},{16,24},{18,... | collective-permute-start | bytes 442376 | tf_op jit(solution)/shard_map/ppermute | solution.py:21
  34.8 9.7 %collective-permute-start.10 = (bf16[384,3,128]{2,0,1:T(8,128)(2,1)S(1)}, bf16[384,3,128]{2,0,1:T(8,128)(2,1)S(1)}, u32[]{:S(2)}, u32[]{:S(2)}) collective-permute-start(bf16[384,3,128]{2,0,1:T(8,128)(2,1)S(1)} %pad_maximum_fusion.1), channel_id=1, source_target_pairs={{0,16},{2,18},{4,20},{6,22},{8,24},{10,26},{12,28},{14,30},{16,0},... | collective-permute-start | bytes 884744 | tf_op jit(solution)/shard_map/ppermute | solution.py:21
  62.2 6.1 %collective-permute-start.11 = (f32[384,128]{1,0:T(8,128)S(1)}, f32[384,128]{1,0:T(8,128)S(1)}, u32[]{:S(2)}, u32[]{:S(2)}) collective-permute-start(f32[384,128]{1,0:T(8,128)S(1)} %bitcast.110), channel_id=1, source_target_pairs={{0,128},{2,130},{4,132},{6,134},{8,136},{10,138},{12,140},{14,142}... | collective-permute-start | bytes 589832 | tf_op jit(solution)/shard_map/ppermute | solution.py:21
  68.3 6.8 %copy-start.3 = (s32[96]{0:T(128)S(1)}, s32[96]{0:T(128)}, u32[]{:S(2)}) copy-start(s32[96]{0:T(128)} %param.17) | copy-start | bytes 1156
  68.3 11.1 %copy-start.1 = (f32[96]{0:T(128)S(1)}, f32[96]{0:T(128)}, u32[]{:S(2)}) copy-start(f32[96]{0:T(128)} %param.16) | copy-start | bytes 1156
  68.3 11.1 %copy-start.2 = (f32[96]{0:T(128)S(1)}, f32[96]{0:T(128)}, u32[]{:S(2)}) copy-start(f32[96]{0:T(128)} %param.15) | copy-start | bytes 1156
  68.4 3.6 %collective-permute-start.12 = (f32[192,128]{1,0:T(8,128)S(1)}, f32[192,128]{1,0:T(8,128)S(1)}, u32[]{:S(2)}, u32[]{:S(2)}) collective-permute-start(f32[192,128]{1,0:T(8,128)S(1)} %slice_select_fusion.2), channel_id=1, source_target_pairs={{0,64},{2,66},{4,68},{6,70},{8,72},{10,74},{12,76},{14,78},{16,80}... | collective-permute-start | bytes 294920 | tf_op jit(solution)/shard_map/ppermute | solution.py:21
  72.0 7.5 %collective-permute-start.13 = (f32[96,128]{1,0:T(8,128)S(1)}, f32[96,128]{1,0:T(8,128)S(1)}, u32[]{:S(2)}, u32[]{:S(2)}) collective-permute-start(f32[96,128]{1,0:T(8,128)S(1)} %slice_select_fusion.3), channel_id=1, source_target_pairs={{0,32},{2,34},{4,36},{6,38},{8,40},{10,42},{12,44},{14,46},{16,48}... | collective-permute-start | bytes 147464 | tf_op jit(solution)/shard_map/ppermute | solution.py:21
where the time goes:
time: 130 us
  blocking collectives  49.4 us (38%)
  waiting for transfers between devices  30.5 us (23%)
  starting transfers between devices  26.4 us (20%)
  other arithmetic  17.3 us (13%)
  matrix products  3.4 us (3%)
  local copies, waits for them, and re-layouts  1.47 us (1%)
    psum x4, blocking collectives, one_axis_at_a_time(): return functools.reduce(lax.psum, axes, value)  49.4 us
    ppermute x14, waiting for transfers between devices, partner(): return lax.ppermute(value, axis, pairs)  30.5 us
    ppermute x14, starting transfers between devices, partner(): return lax.ppermute(value, axis, pairs)  26.4 us
    another operation x56, other arithmetic  12.6 us
    dot_general x16, matrix products, tile_product(): lax.dot_general(green_tile, slip_table, (((0,), (0,)), ((), ())), preferr...  3.4 us
  transfers between devices with their start and end apart: 14, of which 8 were waited for; matrix products, arithmetic and copies ran while one was open for 3% of the time, Pallas kernels for 0%

commit v1 on v0

v1 whole, which is shorter than its diff:
```python
import functools
import math

import jax
import jax.numpy as jnp
from jax import lax
from jax.experimental import pallas as pl
from jax.experimental.pallas import tpu as pltpu
from jax.sharding import Mesh
from jax.sharding import PartitionSpec as P

PATCH = ("y", "z", "x")
PATCH_PIX = ("y", "z", "x", "pix")

LANES = 128
SUB = 8
GROUPS = 3
PIECE = SUB * GROUPS
SLIP_ROWS = 3 * PIECE
ROWS = SLIP_ROWS + SUB
FRAME_STRIDE = 40
UNIT = LANES // SUB
VIEW_SCALE = 3.0 / (2.0 * math.pi)


def xor_pairs(count, mask):
    return [(i, i ^ mask) for i in range(count)]


def mirror_pairs(count):
    return [(i, count - 1 - i) for i in range(count)]


def rounded(value):
    return value.astype(jnp.bfloat16).astype(jnp.float32)


def pack_kernel(core_ref, strike_ref, dip_ref, pos_ref, depth_ref, ids_ref, slip_ref, out_ref, turned_ref):
    ids = ids_ref[...]
    strike = jnp.zeros(ids.shape, jnp.float32)
    dip = jnp.zeros(ids.shape, jnp.float32)
    for segment in range(strike_ref.shape[0]):
        same = ids == segment
        strike = jnp.where(same, strike_ref[segment], strike)
        dip = jnp.where(same, dip_ref[segment], dip)
    pos = pos_ref[...]
    angles = jnp.concatenate([strike, dip], axis=0)
    sines = jnp.sin(angles)
    cosines = jnp.cos(angles)
    rows = jnp.concatenate(
        [pos, depth_ref[...], sines[0:1], cosines[0:1], sines[1:2], cosines[1:2], jnp.zeros(ids.shape, jnp.float32)],
        axis=0,
    )
    high = rounded(rows)
    rest = rows - high
    middle = rounded(rest)
    low = rounded(rest - middle)
    count = rows.shape[1]
    pieces = jnp.concatenate([high, middle, low], axis=0)
    pieces = jnp.concatenate([pieces, jnp.zeros((24, LANES - count), jnp.float32)], axis=1)
    pieces = jnp.concatenate([pieces, jnp.zeros((LANES - 24, LANES), jnp.float32)], axis=0)
    turned_ref[...] = jnp.transpose(pieces)
    first = core_ref[0] * PIECE
    tile = jnp.zeros((SUB, LANES), jnp.float32)
    for group in range(GROUPS):
        start = pl.multiple_of(first + SUB * group, SUB)
        part = turned_ref[pl.ds(start, SUB), :]
        tile = tile + (part if group == 0 else pltpu.roll(part, FRAME_STRIDE * group, 1))
        for k in range(3):
            row = (k * GROUPS + group) * SUB
            out_ref[row : row + SUB, :] = slip_ref[k, pl.ds(start, SUB), :]
    out_ref[SLIP_ROWS:ROWS, :] = tile.astype(jnp.bfloat16)


def pack(core, seg_strike, seg_dip, patch_pos, patch_depth, segment_ids, slip):
    smem = pl.BlockSpec(memory_space=pltpu.SMEM)
    vmem = pl.BlockSpec(memory_space=pltpu.VMEM)
    return pl.pallas_call(
        pack_kernel,
        out_shape=jax.ShapeDtypeStruct((ROWS, LANES), jnp.bfloat16),
        in_specs=[smem, smem, smem, vmem, vmem, vmem, vmem],
        out_specs=vmem,
        scratch_shapes=[pltpu.VMEM((LANES, LANES), jnp.float32)],
        name="pack",
    )(core, seg_strike, seg_dip, patch_pos, patch_depth[None, :], segment_ids[None, :], jnp.transpose(slip, (1, 0, 2)))


def unit_kernel(sites_ref, unit_ref, acc_ref, out_ref, pix_ref, green_ref):
    blocks, _, width = sites_ref.shape
    pixels = blocks * width
    for block in range(blocks):
        site = jnp.concatenate([sites_ref[block], jnp.zeros((SUB, LANES - width), jnp.float32)], axis=1)
        columns = jnp.transpose(site)[:width]
        for f in range(5):
            column = columns[:, f : f + 1]
            if f >= 2:
                column = column * VIEW_SCALE
            pix_ref[f, block * width : (block + 1) * width, :] = jnp.broadcast_to(column, (width, LANES))
    frames = unit_ref[:, SLIP_ROWS:ROWS, :].astype(jnp.float32).reshape(LANES, LANES)
    turned = jnp.transpose(frames)
    total = acc_ref[...]
    step = 16
    for group in range(GROUPS):
        base = FRAME_STRIDE * group
        rows = (turned[base : base + 8] + turned[base + 8 : base + 16]) + turned[base + 16 : base + 24]
        def spread(i):
            return jnp.broadcast_to(rows[i : i + 1], (step, LANES))
        src_e, src_n, d, s, c, sd, cd = [spread(i) for i in range(7)]
        dd = d * d
        d_sd = d * sd
        d_cd = d * cd
        k0 = sd * (-1.0 / 6.0)
        k1 = sd * cd * (1.0 / 6.0)
        k2 = sd * sd * (1.0 / 6.0)

        def chunk(i, carry):
            start = pl.multiple_of(i * step, step)
            here = pl.ds(start, step)
            e = pix_ref[0, here, :] - src_e
            n = pix_ref[1, here, :] - src_n
            v0 = pix_ref[2, here, :]
            v1 = pix_ref[3, here, :]
            w = pix_ref[4, here, :]
            x = e * s + n * c
            y = n * s - e * c
            a = v0 * s + v1 * c
            b = v1 * s - v0 * c
            xx = x * x
            r2 = xx + y * y + dd
            rho = lax.rsqrt(r2)
            t = r2 * rho + d
            tau = 1.0 / t
            rho2 = rho * rho
            rho3 = rho2 * rho
            g = rho * tau
            g2 = g + rho2
            ga = g * tau
            gc = g * g2
            gb = ga * (g + g2)
            ax = a * x
            by = b * y
            ay = a * y
            bx = b * x
            h = ax + by
            xy = x * y
            j0 = ga * (ay + bx) - xy * (gb * h + w * gc)
            j1 = (ax * rho3 - ga * (ax - by)) + xy * (gb * (ay - bx)) + w * (g - xx * gc)
            q = y * sd - d_cd
            p = y * cd + d_sd
            f = (q * (rho3 * rho2)) * (h + w * d)
            green_ref[here, 0:LANES] = (k0 * j0 - x * f).astype(jnp.bfloat16)
            green_ref[here, LANES : 2 * LANES] = (k1 * j1 - p * f).astype(jnp.bfloat16)
            green_ref[here, 2 * LANES : 3 * LANES] = (q * f - k2 * j1).astype(jnp.bfloat16)
            return carry

        lax.fori_loop(0, pixels // step, chunk, 0, unroll=2)
        slip = [
            unit_ref[:, (k * GROUPS + group) * SUB : (k * GROUPS + group + 1) * SUB, :].reshape(LANES, LANES)
            for k in range(3)
        ]
        table = jnp.concatenate(slip, axis=0)
        total = total + jnp.dot(green_ref[...], table, preferred_element_type=jnp.float32)
    out_ref[...] = total


def unit_product(sites, unit, acc):
    pixels = sites.shape[0] * sites.shape[2]
    vmem = pl.BlockSpec(memory_space=pltpu.VMEM)
    pairs = pixels * LANES * GROUPS
    return pl.pallas_call(
        unit_kernel,
        out_shape=jax.ShapeDtypeStruct((pixels, LANES), jnp.float32),
        in_specs=[vmem, vmem, vmem],
        out_specs=vmem,
        scratch_shapes=[
            pltpu.VMEM((5, pixels, LANES), jnp.float32),
            pltpu.VMEM((pixels, 3 * LANES), jnp.bfloat16),
        ],
        cost_estimate=pl.CostEstimate(flops=pairs * 3 * LANES * 2 + pairs * 80, transcendentals=2 * pairs, bytes_accessed=2**19),
        name="unit_product",
    )(sites, unit, acc)


def residual_kernel(sites_ref, pred_ref, res_ref, sum_ref):
    blocks, _, width = sites_ref.shape
    sums = []
    for block in range(blocks):
        site = jnp.concatenate([sites_ref[block], jnp.zeros((SUB, LANES - width), jnp.float32)], axis=1)
        columns = jnp.transpose(site)[:width]
        value = pred_ref[block]
        observed = jnp.broadcast_to(columns[:, 5:6], value.shape)
        noise = jnp.broadcast_to(columns[:, 6:7], value.shape)
        mask = jnp.broadcast_to(columns[:, 7:8], value.shape)
        res = mask * (value - observed) / noise
        if block == 0:
            res_ref[...] = res
        sums.append(jnp.sum(res * res, axis=0, keepdims=True))
    sum_ref[...] = (sums[0] + sums[1]) + (sums[2] + sums[3])


def residual_part(sites, pred):
    vmem = pl.BlockSpec(memory_space=pltpu.VMEM)
    return pl.pallas_call(
        residual_kernel,
        out_shape=(
            jax.ShapeDtypeStruct(pred.shape[1:], jnp.float32),
            jax.ShapeDtypeStruct((1, LANES), jnp.float32),
        ),
        in_specs=[vmem, vmem],
        out_specs=(vmem, vmem),
        name="residual_part",
    )(sites, pred)


def per_device(
    pixel_pos,
    pixel_view,
    observed,
    noise_scale,
    valid_mask,
    patch_pos,
    patch_depth,
    segment_ids,
    seg_strike,
    seg_dip,
    slip_models,
):
    own_pixels = pixel_pos.shape[1]
    y_near, y_far = xor_pairs(4, 1), mirror_pairs(4)
    x_near, x_far = xor_pairs(4, 1), mirror_pairs(4)
    z_steps = [xor_pairs(8, 1), xor_pairs(8, 2), mirror_pairs(8)]
    core = lax.axis_index("pix").astype(jnp.int32)[None]
    piece = pack(core, seg_strike, seg_dip, patch_pos, patch_depth, segment_ids, slip_models)
    sites = jnp.concatenate(
        [pixel_pos, pixel_view, observed[None], noise_scale[None], valid_mask.astype(jnp.float32)[None]], axis=0
    )[None]

    def join(value, axis, pairs):
        return jnp.concatenate([value, lax.ppermute(value, axis, pairs)], axis=0)

    sites = join(join(sites, "y", y_near), "y", y_far)
    pieces = piece[None]
    for pairs in z_steps:
        pieces = join(pieces, "z", pairs)
    swap = xor_pairs(2, 1)
    near = join(pieces, "x", x_near)
    far = lax.ppermute(near, "x", x_far)
    near_other = lax.ppermute(near, "pix", swap)
    acc = jnp.zeros((4 * own_pixels, LANES), jnp.float32)
    acc = unit_product(sites, near, acc)
    acc = unit_product(sites, near_other, acc)
    far_other = lax.ppermute(far, "pix", swap)
    acc = unit_product(sites, far, acc)
    acc = unit_product(sites, far_other, acc)

    part = acc.reshape(4, own_pixels, LANES)
    half = own_pixels // 2

    def add(mine, axis, pairs, order):
        other = lax.ppermute(mine, axis, pairs)
        return jnp.stack([mine[i] + other[j] for i, j in enumerate(order)])

    low, high = part[:, :half], part[:, half:]
    low = add(low, "y", y_near, (1, 0, 3, 2))
    high = add(high, "y", y_far, (2, 3, 0, 1))
    low = add(low, "y", y_far, (2, 3, 0, 1))
    high = add(high, "y", y_near, (1, 0, 3, 2))
    pred = jnp.concatenate([low, high], axis=1)
    residual, own_sum = residual_part(sites, pred)
    total = own_sum
    for axis, pairs in [("pix", swap), ("x", x_near), ("x", xor_pairs(4, 2))] + [("z", pairs) for pairs in z_steps]:
        total = total + lax.ppermute(total, axis, pairs)
    pixels = own_pixels * lax.axis_size(PATCH) * lax.axis_size("pix")
    return (residual, total[0] / pixels)


def solution(mesh):
    finer = Mesh(mesh.devices.reshape(4, 8, 4, mesh.shape["pix"]), PATCH_PIX)
    placed = (
        P(None, PATCH_PIX),
        P(None, PATCH_PIX),
        P(PATCH_PIX),
        P(PATCH_PIX),
        P(PATCH_PIX),
        P(None, PATCH),
        P(PATCH),
        P(PATCH),
        P(),
        P(),
        P(PATCH, None, None),
    )
    return jax.shard_map(
        per_device,
        mesh=finer,
        in_specs=placed,
        out_specs=(P(PATCH_PIX, None), P()),
        check_vma=False,
    )
```

time: 130 us -> 109 us (0.84)
  the two profiles are of different devices: /device:TPU:1 before, /device:TPU:38 now
where the time goes in v1:
time: 109 us; the launch traced here: 108 us
  waiting for transfers between devices  50.6 us (46%)
  starting transfers between devices  27.2 us (25%)
  Pallas kernels  22.5 us (21%)
  local copies, waits for them, and re-layouts  4.67 us (4%)
  other arithmetic  2.66 us (2%)
    pallas_call x4, Pallas kernels, unit_product(): pl.pallas_call(unit_kernel, out_shape=jax.ShapeDtypeStruct((pixels, LANES...  19 us
    ppermute x6, waiting for transfers between devices, per_device(): total = total + lax.ppermute(total, axis, pairs)  16.9 us
    ppermute x6, waiting for transfers between devices, join(): return jnp.concatenate([value, lax.ppermute(value, axis, pairs)], axis=0)  16.7 us
    ppermute x6, starting transfers between devices, join(): return jnp.concatenate([value, lax.ppermute(value, axis, pairs)], axis=0)  14.5 us
    ppermute x4, waiting for transfers between devices, add(): other = lax.ppermute(mine, axis, pairs)  9.2 us
    ppermute x1, waiting for transfers between devices, per_device(): far = lax.ppermute(near, 'x', x_far)  7.8 us
    ppermute x6, starting transfers between devices, per_device(): total = total + lax.ppermute(total, axis, pairs)  7.55 us
    ppermute x4, starting transfers between devices, add(): other = lax.ppermute(mine, axis, pairs)  4.49 us
  transfers between devices with their start and end apart: 19, of which 17 were waited for; matrix products, arithmetic and copies ran while one was open for 1% of the time, Pallas kernels for 13%

profile of v1, /device:TPU:38, one launch (start us, length us, event | category | flops | bytes accessed | tf_op | source)
XLA Modules:
  0.0 108.3 jit_solution(9595538587952506363)
XLA Ops:
  0.6 1.7 %pack.1 = bf16[80,128]{1,0:T(8,128)(2,1)} custom-call(s32[1]{0:T(128)} %bitcast.4.core_ref, f32[16]{0:T(128)} %strike_ref.1, f32[16]{0:T(128)} %dip_ref.1, f32[2,48]{1,0:T(2,128)} %pos_ref.1, f32[1,48]{1,0:T(1,128)} %bitcast.24, s32[1,48]{1,0:T(1,128)} %bitcast.25, bf16[3,48,128]{2,1,0:T(8,128)(2,1)} %bitcast.20), custom_call_target="tpu_custom_call" | custom-call | tf_op jit(solution)/shard_map/pack/pallas_call | solution.py:78
  2.3 0.1 collective-permute-start.2
  2.4 3.9 %collective-permute-done.2 = bf16[1,80,128]{2,1,0:T(8,128)(2,1)S(1)} collective-permute-done((bf16[1,80,128]{2,1,0:T(8,128)(2,1)}, bf16[1,80,128]{2,1,0:T(8,128)(2,1)S(1)}, u32[]{:S(2)}, u32[]{:S(2)}) %collective-permute-start.2) | collective-permute-done | bytes 20512 | tf_op jit(solution)/shard_map/ppermute | solution.py:239
  6.3 0.7 pad_maximum_fusion.4
  7.0 3.3 %collective-permute-start.3 = (bf16[2,80,128]{2,1,0:T(8,128)(2,1)S(1)}, bf16[2,80,128]{2,1,0:T(8,128)(2,1)S(1)}, u32[]{:S(2)}, u32[]{:S(2)}) collective-permute-start(bf16[2,80,128]{2,1,0:T(8,128)(2,1)S(1)} %pad_maximum_fusion.4), channel_id=1, source_target_pairs={{0,16},{8,24},{16,0},{24,8},{32,48},{40,56},{48,32},{56,40},{1,17}... | collective-permute-start | bytes 122888 | tf_op jit(solution)/shard_map/ppermute | solution.py:239
  10.3 0.0 copy-done.1
  10.3 2.0 %collective-permute-done.3 = bf16[2,80,128]{2,1,0:T(8,128)(2,1)S(1)} collective-permute-done((bf16[2,80,128]{2,1,0:T(8,128)(2,1)S(1)}, bf16[2,80,128]{2,1,0:T(8,128)(2,1)S(1)}, u32[]{:S(2)}, u32[]{:S(2)}) %collective-permute-start.3) | collective-permute-done | bytes 40992 | tf_op jit(solution)/shard_map/ppermute | solution.py:239
  12.3 5.6 %collective-permute-start.4 = (bf16[4,80,128]{2,1,0:T(8,128)(2,1)S(1)}, bf16[4,80,128]{2,1,0:T(8,128)(2,1)S(1)}, u32[]{:S(2)}, u32[]{:S(2)}) collective-permute-start(bf16[4,80,128]{2,1,0:T(8,128)(2,1)S(1)} %pad_maximum_fusion.3), channel_id=1, source_target_pairs={{0,56},{8,48},{16,40},{24,32},{32,24},{40,16},{48,8},{56,0},{1,57}... | collective-permute-start | bytes 245768 | tf_op jit(solution)/shard_map/ppermute | solution.py:239
  17.9 2.5 %collective-permute-done.4 = bf16[4,80,128]{2,1,0:T(8,128)(2,1)S(1)} collective-permute-done((bf16[4,80,128]{2,1,0:T(8,128)(2,1)S(1)}, bf16[4,80,128]{2,1,0:T(8,128)(2,1)S(1)}, u32[]{:S(2)}, u32[]{:S(2)}) %collective-permute-start.4) | collective-permute-done | bytes 81952 | tf_op jit(solution)/shard_map/ppermute | solution.py:239
  20.4 0.9 collective-permute-start.5
  21.4 0.0 copy-start.10
  21.4 4.5 %collective-permute-done.5 = bf16[8,80,128]{2,1,0:T(8,128)(2,1)S(1)} collective-permute-done((bf16[8,80,128]{2,1,0:T(8,128)(2,1)S(1)}, bf16[8,80,128]{2,1,0:T(8,128)(2,1)S(1)}, u32[]{:S(2)}, u32[]{:S(2)}) %collective-permute-start.5) | collective-permute-done | bytes 163872 | tf_op jit(solution)/shard_map/ppermute | solution.py:239
  25.9 0.0 copy-start.2
  25.9 0.6 collective-permute-start.6
  26.4 0.0 collective-permute-start.8
  26.4 7.8 %collective-permute-done.6.unit_ref = bf16[16,80,128]{2,1,0:T(8,128)(2,1)S(1)} collective-permute-done((bf16[16,80,128]{2,1,0:T(8,128)(2,1)S(1)}, bf16[16,80,128]{2,1,0:T(8,128)(2,1)S(1)}, u32[]{:S(2)}, u32[]{:S(2)}) %collective-permute-start.6) | collective-permute-done | bytes 327712 | tf_op jit(solution)/shard_map/ppermute | solution.py:247
  34.2 0.0 collective-permute-start.7
  34.3 0.0 copy-done.10
  34.3 0.0 copy-start.6
  34.3 0.0 copy-start.7
  34.3 0.0 copy-start.8
  34.3 0.7 copy-done.6
  35.0 0.1 copy-done.7
  35.1 0.0 copy-done.8
  35.1 1.7 %collective-permute-start = (f32[1,8,96]{2,1,0:T(8,128)S(1)}, f32[1,8,96]{2,1,0:T(8,128)S(1)}, u32[]{:S(2)}, u32[]{:S(2)}) collective-permute-start(f32[1,8,96]{2,1,0:T(8,128)S(1)} %bitcast.21), channel_id=1, source_target_pairs={{0,64},{64,0},{128,192},{192,128},{1,65},{65,1},{129,193},{193,129... | collective-permute-start | bytes 9224 | tf_op jit(solution)/shard_map/ppermute | solution.py:239
  36.8 2.0 %collective-permute-done = f32[1,8,96]{2,1,0:T(8,128)S(1)} collective-permute-done((f32[1,8,96]{2,1,0:T(8,128)S(1)}, f32[1,8,96]{2,1,0:T(8,128)S(1)}, u32[]{:S(2)}, u32[]{:S(2)}) %collective-permute-start) | collective-permute-done | bytes 3104 | tf_op jit(solution)/shard_map/ppermute | solution.py:239
  38.8 3.0 %collective-permute-start.1 = (f32[2,8,96]{2,1,0:T(8,128)S(1)}, f32[2,8,96]{2,1,0:T(8,128)S(1)}, u32[]{:S(2)}, u32[]{:S(2)}) collective-permute-start(f32[2,8,96]{2,1,0:T(8,128)S(1)} %pad_maximum_fusion.6), channel_id=1, source_target_pairs={{0,192},{64,128},{128,64},{192,0},{1,193},{65,129},{129,65},{193,1... | collective-permute-start | bytes 18440 | tf_op jit(solution)/shard_map/ppermute | solution.py:239
  41.8 1.8 %collective-permute-done.1 = f32[2,8,96]{2,1,0:T(8,128)S(1)} collective-permute-done((f32[2,8,96]{2,1,0:T(8,128)S(1)}, f32[2,8,96]{2,1,0:T(8,128)S(1)}, u32[]{:S(2)}, u32[]{:S(2)}) %collective-permute-start.1) | collective-permute-done | bytes 6176 | tf_op jit(solution)/shard_map/ppermute | solution.py:239
  43.6 0.6 pad_maximum_fusion.5.sites_ref
  44.3 0.7 broadcast_in_dim.35.acc_ref
  45.0 4.7 %unit_product.4.acc_ref = f32[384,128]{1,0:T(8,128)} custom-call(f32[4,8,96]{2,1,0:T(8,128)} %pad_maximum_fusion.5.sites_ref, bf16[16,80,128]{2,1,0:T(8,128)(2,1)} %copy-done.2, f32[384,128]{1,0:T(8,128)} %broadcast_in_dim.35.acc_ref), custom_call_target="tpu_custom_call" | custom-call | flops 125042688 | bytes 524288 | tf_op jit(solution)/shard_map/unit_product/pallas_call | solution.py:170
  49.7 0.0 copy-done.3
  49.7 0.0 collective-permute-done.8.unit_ref
  49.7 0.7 copy-done.5
  50.4 4.8 %unit_product.5.acc_ref = f32[384,128]{1,0:T(8,128)} custom-call(f32[4,8,96]{2,1,0:T(8,128)} %pad_maximum_fusion.5.sites_ref, bf16[16,80,128]{2,1,0:T(8,128)(2,1)} %copy-done.5, f32[384,128]{1,0:T(8,128)} %unit_product.4.acc_ref), custom_call_target="tpu_custom_call" | custom-call | flops 125042688 | bytes 524288 | tf_op jit(solution)/shard_map/unit_product/pallas_call | solution.py:170
  55.2 4.7 %unit_product.6.acc_ref = f32[384,128]{1,0:T(8,128)} custom-call(f32[4,8,96]{2,1,0:T(8,128)} %pad_maximum_fusion.5.sites_ref, bf16[16,80,128]{2,1,0:T(8,128)(2,1)} %copy-done.3, f32[384,128]{1,0:T(8,128)} %unit_product.5.acc_ref), custom_call_target="tpu_custom_call" | custom-call | flops 125042688 | bytes 524288 | tf_op jit(solution)/shard_map/unit_product/pallas_call | solution.py:170
  59.9 0.0 collective-permute-done.7.unit_ref
  59.9 0.7 copy-done.4
  60.7 4.7 %unit_product.7 = f32[384,128]{1,0:T(8,128)} custom-call(f32[4,8,96]{2,1,0:T(8,128)} %pad_maximum_fusion.5.sites_ref, bf16[16,80,128]{2,1,0:T(8,128)(2,1)} %copy-done.4, f32[384,128]{1,0:T(8,128)} %unit_product.6.acc_ref), custom_call_target="tpu_custom_call" | custom-call | flops 125042688 | bytes 524288 | tf_op jit(solution)/shard_map/unit_product/pallas_call | solution.py:170
  65.4 1.0 fusion
  66.4 3.1 %collective-permute-start.11 = (f32[4,48,128]{2,1,0:T(8,128)S(1)}, f32[4,48,128]{2,1,0:T(8,128)S(1)}, u32[]{:S(2)}, u32[]{:S(2)}) collective-permute-start(f32[4,48,128]{2,1,0:T(8,128)S(1)} %get-tuple-element.19), channel_id=1, source_target_pairs={{0,192},{64,128},{128,64},{192,0},{1,193},{65,129},{129,65},{193,1... | collective-permute-start | bytes 294920 | tf_op jit(solution)/shard_map/ppermute | solution.py:260
  69.5 0.0 collective-permute-start.9
  69.5 2.8 %collective-permute-done.11 = f32[4,48,128]{2,1,0:T(8,128)S(1)} collective-permute-done((f32[4,48,128]{2,1,0:T(8,128)S(1)}, f32[4,48,128]{2,1,0:T(8,128)S(1)}, u32[]{:S(2)}, u32[]{:S(2)}) %collective-permute-start.11) | collective-permute-done | bytes 98336 | tf_op jit(solution)/shard_map/ppermute | solution.py:260
  72.3 1.8 %collective-permute-done.9 = f32[4,48,128]{2,1,0:T(8,128)S(1)} collective-permute-done((f32[4,48,128]{2,1,0:T(8,128)S(1)}, f32[4,48,128]{2,1,0:T(8,128)S(1)}, u32[]{:S(2)}, u32[]{:S(2)}) %collective-permute-start.9) | collective-permute-done | bytes 98336 | tf_op jit(solution)/shard_map/ppermute | solution.py:260
  74.2 1.3 %collective-permute-start.10 = (f32[4,48,128]{2,1,0:T(8,128)S(1)}, f32[4,48,128]{2,1,0:T(8,128)S(1)}, u32[]{:S(2)}, u32[]{:S(2)}) collective-permute-start(f32[4,48,128]{2,1,0:T(8,128)S(1)} %pad_maximum_fusion.1), channel_id=1, source_target_pairs={{0,192},{64,128},{128,64},{192,0},{1,193},{65,129},{129,65},{193,1... | collective-permute-start | bytes 294920 | tf_op jit(solution)/shard_map/ppermute | solution.py:260
  75.5 0.1 collective-permute-start.12
  75.6 4.5 %collective-permute-done.10 = f32[4,48,128]{2,1,0:T(8,128)S(1)} collective-permute-done((f32[4,48,128]{2,1,0:T(8,128)S(1)}, f32[4,48,128]{2,1,0:T(8,128)S(1)}, u32[]{:S(2)}, u32[]{:S(2)}) %collective-permute-start.10) | collective-permute-done | bytes 98336 | tf_op jit(solution)/shard_map/ppermute | solution.py:260
  80.1 0.1 collective-permute-done.12
  80.2 0.7 maximum_maximum_fusion.pred_ref
  80.9 1.8 %residual_part.1 = (f32[96,128]{1,0:T(8,128)}, f32[1,128]{1,0:T(1,128)}) custom-call(f32[4,8,96]{2,1,0:T(8,128)} %pad_maximum_fusion.5.sites_ref, f32[4,96,128]{2,1,0:T(8,128)} %maximum_maximum_fusion.pred_ref), custom_call_target="tpu_custom_call" | custom-call | tf_op jit(solution)/shard_map/residual_part/pallas_call | solution.py:203
  82.7 0.7 copy-done.11
  83.3 0.0 collective-permute-start.13
  83.4 1.2 %collective-permute-done.13 = f32[1,128]{1,0:T(1,128)S(1)} collective-permute-done((f32[1,128]{1,0:T(1,128)S(1)}, f32[1,128]{1,0:T(1,128)S(1)}, u32[]{:S(2)}, u32[]{:S(2)}) %collective-permute-start.13) | collective-permute-done | bytes 544 | tf_op jit(solution)/shard_map/ppermute | solution.py:272
  84.5 0.0 collective-permute-start.14
  84.5 3.6 %collective-permute-done.14 = f32[1,128]{1,0:T(1,128)S(1)} collective-permute-done((f32[1,128]{1,0:T(1,128)S(1)}, f32[1,128]{1,0:T(1,128)S(1)}, u32[]{:S(2)}, u32[]{:S(2)}) %collective-permute-start.14) | collective-permute-done | bytes 544 | tf_op jit(solution)/shard_map/ppermute | solution.py:272
  88.1 0.2 collective-permute-start.15
  88.3 4.9 %collective-permute-done.15 = f32[1,128]{1,0:T(1,128)S(1)} collective-permute-done((f32[1,128]{1,0:T(1,128)S(1)}, f32[1,128]{1,0:T(1,128)S(1)}, u32[]{:S(2)}, u32[]{:S(2)}) %collective-permute-start.15) | collective-permute-done | bytes 544 | tf_op jit(solution)/shard_map/ppermute | solution.py:272
  93.2 1.0 collective-permute-start.16
  94.2 2.6 %collective-permute-done.16 = f32[1,128]{1,0:T(1,128)S(1)} collective-permute-done((f32[1,128]{1,0:T(1,128)S(1)}, f32[1,128]{1,0:T(1,128)S(1)}, u32[]{:S(2)}, u32[]{:S(2)}) %collective-permute-start.16) | collective-permute-done | bytes 544 | tf_op jit(solution)/shard_map/ppermute | solution.py:272
  96.7 1.4 %collective-permute-start.17 = (f32[1,128]{1,0:T(1,128)S(1)}, f32[1,128]{1,0:T(1,128)S(1)}, u32[]{:S(2)}, u32[]{:S(2)}) collective-permute-start(f32[1,128]{1,0:T(1,128)S(1)} %add.109), channel_id=1, source_target_pairs={{0,16},{8,24},{16,0},{24,8},{32,48},{40,56},{48,32},{56,40},{1,17}... | collective-permute-start | bytes 1544 | tf_op jit(solution)/shard_map/ppermute | solution.py:272
  98.2 3.0 %collective-permute-done.17 = f32[1,128]{1,0:T(1,128)S(1)} collective-permute-done((f32[1,128]{1,0:T(1,128)S(1)}, f32[1,128]{1,0:T(1,128)S(1)}, u32[]{:S(2)}, u32[]{:S(2)}) %collective-permute-start.17) | collective-permute-done | bytes 544 | tf_op jit(solution)/shard_map/ppermute | solution.py:272
  101.2 4.9 %collective-permute-start.18 = (f32[1,128]{1,0:T(1,128)S(1)}, f32[1,128]{1,0:T(1,128)S(1)}, u32[]{:S(2)}, u32[]{:S(2)}) collective-permute-start(f32[1,128]{1,0:T(1,128)S(1)} %add.110), channel_id=1, source_target_pairs={{0,56},{8,48},{16,40},{24,32},{32,24},{40,16},{48,8},{56,0},{1,57}... | collective-permute-start | bytes 1544 | tf_op jit(solution)/shard_map/ppermute | solution.py:272
  106.1 1.7 %collective-permute-done.18 = f32[1,128]{1,0:T(1,128)S(1)} collective-permute-done((f32[1,128]{1,0:T(1,128)S(1)}, f32[1,128]{1,0:T(1,128)S(1)}, u32[]{:S(2)}, u32[]{:S(2)}) %collective-permute-start.18) | collective-permute-done | bytes 544 | tf_op jit(solution)/shard_map/ppermute | solution.py:272
  107.8 0.5 multiply_bitcast_fusion
  (30 shorter events, 0.2 us)
Async XLA Ops:
  2.3 8.0 %copy-start.1 = (bf16[80,128]{1,0:T(8,128)(2,1)S(1)}, bf16[80,128]{1,0:T(8,128)(2,1)}, u32[]{:S(2)}) copy-start(bf16[80,128]{1,0:T(8,128)(2,1)} %pack.1) | copy-start | bytes 61444
  2.3 4.0 %collective-permute-start.2 = (bf16[1,80,128]{2,1,0:T(8,128)(2,1)}, bf16[1,80,128]{2,1,0:T(8,128)(2,1)S(1)}, u32[]{:S(2)}, u32[]{:S(2)}) collective-permute-start(bf16[1,80,128]{2,1,0:T(8,128)(2,1)} %bitcast.16), channel_id=1, source_target_pairs={{0,8},{8,0},{16,24},{24,16},{32,40},{40,32},{48,56},{56,48},{1,9},... | collective-permute-start | bytes 61448 | tf_op jit(solution)/shard_map/ppermute | solution.py:239
  7.0 5.2 %collective-permute-start.3 = (bf16[2,80,128]{2,1,0:T(8,128)(2,1)S(1)}, bf16[2,80,128]{2,1,0:T(8,128)(2,1)S(1)}, u32[]{:S(2)}, u32[]{:S(2)}) collective-permute-start(bf16[2,80,128]{2,1,0:T(8,128)(2,1)S(1)} %pad_maximum_fusion.4), channel_id=1, source_target_pairs={{0,16},{8,24},{16,0},{24,8},{32,48},{40,56},{48,32},{56,40},{1,17}... | collective-permute-start | bytes 122888 | tf_op jit(solution)/shard_map/ppermute | solution.py:239
  12.3 8.1 %collective-permute-start.4 = (bf16[4,80,128]{2,1,0:T(8,128)(2,1)S(1)}, bf16[4,80,128]{2,1,0:T(8,128)(2,1)S(1)}, u32[]{:S(2)}, u32[]{:S(2)}) collective-permute-start(bf16[4,80,128]{2,1,0:T(8,128)(2,1)S(1)} %pad_maximum_fusion.3), channel_id=1, source_target_pairs={{0,56},{8,48},{16,40},{24,32},{32,24},{40,16},{48,8},{56,0},{1,57}... | collective-permute-start | bytes 245768 | tf_op jit(solution)/shard_map/ppermute | solution.py:239
  20.4 5.4 %collective-permute-start.5 = (bf16[8,80,128]{2,1,0:T(8,128)(2,1)S(1)}, bf16[8,80,128]{2,1,0:T(8,128)(2,1)S(1)}, u32[]{:S(2)}, u32[]{:S(2)}) collective-permute-start(bf16[8,80,128]{2,1,0:T(8,128)(2,1)S(1)} %pad_maximum_fusion), channel_id=1, source_target_pairs={{0,2},{2,0},{4,6},{6,4},{1,3},{3,1},{5,7},{7,5},{8,10},{10,8},{12,... | collective-permute-start | bytes 491528 | tf_op jit(solution)/shard_map/ppermute | solution.py:239
  21.4 12.9 %copy-start.10 = (s32[96]{0:T(128)S(1)}, s32[96]{0:T(128)}, u32[]{:S(2)}) copy-start(s32[96]{0:T(128)} %param.15) | copy-start | bytes 1156
  25.8 8.5 %copy-start.9 = (f32[96]{0:T(128)S(1)}, f32[96]{0:T(128)}, u32[]{:S(2)}) copy-start(f32[96]{0:T(128)} %param.14) | copy-start | bytes 1156
  25.9 19.1 %copy-start.2 = (bf16[16,80,128]{2,1,0:T(8,128)(2,1)}, bf16[16,80,128]{2,1,0:T(8,128)(2,1)S(1)}, u32[]{:S(2)}) copy-start(bf16[16,80,128]{2,1,0:T(8,128)(2,1)S(1)} %constant_dynamic-update-slice_fusion.unit_ref) | copy-start | bytes 983044
  25.9 8.4 %collective-permute-start.6 = (bf16[16,80,128]{2,1,0:T(8,128)(2,1)S(1)}, bf16[16,80,128]{2,1,0:T(8,128)(2,1)S(1)}, u32[]{:S(2)}, u32[]{:S(2)}) collective-permute-start(bf16[16,80,128]{2,1,0:T(8,128)(2,1)S(1)} %constant_dynamic-update-slice_fusion.unit_ref), channel_id=1, source_target_pairs={{0,6},{2,4},{4,2},{6,0},{1,7},{3,5},{5,3},{7,1},{8,14},{10,12},{12... | collective-permute-start | bytes 983048 | tf_op jit(solution)/shard_map/ppermute | solution.py:247
  26.4 23.3 %collective-permute-start.8 = (bf16[16,80,128]{2,1,0:T(8,128)(2,1)S(1)}, bf16[16,80,128]{2,1,0:T(8,128)(2,1)S(1)}, u32[]{:S(2)}, u32[]{:S(2)}) collective-permute-start(bf16[16,80,128]{2,1,0:T(8,128)(2,1)S(1)} %constant_dynamic-update-slice_fusion.unit_ref), channel_id=1, source_target_pairs={{0,1},{1,0},{2,3},{3,2},{4,5},{5,4},{6,7},{7,6},{8,9},{9,8},{10,11... | collective-permute-start | bytes 983048 | tf_op jit(solution)/shard_map/ppermute | solution.py:248
  34.2 15.4 %copy-start.3 = (bf16[16,80,128]{2,1,0:T(8,128)(2,1)}, bf16[16,80,128]{2,1,0:T(8,128)(2,1)S(1)}, u32[]{:S(2)}) copy-start(bf16[16,80,128]{2,1,0:T(8,128)(2,1)S(1)} %collective-permute-done.6.unit_ref) | copy-start | bytes 983044
  34.2 25.7 %collective-permute-start.7 = (bf16[16,80,128]{2,1,0:T(8,128)(2,1)S(1)}, bf16[16,80,128]{2,1,0:T(8,128)(2,1)S(1)}, u32[]{:S(2)}, u32[]{:S(2)}) collective-permute-start(bf16[16,80,128]{2,1,0:T(8,128)(2,1)S(1)} %collective-permute-done.6.unit_ref), channel_id=1, source_target_pairs={{0,1},{1,0},{2,3},{3,2},{4,5},{5,4},{6,7},{7,6},{8,9},{9,8},{10,11... | collective-permute-start | bytes 983048 | tf_op jit(solution)/shard_map/ppermute | solution.py:252
  34.3 0.7 copy-start.6
  34.3 0.8 copy-start.7
  34.3 0.8 copy-start.8
  35.1 3.7 %collective-permute-start = (f32[1,8,96]{2,1,0:T(8,128)S(1)}, f32[1,8,96]{2,1,0:T(8,128)S(1)}, u32[]{:S(2)}, u32[]{:S(2)}) collective-permute-start(f32[1,8,96]{2,1,0:T(8,128)S(1)} %bitcast.21), channel_id=1, source_target_pairs={{0,64},{64,0},{128,192},{192,128},{1,65},{65,1},{129,193},{193,129... | collective-permute-start | bytes 9224 | tf_op jit(solution)/shard_map/ppermute | solution.py:239
  38.8 4.9 %collective-permute-start.1 = (f32[2,8,96]{2,1,0:T(8,128)S(1)}, f32[2,8,96]{2,1,0:T(8,128)S(1)}, u32[]{:S(2)}, u32[]{:S(2)}) collective-permute-start(f32[2,8,96]{2,1,0:T(8,128)S(1)} %pad_maximum_fusion.6), channel_id=1, source_target_pairs={{0,192},{64,128},{128,64},{192,0},{1,193},{65,129},{129,65},{193,1... | collective-permute-start | bytes 18440 | tf_op jit(solution)/shard_map/ppermute | solution.py:239
  49.7 0.7 copy-start.5
  59.9 0.7 copy-start.4
  65.4 8.7 %copy-start = (f32[384,128]{1,0:T(8,128)S(1)}, f32[384,128]{1,0:T(8,128)}, u32[]{:S(2)}) copy-start(f32[384,128]{1,0:T(8,128)} %unit_product.7) | copy-start | bytes 589828
  66.4 5.9 %collective-permute-start.11 = (f32[4,48,128]{2,1,0:T(8,128)S(1)}, f32[4,48,128]{2,1,0:T(8,128)S(1)}, u32[]{:S(2)}, u32[]{:S(2)}) collective-permute-start(f32[4,48,128]{2,1,0:T(8,128)S(1)} %get-tuple-element.19), channel_id=1, source_target_pairs={{0,192},{64,128},{128,64},{192,0},{1,193},{65,129},{129,65},{193,1... | collective-permute-start | bytes 294920 | tf_op jit(solution)/shard_map/ppermute | solution.py:260
  69.5 4.6 %collective-permute-start.9 = (f32[4,48,128]{2,1,0:T(8,128)S(1)}, f32[4,48,128]{2,1,0:T(8,128)S(1)}, u32[]{:S(2)}, u32[]{:S(2)}) collective-permute-start(f32[4,48,128]{2,1,0:T(8,128)S(1)} %get-tuple-element.18), channel_id=1, source_target_pairs={{0,64},{64,0},{128,192},{192,128},{1,65},{65,1},{129,193},{193,129... | collective-permute-start | bytes 294920 | tf_op jit(solution)/shard_map/ppermute | solution.py:260
  74.2 5.9 %collective-permute-start.10 = (f32[4,48,128]{2,1,0:T(8,128)S(1)}, f32[4,48,128]{2,1,0:T(8,128)S(1)}, u32[]{:S(2)}, u32[]{:S(2)}) collective-permute-start(f32[4,48,128]{2,1,0:T(8,128)S(1)} %pad_maximum_fusion.1), channel_id=1, source_target_pairs={{0,192},{64,128},{128,64},{192,0},{1,193},{65,129},{129,65},{193,1... | collective-permute-start | bytes 294920 | tf_op jit(solution)/shard_map/ppermute | solution.py:260
  75.5 4.7 %collective-permute-start.12 = (f32[4,48,128]{2,1,0:T(8,128)S(1)}, f32[4,48,128]{2,1,0:T(8,128)S(1)}, u32[]{:S(2)}, u32[]{:S(2)}) collective-permute-start(f32[4,48,128]{2,1,0:T(8,128)S(1)} %pad_maximum_fusion.2), channel_id=1, source_target_pairs={{0,64},{64,0},{128,192},{192,128},{1,65},{65,1},{129,193},{193,129... | collective-permute-start | bytes 294920 | tf_op jit(solution)/shard_map/ppermute | solution.py:260
  82.7 0.7 copy-start.11
  83.3 1.2 %collective-permute-start.13 = (f32[1,128]{1,0:T(1,128)S(1)}, f32[1,128]{1,0:T(1,128)S(1)}, u32[]{:S(2)}, u32[]{:S(2)}) collective-permute-start(f32[1,128]{1,0:T(1,128)S(1)} %copy-done.11), channel_id=1, source_target_pairs={{0,1},{1,0},{2,3},{3,2},{4,5},{5,4},{6,7},{7,6},{8,9},{9,8},{10,11... | collective-permute-start | bytes 1544 | tf_op jit(solution)/shard_map/ppermute | solution.py:272
  84.5 3.6 %collective-permute-start.14 = (f32[1,128]{1,0:T(1,128)S(1)}, f32[1,128]{1,0:T(1,128)S(1)}, u32[]{:S(2)}, u32[]{:S(2)}) collective-permute-start(f32[1,128]{1,0:T(1,128)S(1)} %add.106), channel_id=1, source_target_pairs={{0,2},{2,0},{4,6},{6,4},{1,3},{3,1},{5,7},{7,5},{8,10},{10,8},{12,... | collective-permute-start | bytes 1544 | tf_op jit(solution)/shard_map/ppermute | solution.py:272
  88.1 5.1 %collective-permute-start.15 = (f32[1,128]{1,0:T(1,128)S(1)}, f32[1,128]{1,0:T(1,128)S(1)}, u32[]{:S(2)}, u32[]{:S(2)}) collective-permute-start(f32[1,128]{1,0:T(1,128)S(1)} %add.107), channel_id=1, source_target_pairs={{0,4},{2,6},{4,0},{6,2},{1,5},{3,7},{5,1},{7,3},{8,12},{10,14},{12... | collective-permute-start | bytes 1544 | tf_op jit(solution)/shard_map/ppermute | solution.py:272
  93.2 3.6 %collective-permute-start.16 = (f32[1,128]{1,0:T(1,128)S(1)}, f32[1,128]{1,0:T(1,128)S(1)}, u32[]{:S(2)}, u32[]{:S(2)}) collective-permute-start(f32[1,128]{1,0:T(1,128)S(1)} %add.108), channel_id=1, source_target_pairs={{0,8},{8,0},{16,24},{24,16},{32,40},{40,32},{48,56},{56,48},{1,9},... | collective-permute-start | bytes 1544 | tf_op jit(solution)/shard_map/ppermute | solution.py:272
  96.7 4.5 %collective-permute-start.17 = (f32[1,128]{1,0:T(1,128)S(1)}, f32[1,128]{1,0:T(1,128)S(1)}, u32[]{:S(2)}, u32[]{:S(2)}) collective-permute-start(f32[1,128]{1,0:T(1,128)S(1)} %add.109), channel_id=1, source_target_pairs={{0,16},{8,24},{16,0},{24,8},{32,48},{40,56},{48,32},{56,40},{1,17}... | collective-permute-start | bytes 1544 | tf_op jit(solution)/shard_map/ppermute | solution.py:272
  101.2 6.6 %collective-permute-start.18 = (f32[1,128]{1,0:T(1,128)S(1)}, f32[1,128]{1,0:T(1,128)S(1)}, u32[]{:S(2)}, u32[]{:S(2)}) collective-permute-start(f32[1,128]{1,0:T(1,128)S(1)} %add.110), channel_id=1, source_target_pairs={{0,56},{8,48},{16,40},{24,32},{32,24},{40,16},{48,8},{56,0},{1,57}... | collective-permute-start | bytes 1544 | tf_op jit(solution)/shard_map/ppermute | solution.py:272

commit v2 on v1

--- a/solution.py
+++ b/solution.py
@@ -19,7 +19,8 @@
 SLIP_ROWS = 3 * PIECE
 ROWS = SLIP_ROWS + SUB
 FRAME_STRIDE = 40
-UNIT = LANES // SUB
+NEAR_ORDER = (1, 0, 3, 2)
+FAR_ORDER = (2, 3, 0, 1)
 VIEW_SCALE = 3.0 / (2.0 * math.pi)
 
 
@@ -29,6 +30,20 @@
 
 def mirror_pairs(count):
     return [(i, count - 1 - i) for i in range(count)]
+
+
+VMEM_SPEC = pl.BlockSpec(memory_space=pltpu.VMEM)
+
+
+LIMITS = pltpu.CompilerParams(vmem_limit_bytes=12 * 2**20)
+
+
+def vmem_array(shape, dtype):
+    return pltpu.VMEM(shape, dtype)
+
+
+def in_vmem(array):
+    return pltpu.with_memory_space_constraint(array, pltpu.VMEM)
 
 
 def rounded(value):
@@ -77,34 +92,71 @@
     vmem = pl.BlockSpec(memory_space=pltpu.VMEM)
     return pl.pallas_call(
         pack_kernel,
-        out_shape=jax.ShapeDtypeStruct((ROWS, LANES), jnp.bfloat16),
+        out_shape=vmem_array((ROWS, LANES), jnp.bfloat16),
         in_specs=[smem, smem, smem, vmem, vmem, vmem, vmem],
         out_specs=vmem,
         scratch_shapes=[pltpu.VMEM((LANES, LANES), jnp.float32)],
+        compiler_params=LIMITS,
         name="pack",
     )(core, seg_strike, seg_dip, patch_pos, patch_depth[None, :], segment_ids[None, :], jnp.transpose(slip, (1, 0, 2)))
 
 
-def unit_kernel(sites_ref, unit_ref, acc_ref, out_ref, pix_ref, green_ref):
+def columns_kernel(sites_ref, pix_ref):
     blocks, _, width = sites_ref.shape
-    pixels = blocks * width
     for block in range(blocks):
         site = jnp.concatenate([sites_ref[block], jnp.zeros((SUB, LANES - width), jnp.float32)], axis=1)
         columns = jnp.transpose(site)[:width]
-        for f in range(5):
+        for f in range(SUB):
             column = columns[:, f : f + 1]
-            if f >= 2:
+            if 2 <= f < 5:
                 column = column * VIEW_SCALE
             pix_ref[f, block * width : (block + 1) * width, :] = jnp.broadcast_to(column, (width, LANES))
+
+
+def pixel_columns(sites):
+    pixels = sites.shape[0] * sites.shape[2]
+    return pl.pallas_call(
+        columns_kernel,
+        out_shape=vmem_array((SUB, pixels, LANES), jnp.float32),
+        in_specs=[VMEM_SPEC],
+        out_specs=VMEM_SPEC,
+        compiler_params=LIMITS,
+        name="pixel_columns",
+    )(in_vmem(sites))
+
+
+def unit_kernel(has_acc, pix_ref, unit_ref, *refs):
+    acc_ref = refs[0] if has_acc else None
+    out_ref, green_ref = refs[-2:]
+    pixels = pix_ref.shape[1]
     frames = unit_ref[:, SLIP_ROWS:ROWS, :].astype(jnp.float32).reshape(LANES, LANES)
     turned = jnp.transpose(frames)
-    total = acc_ref[...]
     step = 16
+    span = 64
+
+    def table_of(group):
+        slip = [
+            unit_ref[:, (k * GROUPS + group) * SUB : (k * GROUPS + group + 1) * SUB, :].reshape(LANES, LANES)
+            for k in range(3)
+        ]
+        return jnp.concatenate(slip, axis=0)
+
+    def add_product(group, here):
+        value = jnp.dot(green_ref[group % 2, here, :], table_of(group), preferred_element_type=jnp.float32)
+        if group == 0:
+            if has_acc:
+                value = value + acc_ref[here, :]
+        else:
+            value = value + out_ref[here, :]
+        out_ref[here, :] = value
+
     for group in range(GROUPS):
         base = FRAME_STRIDE * group
         rows = (turned[base : base + 8] + turned[base + 8 : base + 16]) + turned[base + 16 : base + 24]
+
         def spread(i):
             return jnp.broadcast_to(rows[i : i + 1], (step, LANES))
+
         src_e, src_n, d, s, c, sd, cd = [spread(i) for i in range(7)]
         dd = d * d
         d_sd = d * sd
@@ -113,8 +165,7 @@
         k1 = sd * cd * (1.0 / 6.0)
         k2 = sd * sd * (1.0 / 6.0)
 
-        def chunk(i, carry):
-            start = pl.multiple_of(i * step, step)
+        def chunk(start):
             here = pl.ds(start, step)
             e = pix_ref[0, here, :] - src_e
             n = pix_ref[1, here, :] - src_n
@@ -148,68 +199,86 @@
             q = y * sd - d_cd
             p = y * cd + d_sd
             f = (q * (rho3 * rho2)) * (h + w * d)
-            green_ref[here, 0:LANES] = (k0 * j0 - x * f).astype(jnp.bfloat16)
-            green_ref[here, LANES : 2 * LANES] = (k1 * j1 - p * f).astype(jnp.bfloat16)
-            green_ref[here, 2 * LANES : 3 * LANES] = (q * f - k2 * j1).astype(jnp.bfloat16)
+            slot = group % 2
+            green_ref[slot, here, 0:LANES] = (k0 * j0 - x * f).astype(jnp.bfloat16)
+            green_ref[slot, here, LANES : 2 * LANES] = (k1 * j1 - p * f).astype(jnp.bfloat16)
+            green_ref[slot, here, 2 * LANES : 3 * LANES] = (q * f - k2 * j1).astype(jnp.bfloat16)
+
+        def stretch(i, carry):
+            start = pl.multiple_of(i * span, span)
+            if group > 0:
+                add_product(group - 1, pl.ds(start, span))
+            for j in range(span // step):
+                chunk(pl.multiple_of(start + j * step, step))
             return carry
 
-        lax.fori_loop(0, pixels // step, chunk, 0, unroll=2)
-        slip = [
-            unit_ref[:, (k * GROUPS + group) * SUB : (k * GROUPS + group + 1) * SUB, :].reshape(LANES, LANES)
-            for k in range(3)
-        ]
-        table = jnp.concatenate(slip, axis=0)
-        total = total + jnp.dot(green_ref[...], table, preferred_element_type=jnp.float32)
-    out_ref[...] = total
-
-
-def unit_product(sites, unit, acc):
-    pixels = sites.shape[0] * sites.shape[2]
-    vmem = pl.BlockSpec(memory_space=pltpu.VMEM)
+        lax.fori_loop(0, pixels // span, stretch, 0)
+    add_product(GROUPS - 1, pl.ds(0, pixels))
+
+
+def unit_product(pix, unit, acc=None):
+    pixels = pix.shape[1]
     pairs = pixels * LANES * GROUPS
-    return pl.pallas_call(
-        unit_kernel,
-        out_shape=jax.ShapeDtypeStruct((pixels, LANES), jnp.float32),
-        in_specs=[vmem, vmem, vmem],
-        out_specs=vmem,
-        scratch_shapes=[
-            pltpu.VMEM((5, pixels, LANES), jnp.float32),
-            pltpu.VMEM((pixels, 3 * LANES), jnp.bfloat16),
-        ],
-        cost_estimate=pl.CostEstimate(flops=pairs * 3 * LANES * 2 + pairs * 80, transcendentals=2 * pairs, bytes_accessed=2**19),
+    arrays = [pix, unit] if acc is None else [pix, unit, acc]
+    return pl.pallas_call(
+        functools.partial(unit_kernel, acc is not None),
+        out_shape=vmem_array((pixels, LANES), jnp.float32),
+        in_specs=[VMEM_SPEC] * len(arrays),
+        out_specs=VMEM_SPEC,
+        scratch_shapes=[pltpu.VMEM((2, pixels, 3 * LANES), jnp.bfloat16)],
+        cost_estimate=pl.CostEstimate(flops=pairs * 1000, transcendentals=2 * pairs, bytes_accessed=2**19),
+        compiler_params=LIMITS,
         name="unit_product",
-    )(sites, unit, acc)
-
-
-def residual_kernel(sites_ref, pred_ref, res_ref, sum_ref):
-    blocks, _, width = sites_ref.shape
+    )(*[in_vmem(array) for array in arrays])
+
+
+def residual_kernel(pix_ref, low_ref, low_got_ref, high_ref, high_got_ref, res_ref, sum_ref):
+    half = low_ref.shape[1]
     sums = []
-    for block in range(blocks):
-        site = jnp.concatenate([sites_ref[block], jnp.zeros((SUB, LANES - width), jnp.float32)], axis=1)
-        columns = jnp.transpose(site)[:width]
-        value = pred_ref[block]
-        observed = jnp.broadcast_to(columns[:, 5:6], value.shape)
-        noise = jnp.broadcast_to(columns[:, 6:7], value.shape)
-        mask = jnp.broadcast_to(columns[:, 7:8], value.shape)
-        res = mask * (value - observed) / noise
-        if block == 0:
-            res_ref[...] = res
-        sums.append(jnp.sum(res * res, axis=0, keepdims=True))
+    for block in range(4):
+        total = jnp.zeros((1, LANES), jnp.float32)
+        for part, (mine, got, order) in enumerate(
+            [(low_ref, low_got_ref, FAR_ORDER), (high_ref, high_got_ref, NEAR_ORDER)]
+        ):
+            value = mine[block] + got[order[block]]
+            here = slice(block * 2 * half + part * half, block * 2 * half + (part + 1) * half)
+            res = pix_ref[7, here, :] * (value - pix_ref[5, here, :]) / pix_ref[6, here, :]
+            if block == 0:
+                res_ref[part * half : (part + 1) * half, :] = res
+            total = total + jnp.sum(res * res, axis=0, keepdims=True)
+        sums.append(total)
     sum_ref[...] = (sums[0] + sums[1]) + (sums[2] + sums[3])
 
 
-def residual_part(sites, pred):
-    vmem = pl.BlockSpec(memory_space=pltpu.VMEM)
+def residual_part(pix, low, low_got, high, high_got):
     return pl.pallas_call(
         residual_kernel,
         out_shape=(
-            jax.ShapeDtypeStruct(pred.shape[1:], jnp.float32),
-            jax.ShapeDtypeStruct((1, LANES), jnp.float32),
+            jax.ShapeDtypeStruct((2 * low.shape[1], LANES), jnp.float32),
+            vmem_array((1, LANES), jnp.float32),
         ),
-        in_specs=[vmem, vmem],
-        out_specs=(vmem, vmem),
+        in_specs=[VMEM_SPEC] * 5,
+        out_specs=(VMEM_SPEC, VMEM_SPEC),
+        compiler_params=LIMITS,
         name="residual_part",
-    )(sites, pred)
+    )(*[in_vmem(array) for array in (pix, low, low_got, high, high_got)])
+
+
+def exchange_add_kernel(low_ref, low_got_ref, high_ref, high_got_ref, low_out_ref, high_out_ref):
+    for i in range(4):
+        low_out_ref[i] = low_ref[i] + low_got_ref[NEAR_ORDER[i]]
+        high_out_ref[i] = high_ref[i] + high_got_ref[FAR_ORDER[i]]
+
+
+def exchange_add(low, low_got, high, high_got):
+    return pl.pallas_call(
+        exchange_add_kernel,
+        out_shape=(vmem_array(low.shape, jnp.float32), vmem_array(high.shape, jnp.float32)),
+        in_specs=[VMEM_SPEC] * 4,
+        out_specs=(VMEM_SPEC, VMEM_SPEC),
+        compiler_params=LIMITS,
+        name="exchange_add",
+    )(*[in_vmem(array) for array in (low, low_got, high, high_got)])
 
 
 def per_device(
@@ -238,35 +307,31 @@
     def join(value, axis, pairs):
         return jnp.concatenate([value, lax.ppermute(value, axis, pairs)], axis=0)
 
-    sites = join(join(sites, "y", y_near), "y", y_far)
     pieces = piece[None]
-    for pairs in z_steps:
-        pieces = join(pieces, "z", pairs)
+    pieces, sites = lax.optimization_barrier((join(pieces, "z", z_steps[0]), join(sites, "y", y_near)))
+    pieces, sites = lax.optimization_barrier((join(pieces, "z", z_steps[1]), join(sites, "y", y_far)))
+    pix = pixel_columns(sites)
+    pieces = join(pieces, "z", z_steps[2])
     swap = xor_pairs(2, 1)
     near = join(pieces, "x", x_near)
     far = lax.ppermute(near, "x", x_far)
     near_other = lax.ppermute(near, "pix", swap)
-    acc = jnp.zeros((4 * own_pixels, LANES), jnp.float32)
-    acc = unit_product(sites, near, acc)
-    acc = unit_product(sites, near_other, acc)
+    acc = unit_product(pix, near)
+    near_other, acc = lax.optimization_barrier((near_other, acc))
+    acc = unit_product(pix, near_other, acc)
+    far, acc = lax.optimization_barrier((far, acc))
     far_other = lax.ppermute(far, "pix", swap)
-    acc = unit_product(sites, far, acc)
-    acc = unit_product(sites, far_other, acc)
+    acc = unit_product(pix, far, acc)
+    far_other, acc = lax.optimization_barrier((far_other, acc))
+    acc = unit_product(pix, far_other, acc)
 
     part = acc.reshape(4, own_pixels, LANES)
     half = own_pixels // 2
-
-    def add(mine, axis, pairs, order):
-        other = lax.ppermute(mine, axis, pairs)
-        return jnp.stack([mine[i] + other[j] for i, j in enumerate(order)])
-
     low, high = part[:, :half], part[:, half:]
-    low = add(low, "y", y_near, (1, 0, 3, 2))
-    high = add(high, "y", y_far, (2, 3, 0, 1))
-    low = add(low, "y", y_far, (2, 3, 0, 1))
-    high = add(high, "y", y_near, (1, 0, 3, 2))
-    pred = jnp.concatenate([low, high], axis=1)
-    residual, own_sum = residual_part(sites, pred)
+    low, high = exchange_add(low, lax.ppermute(low, "y", y_near), high, lax.ppermute(high, "y", y_far))
+    residual, own_sum = residual_part(
+        pix, low, lax.ppermute(low, "y", y_far), high, lax.ppermute(high, "y", y_near)
+    )
     total = own_sum
     for axis, pairs in [("pix", swap), ("x", x_near), ("x", xor_pairs(4, 2))] + [("z", pairs) for pairs in z_steps]:
         total = total + lax.ppermute(total, axis, pairs)

time: 109 us -> 89.2 us (0.82)
  Pallas kernels: 22.5 us -> 13.3 us
  waiting for transfers between devices: 50.6 us -> 43.9 us
  starting transfers between devices: 27.2 us -> 24.9 us
  other arithmetic: 2.66 us -> 1.23 us
    pallas_call x6 -> x8, Pallas kernels: 22.5 us -> 13.3 us  [the longest x4 11.1 us: unit_product(): pl.pallas_call(functools.partial(unit_kernel, acc is not None), out_shape...]
    ppermute x6, waiting for transfers between devices: 16.7 us -> 12.6 us  [join(): return jnp.concatenate([value, lax.ppermute(value, axis, pairs)], axis=0)]
    ppermute x1, waiting for transfers between devices: 7.8 us -> 4.49 us  [per_device(): far = lax.ppermute(near, 'x', x_far)]
    ppermute x4, starting transfers between devices: 4.49 us -> 2.98 us  [the longest x1 1.83 us: per_device(): lax.ppermute(low, 'y', y_far)]
    concatenate x5, other arithmetic: 1.37 us -> 0.04 us  [join(): return jnp.concatenate([value, lax.ppermute(value, axis, pairs)], axis=0)]
    unnamed x28 -> x14, local copies, waits for them, and re-layouts: 2.93 us -> 4.08 us
  transfers between devices with their start and end apart: 19 -> 19, of which waited for: 17 -> 14; matrix products, arithmetic and copies ran while one was open for 1% -> 0% of each run, Pallas kernels for 13% -> 11%
where the time goes in v2:
time: 89.2 us; the launch traced here: 89 us
  waiting for transfers between devices  43.9 us (49%)
  starting transfers between devices  24.9 us (28%)
  Pallas kernels  13.3 us (15%)
  local copies, waits for them, and re-layouts  4.84 us (5%)
  other arithmetic  1.23 us (1%)
    ppermute x6, waiting for transfers between devices, per_device(): total = total + lax.ppermute(total, axis, pairs)  16.8 us
    ppermute x6, starting transfers between devices, join(): return jnp.concatenate([value, lax.ppermute(value, axis, pairs)], axis=0)  13.7 us
    ppermute x6, waiting for transfers between devices, join(): return jnp.concatenate([value, lax.ppermute(value, axis, pairs)], axis=0)  12.6 us
    pallas_call x4, Pallas kernels, unit_product(): pl.pallas_call(functools.partial(unit_kernel, acc is not None), out_shape...  11.1 us
    ppermute x6, starting transfers between devices, per_device(): total = total + lax.ppermute(total, axis, pairs)  7.58 us
    ppermute x1, waiting for transfers between devices, per_device(): lax.ppermute(high, 'y', y_far)  5.35 us
    ppermute x1, waiting for transfers between devices, per_device(): far = lax.ppermute(near, 'x', x_far)  4.49 us
    unnamed x14, local copies, waits for them, and re-layouts  4.08 us
  transfers between devices with their start and end apart: 19, of which 14 were waited for; matrix products, arithmetic and copies ran while one was open for 0% of the time, Pallas kernels for 11%

profile of v2, /device:TPU:38, one launch (start us, length us, event | category | flops | bytes accessed | tf_op | source)
XLA Modules:
  0.0 89.0 jit_solution(15807723789181492316)
XLA Ops:
  0.6 0.7 convert_bitcast_fusion
  1.3 0.7 concatenate.23
  2.0 1.7 %collective-permute-start.1 = (f32[1,8,96]{2,1,0:T(8,128)S(1)}, f32[1,8,96]{2,1,0:T(8,128)S(1)}, u32[]{:S(2)}, u32[]{:S(2)}) collective-permute-start(f32[1,8,96]{2,1,0:T(8,128)S(1)} %bitcast.19), channel_id=1, source_target_pairs={{0,64},{64,0},{128,192},{192,128},{1,65},{65,1},{129,193},{193,129... | collective-permute-start | bytes 9224 | tf_op jit(solution)/shard_map/ppermute | solution.py:308
  3.7 0.0 copy-start
  3.7 0.8 copy-done
  4.4 0.0 copy-start.1
  4.4 0.7 copy-done.1
  5.1 0.0 copy-start.2
  5.1 0.7 copy-done.2
  5.8 0.0 copy-start.3
  5.8 0.7 copy-done.3
  6.4 0.0 copy-start.4
  6.4 0.7 copy-done.4
  7.1 0.0 copy-start.5
  7.1 0.7 copy-done.5
  7.7 0.8 pack.1
  8.5 0.1 collective-permute-start
  8.6 0.0 collective-permute-done.1
  8.7 3.7 %collective-permute-done = bf16[1,80,128]{2,1,0:T(8,128)(2,1)S(1)} collective-permute-done((bf16[1,80,128]{2,1,0:T(8,128)(2,1)S(1)}, bf16[1,80,128]{2,1,0:T(8,128)(2,1)S(1)}, u32[]{:S(2)}, u32[]{:S(2)}) %collective-permute-start) | collective-permute-done | bytes 20512 | tf_op jit(solution)/shard_map/ppermute | solution.py:308
  12.3 2.2 %collective-permute-start.3 = (f32[2,8,96]{2,1,0:T(8,128)S(1)}, f32[2,8,96]{2,1,0:T(8,128)S(1)}, u32[]{:S(2)}, u32[]{:S(2)}) collective-permute-start(f32[2,8,96]{2,1,0:T(8,128)S(1)} %pad_maximum_fusion.4), channel_id=1, source_target_pairs={{0,192},{64,128},{128,64},{192,0},{1,193},{65,129},{129,65},{193,1... | collective-permute-start | bytes 18440 | tf_op jit(solution)/shard_map/ppermute | solution.py:308
  14.5 3.3 %collective-permute-start.2 = (bf16[2,80,128]{2,1,0:T(8,128)(2,1)S(1)}, bf16[2,80,128]{2,1,0:T(8,128)(2,1)S(1)}, u32[]{:S(2)}, u32[]{:S(2)}) collective-permute-start(bf16[2,80,128]{2,1,0:T(8,128)(2,1)S(1)} %pad_maximum_fusion.2), channel_id=1, source_target_pairs={{0,16},{8,24},{16,0},{24,8},{32,48},{40,56},{48,32},{56,40},{1,17}... | collective-permute-start | bytes 122888 | tf_op jit(solution)/shard_map/ppermute | solution.py:308
  17.8 0.0 collective-permute-done.3
  17.8 2.0 %collective-permute-done.2 = bf16[2,80,128]{2,1,0:T(8,128)(2,1)S(1)} collective-permute-done((bf16[2,80,128]{2,1,0:T(8,128)(2,1)S(1)}, bf16[2,80,128]{2,1,0:T(8,128)(2,1)S(1)}, u32[]{:S(2)}, u32[]{:S(2)}) %collective-permute-start.2) | collective-permute-done | bytes 40992 | tf_op jit(solution)/shard_map/ppermute | solution.py:308
  19.8 5.6 %collective-permute-start.4 = (bf16[4,80,128]{2,1,0:T(8,128)(2,1)S(1)}, bf16[4,80,128]{2,1,0:T(8,128)(2,1)S(1)}, u32[]{:S(2)}, u32[]{:S(2)}) collective-permute-start(bf16[4,80,128]{2,1,0:T(8,128)(2,1)S(1)} %pad_maximum_fusion.1), channel_id=1, source_target_pairs={{0,56},{8,48},{16,40},{24,32},{32,24},{40,16},{48,8},{56,0},{1,57}... | collective-permute-start | bytes 245768 | tf_op jit(solution)/shard_map/ppermute | solution.py:308
  25.4 2.5 %collective-permute-done.4 = bf16[4,80,128]{2,1,0:T(8,128)(2,1)S(1)} collective-permute-done((bf16[4,80,128]{2,1,0:T(8,128)(2,1)S(1)}, bf16[4,80,128]{2,1,0:T(8,128)(2,1)S(1)}, u32[]{:S(2)}, u32[]{:S(2)}) %collective-permute-start.4) | collective-permute-done | bytes 81952 | tf_op jit(solution)/shard_map/ppermute | solution.py:308
  27.9 0.9 %collective-permute-start.5 = (bf16[8,80,128]{2,1,0:T(8,128)(2,1)S(1)}, bf16[8,80,128]{2,1,0:T(8,128)(2,1)S(1)}, u32[]{:S(2)}, u32[]{:S(2)}) collective-permute-start(bf16[8,80,128]{2,1,0:T(8,128)(2,1)S(1)} %pad_maximum_fusion), channel_id=1, source_target_pairs={{0,2},{2,0},{4,6},{6,4},{1,3},{3,1},{5,7},{7,5},{8,10},{10,8},{12,... | collective-permute-start | bytes 491528 | tf_op jit(solution)/shard_map/ppermute | solution.py:308
  28.8 4.5 %collective-permute-done.5 = bf16[8,80,128]{2,1,0:T(8,128)(2,1)S(1)} collective-permute-done((bf16[8,80,128]{2,1,0:T(8,128)(2,1)S(1)}, bf16[8,80,128]{2,1,0:T(8,128)(2,1)S(1)}, u32[]{:S(2)}, u32[]{:S(2)}) %collective-permute-start.5) | collective-permute-done | bytes 163872 | tf_op jit(solution)/shard_map/ppermute | solution.py:308
  33.3 0.1 collective-permute-start.7
  33.4 0.6 collective-permute-start.6
  34.0 0.7 pixel_columns.1.pix_ref
  34.7 2.8 %unit_product.4.refs_0_ = f32[384,128]{1,0:T(8,128)S(1)} custom-call(f32[8,384,128]{2,1,0:T(8,128)S(1)} %pixel_columns.1.pix_ref, bf16[16,80,128]{2,1,0:T(8,128)(2,1)S(1)} %constant_dynamic-update-slice_fusion.unit_ref), custom_call_target="tpu_custom_call" | custom-call | flops 147456000 | bytes 524288 | tf_op jit(solution)/shard_map/unit_product/pallas_call | solution.py:223
  37.5 0.0 collective-permute-done.7.unit_ref
  37.5 2.8 %unit_product.5.refs_0_ = f32[384,128]{1,0:T(8,128)S(1)} custom-call(f32[8,384,128]{2,1,0:T(8,128)S(1)} %pixel_columns.1.pix_ref, bf16[16,80,128]{2,1,0:T(8,128)(2,1)S(1)} %collective-permute-done.7.unit_ref, f32[384,128]{1,0:T(8,128)S(1)} %unit_product.4.refs_0_), custom_call_target="tpu_custom_call" | custom-call | flops 147456000 | bytes 524288 | tf_op jit(solution)/shard_map/unit_product/pallas_call | solution.py:223
  40.3 4.5 %collective-permute-done.6.unit_ref = bf16[16,80,128]{2,1,0:T(8,128)(2,1)S(1)} collective-permute-done((bf16[16,80,128]{2,1,0:T(8,128)(2,1)S(1)}, bf16[16,80,128]{2,1,0:T(8,128)(2,1)S(1)}, u32[]{:S(2)}, u32[]{:S(2)}) %collective-permute-start.6) | collective-permute-done | bytes 327712 | tf_op jit(solution)/shard_map/ppermute | solution.py:317
  44.8 0.0 collective-permute-start.8
  44.8 2.8 %unit_product.6.refs_0_ = f32[384,128]{1,0:T(8,128)S(1)} custom-call(f32[8,384,128]{2,1,0:T(8,128)S(1)} %pixel_columns.1.pix_ref, bf16[16,80,128]{2,1,0:T(8,128)(2,1)S(1)} %collective-permute-done.6.unit_ref, f32[384,128]{1,0:T(8,128)S(1)} %unit_product.5.refs_0_), custom_call_target="tpu_custom_call" | custom-call | flops 147456000 | bytes 524288 | tf_op jit(solution)/shard_map/unit_product/pallas_call | solution.py:223
  47.5 0.0 collective-permute-done.8.unit_ref
  47.6 2.8 %unit_product.7 = f32[384,128]{1,0:T(8,128)S(1)} custom-call(f32[8,384,128]{2,1,0:T(8,128)S(1)} %pixel_columns.1.pix_ref, bf16[16,80,128]{2,1,0:T(8,128)(2,1)S(1)} %collective-permute-done.8.unit_ref, f32[384,128]{1,0:T(8,128)S(1)} %unit_product.6.refs_0_), custom_call_target="tpu_custom_call" | custom-call | flops 147456000 | bytes 524288 | tf_op jit(solution)/shard_map/unit_product/pallas_call | solution.py:223
  50.4 1.1 %collective-permute-start.10 = (f32[4,48,128]{2,1,0:T(8,128)S(1)}, f32[4,48,128]{2,1,0:T(8,128)S(1)}, u32[]{:S(2)}, u32[]{:S(2)}) collective-permute-start(f32[4,48,128]{2,1,0:T(8,128)S(1)} %get-tuple-element.30.high_ref), channel_id=1, source_target_pairs={{0,192},{64,128},{128,64},{192,0},{1,193},{65,129},{129,65},{193,1... | collective-permute-start | bytes 294920 | tf_op jit(solution)/shard_map/ppermute | solution.py:331
  51.5 0.0 collective-permute-start.9
  51.5 5.4 %collective-permute-done.10.high_got_ref = f32[4,48,128]{2,1,0:T(8,128)S(1)} collective-permute-done((f32[4,48,128]{2,1,0:T(8,128)S(1)}, f32[4,48,128]{2,1,0:T(8,128)S(1)}, u32[]{:S(2)}, u32[]{:S(2)}) %collective-permute-start.10) | collective-permute-done | bytes 98336 | tf_op jit(solution)/shard_map/ppermute | solution.py:331
  56.9 0.0 collective-permute-done.9.low_got_ref
  56.9 1.8 %collective-permute-start.11 = (f32[4,48,128]{2,1,0:T(8,128)S(1)}, f32[4,48,128]{2,1,0:T(8,128)S(1)}, u32[]{:S(2)}, u32[]{:S(2)}) collective-permute-start(f32[4,48,128]{2,1,0:T(8,128)S(1)} %get-tuple-element.26.low_ref), channel_id=1, source_target_pairs={{0,192},{64,128},{128,64},{192,0},{1,193},{65,129},{129,65},{193,1... | collective-permute-start | bytes 294920 | tf_op jit(solution)/shard_map/ppermute | solution.py:333
  58.7 0.0 collective-permute-start.12
  58.7 4.1 %collective-permute-done.11.low_got_ref = f32[4,48,128]{2,1,0:T(8,128)S(1)} collective-permute-done((f32[4,48,128]{2,1,0:T(8,128)S(1)}, f32[4,48,128]{2,1,0:T(8,128)S(1)}, u32[]{:S(2)}, u32[]{:S(2)}) %collective-permute-start.11) | collective-permute-done | bytes 98336 | tf_op jit(solution)/shard_map/ppermute | solution.py:333
  62.8 0.5 collective-permute-done.12.high_got_ref
  63.3 0.7 residual_part.1
  64.0 0.0 collective-permute-start.13
  64.0 1.2 %collective-permute-done.13 = f32[1,128]{1,0:T(1,128)S(1)} collective-permute-done((f32[1,128]{1,0:T(1,128)S(1)}, f32[1,128]{1,0:T(1,128)S(1)}, u32[]{:S(2)}, u32[]{:S(2)}) %collective-permute-start.13) | collective-permute-done | bytes 544 | tf_op jit(solution)/shard_map/ppermute | solution.py:337
  65.2 0.0 collective-permute-start.14
  65.2 3.6 %collective-permute-done.14 = f32[1,128]{1,0:T(1,128)S(1)} collective-permute-done((f32[1,128]{1,0:T(1,128)S(1)}, f32[1,128]{1,0:T(1,128)S(1)}, u32[]{:S(2)}, u32[]{:S(2)}) %collective-permute-start.14) | collective-permute-done | bytes 544 | tf_op jit(solution)/shard_map/ppermute | solution.py:337
  68.7 0.2 collective-permute-start.15
  68.9 4.9 %collective-permute-done.15 = f32[1,128]{1,0:T(1,128)S(1)} collective-permute-done((f32[1,128]{1,0:T(1,128)S(1)}, f32[1,128]{1,0:T(1,128)S(1)}, u32[]{:S(2)}, u32[]{:S(2)}) %collective-permute-start.15) | collective-permute-done | bytes 544 | tf_op jit(solution)/shard_map/ppermute | solution.py:337
  73.8 1.0 %collective-permute-start.16 = (f32[1,128]{1,0:T(1,128)S(1)}, f32[1,128]{1,0:T(1,128)S(1)}, u32[]{:S(2)}, u32[]{:S(2)}) collective-permute-start(f32[1,128]{1,0:T(1,128)S(1)} %add.20), channel_id=1, source_target_pairs={{0,8},{8,0},{16,24},{24,16},{32,40},{40,32},{48,56},{56,48},{1,9},... | collective-permute-start | bytes 1544 | tf_op jit(solution)/shard_map/ppermute | solution.py:337
  74.8 2.6 %collective-permute-done.16 = f32[1,128]{1,0:T(1,128)S(1)} collective-permute-done((f32[1,128]{1,0:T(1,128)S(1)}, f32[1,128]{1,0:T(1,128)S(1)}, u32[]{:S(2)}, u32[]{:S(2)}) %collective-permute-start.16) | collective-permute-done | bytes 544 | tf_op jit(solution)/shard_map/ppermute | solution.py:337
  77.4 1.4 %collective-permute-start.17 = (f32[1,128]{1,0:T(1,128)S(1)}, f32[1,128]{1,0:T(1,128)S(1)}, u32[]{:S(2)}, u32[]{:S(2)}) collective-permute-start(f32[1,128]{1,0:T(1,128)S(1)} %add.21), channel_id=1, source_target_pairs={{0,16},{8,24},{16,0},{24,8},{32,48},{40,56},{48,32},{56,40},{1,17}... | collective-permute-start | bytes 1544 | tf_op jit(solution)/shard_map/ppermute | solution.py:337
  78.8 3.0 %collective-permute-done.17 = f32[1,128]{1,0:T(1,128)S(1)} collective-permute-done((f32[1,128]{1,0:T(1,128)S(1)}, f32[1,128]{1,0:T(1,128)S(1)}, u32[]{:S(2)}, u32[]{:S(2)}) %collective-permute-start.17) | collective-permute-done | bytes 544 | tf_op jit(solution)/shard_map/ppermute | solution.py:337
  81.9 4.9 %collective-permute-start.18 = (f32[1,128]{1,0:T(1,128)S(1)}, f32[1,128]{1,0:T(1,128)S(1)}, u32[]{:S(2)}, u32[]{:S(2)}) collective-permute-start(f32[1,128]{1,0:T(1,128)S(1)} %add.22), channel_id=1, source_target_pairs={{0,56},{8,48},{16,40},{24,32},{32,24},{40,16},{48,8},{56,0},{1,57}... | collective-permute-start | bytes 1544 | tf_op jit(solution)/shard_map/ppermute | solution.py:337
  86.8 1.6 %collective-permute-done.18 = f32[1,128]{1,0:T(1,128)S(1)} collective-permute-done((f32[1,128]{1,0:T(1,128)S(1)}, f32[1,128]{1,0:T(1,128)S(1)}, u32[]{:S(2)}, u32[]{:S(2)}) %collective-permute-start.18) | collective-permute-done | bytes 544 | tf_op jit(solution)/shard_map/ppermute | solution.py:337
  88.4 0.5 multiply_bitcast_fusion
  (15 shorter events, 0.1 us)
Async XLA Ops:
  2.0 6.6 %collective-permute-start.1 = (f32[1,8,96]{2,1,0:T(8,128)S(1)}, f32[1,8,96]{2,1,0:T(8,128)S(1)}, u32[]{:S(2)}, u32[]{:S(2)}) collective-permute-start(f32[1,8,96]{2,1,0:T(8,128)S(1)} %bitcast.19), channel_id=1, source_target_pairs={{0,64},{64,0},{128,192},{192,128},{1,65},{65,1},{129,193},{193,129... | collective-permute-start | bytes 9224 | tf_op jit(solution)/shard_map/ppermute | solution.py:308
  3.7 0.8 copy-start
  4.4 0.7 copy-start.1
  5.1 0.7 copy-start.2
  5.8 0.7 copy-start.3
  6.4 0.7 copy-start.4
  7.1 0.7 copy-start.5
  8.5 3.8 %collective-permute-start = (bf16[1,80,128]{2,1,0:T(8,128)(2,1)S(1)}, bf16[1,80,128]{2,1,0:T(8,128)(2,1)S(1)}, u32[]{:S(2)}, u32[]{:S(2)}) collective-permute-start(bf16[1,80,128]{2,1,0:T(8,128)(2,1)S(1)} %bitcast.14), channel_id=1, source_target_pairs={{0,8},{8,0},{16,24},{24,16},{32,40},{40,32},{48,56},{56,48},{1,9},... | collective-permute-start | bytes 61448 | tf_op jit(solution)/shard_map/ppermute | solution.py:308
  12.3 5.5 %collective-permute-start.3 = (f32[2,8,96]{2,1,0:T(8,128)S(1)}, f32[2,8,96]{2,1,0:T(8,128)S(1)}, u32[]{:S(2)}, u32[]{:S(2)}) collective-permute-start(f32[2,8,96]{2,1,0:T(8,128)S(1)} %pad_maximum_fusion.4), channel_id=1, source_target_pairs={{0,192},{64,128},{128,64},{192,0},{1,193},{65,129},{129,65},{193,1... | collective-permute-start | bytes 18440 | tf_op jit(solution)/shard_map/ppermute | solution.py:308
  14.5 5.2 %collective-permute-start.2 = (bf16[2,80,128]{2,1,0:T(8,128)(2,1)S(1)}, bf16[2,80,128]{2,1,0:T(8,128)(2,1)S(1)}, u32[]{:S(2)}, u32[]{:S(2)}) collective-permute-start(bf16[2,80,128]{2,1,0:T(8,128)(2,1)S(1)} %pad_maximum_fusion.2), channel_id=1, source_target_pairs={{0,16},{8,24},{16,0},{24,8},{32,48},{40,56},{48,32},{56,40},{1,17}... | collective-permute-start | bytes 122888 | tf_op jit(solution)/shard_map/ppermute | solution.py:308
  19.8 8.1 %collective-permute-start.4 = (bf16[4,80,128]{2,1,0:T(8,128)(2,1)S(1)}, bf16[4,80,128]{2,1,0:T(8,128)(2,1)S(1)}, u32[]{:S(2)}, u32[]{:S(2)}) collective-permute-start(bf16[4,80,128]{2,1,0:T(8,128)(2,1)S(1)} %pad_maximum_fusion.1), channel_id=1, source_target_pairs={{0,56},{8,48},{16,40},{24,32},{32,24},{40,16},{48,8},{56,0},{1,57}... | collective-permute-start | bytes 245768 | tf_op jit(solution)/shard_map/ppermute | solution.py:308
  27.9 5.4 %collective-permute-start.5 = (bf16[8,80,128]{2,1,0:T(8,128)(2,1)S(1)}, bf16[8,80,128]{2,1,0:T(8,128)(2,1)S(1)}, u32[]{:S(2)}, u32[]{:S(2)}) collective-permute-start(bf16[8,80,128]{2,1,0:T(8,128)(2,1)S(1)} %pad_maximum_fusion), channel_id=1, source_target_pairs={{0,2},{2,0},{4,6},{6,4},{1,3},{3,1},{5,7},{7,5},{8,10},{10,8},{12,... | collective-permute-start | bytes 491528 | tf_op jit(solution)/shard_map/ppermute | solution.py:308
  33.3 4.1 %collective-permute-start.7 = (bf16[16,80,128]{2,1,0:T(8,128)(2,1)S(1)}, bf16[16,80,128]{2,1,0:T(8,128)(2,1)S(1)}, u32[]{:S(2)}, u32[]{:S(2)}) collective-permute-start(bf16[16,80,128]{2,1,0:T(8,128)(2,1)S(1)} %constant_dynamic-update-slice_fusion.unit_ref), channel_id=1, source_target_pairs={{0,1},{1,0},{2,3},{3,2},{4,5},{5,4},{6,7},{7,6},{8,9},{9,8},{10,11... | collective-permute-start | bytes 983048 | tf_op jit(solution)/shard_map/ppermute | solution.py:318
  33.4 11.3 %collective-permute-start.6 = (bf16[16,80,128]{2,1,0:T(8,128)(2,1)S(1)}, bf16[16,80,128]{2,1,0:T(8,128)(2,1)S(1)}, u32[]{:S(2)}, u32[]{:S(2)}) collective-permute-start(bf16[16,80,128]{2,1,0:T(8,128)(2,1)S(1)} %constant_dynamic-update-slice_fusion.unit_ref), channel_id=1, source_target_pairs={{0,6},{2,4},{4,2},{6,0},{1,7},{3,5},{5,3},{7,1},{8,14},{10,12},{12... | collective-permute-start | bytes 983048 | tf_op jit(solution)/shard_map/ppermute | solution.py:317
  44.8 2.8 %collective-permute-start.8 = (bf16[16,80,128]{2,1,0:T(8,128)(2,1)S(1)}, bf16[16,80,128]{2,1,0:T(8,128)(2,1)S(1)}, u32[]{:S(2)}, u32[]{:S(2)}) collective-permute-start(bf16[16,80,128]{2,1,0:T(8,128)(2,1)S(1)} %collective-permute-done.6.unit_ref), channel_id=1, source_target_pairs={{0,1},{1,0},{2,3},{3,2},{4,5},{5,4},{6,7},{7,6},{8,9},{9,8},{10,11... | collective-permute-start | bytes 983048 | tf_op jit(solution)/shard_map/ppermute | solution.py:323
  50.4 6.5 %collective-permute-start.10 = (f32[4,48,128]{2,1,0:T(8,128)S(1)}, f32[4,48,128]{2,1,0:T(8,128)S(1)}, u32[]{:S(2)}, u32[]{:S(2)}) collective-permute-start(f32[4,48,128]{2,1,0:T(8,128)S(1)} %get-tuple-element.30.high_ref), channel_id=1, source_target_pairs={{0,192},{64,128},{128,64},{192,0},{1,193},{65,129},{129,65},{193,1... | collective-permute-start | bytes 294920 | tf_op jit(solution)/shard_map/ppermute | solution.py:331
  51.5 5.4 %collective-permute-start.9 = (f32[4,48,128]{2,1,0:T(8,128)S(1)}, f32[4,48,128]{2,1,0:T(8,128)S(1)}, u32[]{:S(2)}, u32[]{:S(2)}) collective-permute-start(f32[4,48,128]{2,1,0:T(8,128)S(1)} %get-tuple-element.31.low_ref), channel_id=1, source_target_pairs={{0,64},{64,0},{128,192},{192,128},{1,65},{65,1},{129,193},{193,129... | collective-permute-start | bytes 294920 | tf_op jit(solution)/shard_map/ppermute | solution.py:331
  56.9 5.9 %collective-permute-start.11 = (f32[4,48,128]{2,1,0:T(8,128)S(1)}, f32[4,48,128]{2,1,0:T(8,128)S(1)}, u32[]{:S(2)}, u32[]{:S(2)}) collective-permute-start(f32[4,48,128]{2,1,0:T(8,128)S(1)} %get-tuple-element.26.low_ref), channel_id=1, source_target_pairs={{0,192},{64,128},{128,64},{192,0},{1,193},{65,129},{129,65},{193,1... | collective-permute-start | bytes 294920 | tf_op jit(solution)/shard_map/ppermute | solution.py:333
  58.7 4.6 %collective-permute-start.12 = (f32[4,48,128]{2,1,0:T(8,128)S(1)}, f32[4,48,128]{2,1,0:T(8,128)S(1)}, u32[]{:S(2)}, u32[]{:S(2)}) collective-permute-start(f32[4,48,128]{2,1,0:T(8,128)S(1)} %get-tuple-element.27.high_ref), channel_id=1, source_target_pairs={{0,64},{64,0},{128,192},{192,128},{1,65},{65,1},{129,193},{193,129... | collective-permute-start | bytes 294920 | tf_op jit(solution)/shard_map/ppermute | solution.py:333
  64.0 1.2 %collective-permute-start.13 = (f32[1,128]{1,0:T(1,128)S(1)}, f32[1,128]{1,0:T(1,128)S(1)}, u32[]{:S(2)}, u32[]{:S(2)}) collective-permute-start(f32[1,128]{1,0:T(1,128)S(1)} %get-tuple-element.29), channel_id=1, source_target_pairs={{0,1},{1,0},{2,3},{3,2},{4,5},{5,4},{6,7},{7,6},{8,9},{9,8},{10,11... | collective-permute-start | bytes 1544 | tf_op jit(solution)/shard_map/ppermute | solution.py:337
  65.2 3.6 %collective-permute-start.14 = (f32[1,128]{1,0:T(1,128)S(1)}, f32[1,128]{1,0:T(1,128)S(1)}, u32[]{:S(2)}, u32[]{:S(2)}) collective-permute-start(f32[1,128]{1,0:T(1,128)S(1)} %add.18), channel_id=1, source_target_pairs={{0,2},{2,0},{4,6},{6,4},{1,3},{3,1},{5,7},{7,5},{8,10},{10,8},{12,... | collective-permute-start | bytes 1544 | tf_op jit(solution)/shard_map/ppermute | solution.py:337
  68.7 5.1 %collective-permute-start.15 = (f32[1,128]{1,0:T(1,128)S(1)}, f32[1,128]{1,0:T(1,128)S(1)}, u32[]{:S(2)}, u32[]{:S(2)}) collective-permute-start(f32[1,128]{1,0:T(1,128)S(1)} %add.19), channel_id=1, source_target_pairs={{0,4},{2,6},{4,0},{6,2},{1,5},{3,7},{5,1},{7,3},{8,12},{10,14},{12... | collective-permute-start | bytes 1544 | tf_op jit(solution)/shard_map/ppermute | solution.py:337
  73.8 3.6 %collective-permute-start.16 = (f32[1,128]{1,0:T(1,128)S(1)}, f32[1,128]{1,0:T(1,128)S(1)}, u32[]{:S(2)}, u32[]{:S(2)}) collective-permute-start(f32[1,128]{1,0:T(1,128)S(1)} %add.20), channel_id=1, source_target_pairs={{0,8},{8,0},{16,24},{24,16},{32,40},{40,32},{48,56},{56,48},{1,9},... | collective-permute-start | bytes 1544 | tf_op jit(solution)/shard_map/ppermute | solution.py:337
  77.4 4.5 %collective-permute-start.17 = (f32[1,128]{1,0:T(1,128)S(1)}, f32[1,128]{1,0:T(1,128)S(1)}, u32[]{:S(2)}, u32[]{:S(2)}) collective-permute-start(f32[1,128]{1,0:T(1,128)S(1)} %add.21), channel_id=1, source_target_pairs={{0,16},{8,24},{16,0},{24,8},{32,48},{40,56},{48,32},{56,40},{1,17}... | collective-permute-start | bytes 1544 | tf_op jit(solution)/shard_map/ppermute | solution.py:337
  81.9 6.6 %collective-permute-start.18 = (f32[1,128]{1,0:T(1,128)S(1)}, f32[1,128]{1,0:T(1,128)S(1)}, u32[]{:S(2)}, u32[]{:S(2)}) collective-permute-start(f32[1,128]{1,0:T(1,128)S(1)} %add.22), channel_id=1, source_target_pairs={{0,56},{8,48},{16,40},{24,32},{32,24},{40,16},{48,8},{56,0},{1,57}... | collective-permute-start | bytes 1544 | tf_op jit(solution)/shard_map/ppermute | solution.py:337

commit v3 on v2

v3 whole, which is shorter than its diff:
```python
import functools
import math

import jax
import jax.numpy as jnp
from jax import lax
from jax.experimental import pallas as pl
from jax.experimental.pallas import tpu as pltpu
from jax.sharding import Mesh
from jax.sharding import PartitionSpec as P


PATCH = ("y", "z", "x")
PATCH_PIX = ("y", "z", "x", "pix")

LANES = 128
SUB = 8
GROUPS = 3
PIECE = SUB * GROUPS
SLIP_ROWS = 3 * PIECE
ROWS = SLIP_ROWS + SUB
FRAME_STRIDE = 40
NEAR_ORDER = (1, 0, 3, 2)
FAR_ORDER = (2, 3, 0, 1)
VIEW_SCALE = 3.0 / (2.0 * math.pi)


def xor_pairs(count, mask):
    return [(i, i ^ mask) for i in range(count)]


def mirror_pairs(count):
    return [(i, count - 1 - i) for i in range(count)]


VMEM_SPEC = pl.BlockSpec(memory_space=pltpu.VMEM)


LIMITS = pltpu.CompilerParams(vmem_limit_bytes=12 * 2**20)


def vmem_array(shape, dtype):
    return pltpu.VMEM(shape, dtype)


def in_hbm(array):
    return pltpu.with_memory_space_constraint(array, pltpu.HBM)


def in_vmem(array):
    return pltpu.with_memory_space_constraint(array, pltpu.VMEM)


def rounded(value):
    return value.astype(jnp.bfloat16).astype(jnp.float32)


def prepare_kernel(
    core_ref,
    strike_ref,
    dip_ref,
    pos_ref,
    depth_ref,
    ids_ref,
    slip_ref,
    pixel_ref,
    view_ref,
    observed_ref,
    noise_ref,
    mask_ref,
    out_ref,
    sites_ref,
    turned_ref,
):
    ids = ids_ref[...]
    strike = jnp.zeros(ids.shape, jnp.float32)
    dip = jnp.zeros(ids.shape, jnp.float32)
    for segment in range(strike_ref.shape[0]):
        same = ids == segment
        strike = jnp.where(same, strike_ref[segment], strike)
        dip = jnp.where(same, dip_ref[segment], dip)
    pos = pos_ref[...]
    angles = jnp.concatenate([strike, dip], axis=0)
    sines = jnp.sin(angles)
    cosines = jnp.cos(angles)
    rows = jnp.concatenate(
        [pos, depth_ref[...], sines[0:1], cosines[0:1], sines[1:2], cosines[1:2], jnp.zeros(ids.shape, jnp.float32)],
        axis=0,
    )
    high = rounded(rows)
    rest = rows - high
    middle = rounded(rest)
    low = rounded(rest - middle)
    count = rows.shape[1]
    pieces = jnp.concatenate([high, middle, low], axis=0)
    pieces = jnp.concatenate([pieces, jnp.zeros((24, LANES - count), jnp.float32)], axis=1)
    pieces = jnp.concatenate([pieces, jnp.zeros((LANES - 24, LANES), jnp.float32)], axis=0)
    turned_ref[...] = jnp.transpose(pieces)
    first = core_ref[0] * PIECE
    tile = jnp.zeros((SUB, LANES), jnp.float32)
    for group in range(GROUPS):
        start = pl.multiple_of(first + SUB * group, SUB)
        part = turned_ref[pl.ds(start, SUB), :]
        tile = tile + (part if group == 0 else pltpu.roll(part, FRAME_STRIDE * group, 1))
        for k in range(3):
            row = (k * GROUPS + group) * SUB
            out_ref[row : row + SUB, :] = slip_ref[k, pl.ds(start, SUB), :]
    out_ref[SLIP_ROWS:ROWS, :] = tile.astype(jnp.bfloat16)
    site = jnp.concatenate(
        [pixel_ref[...], view_ref[...], observed_ref[...], noise_ref[...], mask_ref[...].astype(jnp.float32)], axis=0
    )
    sites_ref[0] = jnp.concatenate([site, jnp.zeros((SUB, LANES - site.shape[1]), jnp.float32)], axis=1)


def prepare(core, tables, patches, pixels):
    smem = pl.BlockSpec(memory_space=pltpu.SMEM)
    vectors = list(patches) + list(pixels)
    return pl.pallas_call(
        prepare_kernel,
        out_shape=(vmem_array((ROWS, LANES), jnp.bfloat16), vmem_array((1, SUB, LANES), jnp.float32)),
        in_specs=[smem] * 3 + [VMEM_SPEC] * len(vectors),
        out_specs=(VMEM_SPEC, VMEM_SPEC),
        scratch_shapes=[pltpu.VMEM((LANES, LANES), jnp.float32)],
        compiler_params=LIMITS,
        name="prepare",
    )(core, *[in_hbm(array) for array in list(tables) + vectors])


def columns_kernel(width, sites_ref, pix_ref):
    blocks = sites_ref.shape[0]
    half = width // 2
    for block in range(blocks):
        columns = jnp.transpose(sites_ref[block])[:width]
        for f in range(SUB):
            column = columns[:, f : f + 1]
            if 2 <= f < 5:
                column = column * VIEW_SCALE
            column = jnp.broadcast_to(column, (width, LANES))
            for part in range(2):
                row = (part * blocks + block) * half
                pix_ref[f, row : row + half, :] = column[part * half : (part + 1) * half]


def pixel_columns(sites, width):
    return pl.pallas_call(
        functools.partial(columns_kernel, width),
        out_shape=vmem_array((SUB, sites.shape[0] * width, LANES), jnp.float32),
        in_specs=[VMEM_SPEC],
        out_specs=VMEM_SPEC,
        compiler_params=LIMITS,
        name="pixel_columns",
    )(in_vmem(sites))


def unit_kernel(units, count, has_acc, first_row, pix_ref, *refs):
    parts_refs = refs[:count]
    acc_ref = refs[count] if has_acc else None
    out_ref, green_ref = refs[-2:]
    pixels = out_ref.shape[0]
    step = 16
    span = 96 if pixels % 96 == 0 else pixels

    def gathered(unit, row, rows):
        return jnp.concatenate(
            [parts_refs[which][start : start + size, row : row + rows, :] for which, start, size in units[unit]], axis=0
        )

    def table_of(index):
        unit, group = divmod(index, GROUPS)
        slip = [gathered(unit, (k * GROUPS + group) * SUB, SUB).reshape(LANES, LANES) for k in range(3)]
        return jnp.concatenate(slip, axis=0)

    def add_product(index, start, size):
        here = pl.ds(start, size)
        value = jnp.dot(green_ref[index % 2, here, :], table_of(index), preferred_element_type=jnp.float32)
        if index > 0:
            value = value + out_ref[here, :]
        elif has_acc:
            value = value + acc_ref[pl.ds(first_row + start, size), :]
        out_ref[here, :] = value

    for index in range(GROUPS * len(units)):
        unit, group = divmod(index, GROUPS)
        if group == 0:
            turned = jnp.transpose(gathered(unit, SLIP_ROWS, SUB).astype(jnp.float32).reshape(LANES, LANES))
        base = FRAME_STRIDE * group
        rows = (turned[base : base + 8] + turned[base + 8 : base + 16]) + turned[base + 16 : base + 24]

        def spread(i):
            return jnp.broadcast_to(rows[i : i + 1], (step, LANES))

        src_e, src_n, d, s, c, sd, cd = [spread(i) for i in range(7)]
        dd = d * d
        d_sd = d * sd
        d_cd = d * cd
        k0 = sd * (-1.0 / 6.0)
        k1 = sd * cd * (1.0 / 6.0)
        k2 = sd * sd * (1.0 / 6.0)

        def chunk(start):
            here = pl.ds(start, step)
            src = pl.ds(first_row + start, step)
            e = pix_ref[0, src, :] - src_e
            n = pix_ref[1, src, :] - src_n
            v0 = pix_ref[2, src, :]
            v1 = pix_ref[3, src, :]
            w = pix_ref[4, src, :]
            x = e * s + n * c
            y = n * s - e * c
            a = v0 * s + v1 * c
            b = v1 * s - v0 * c
            xx = x * x
            r2 = xx + y * y + dd
            rho = lax.rsqrt(r2)
            t = r2 * rho + d
            tau = 1.0 / t
            rho2 = rho * rho
            rho3 = rho2 * rho
            g = rho * tau
            g2 = g + rho2
            ga = g * tau
            gc = g * g2
            gb = ga * (g + g2)
            ax = a * x
            by = b * y
            ay = a * y
            bx = b * x
            h = ax + by
            xy = x * y
            j0 = ga * (ay + bx) - xy * (gb * h + w * gc)
            j1 = (ax * rho3 - ga * (ax - by)) + xy * (gb * (ay - bx)) + w * (g - xx * gc)
            q = y * sd - d_cd
            p = y * cd + d_sd
            f = (q * (rho3 * rho2)) * (h + w * d)
            slot = index % 2
            green_ref[slot, here, 0:LANES] = (k0 * j0 - x * f).astype(jnp.bfloat16)
            green_ref[slot, here, LANES : 2 * LANES] = (k1 * j1 - p * f).astype(jnp.bfloat16)
            green_ref[slot, here, 2 * LANES : 3 * LANES] = (q * f - k2 * j1).astype(jnp.bfloat16)

        def stretch(i, carry):
            start = pl.multiple_of(i * span, span)
            if index > 0:
                add_product(index - 1, start, span)
            for j in range(span // step):
                chunk(pl.multiple_of(start + j * step, step))
            return carry

        lax.fori_loop(0, pixels // span, stretch, 0)
    add_product(GROUPS * len(units) - 1, 0, pixels)


def unit_product(pix, parts, units, acc=None, first_row=0, pixels=None):
    pixels = pixels or pix.shape[1]
    pairs = pixels * LANES * GROUPS * len(units)
    arrays = [pix, *parts] + ([] if acc is None else [acc])
    return pl.pallas_call(
        functools.partial(unit_kernel, units, len(parts), acc is not None, first_row),
        out_shape=vmem_array((pixels, LANES), jnp.float32),
        in_specs=[VMEM_SPEC] * len(arrays),
        out_specs=VMEM_SPEC,
        scratch_shapes=[pltpu.VMEM((2, pixels, 3 * LANES), jnp.bfloat16)],
        compiler_params=LIMITS,
        cost_estimate=pl.CostEstimate(flops=pairs * 1000, transcendentals=2 * pairs, bytes_accessed=2**19),
        name="unit_product",
    )(*[in_vmem(array) for array in arrays])


def residual_kernel(pix_ref, low_ref, low_got_ref, high_ref, high_got_ref, res_ref, sum_ref):
    half = low_ref.shape[1]
    sums = []
    for block in range(4):
        total = jnp.zeros((1, LANES), jnp.float32)
        for part, (mine, got, order) in enumerate(
            [(low_ref, low_got_ref, NEAR_ORDER), (high_ref, high_got_ref, FAR_ORDER)]
        ):
            value = mine[block] + got[order[block]]
            row = (part * 4 + block) * half
            here = slice(row, row + half)
            res = pix_ref[7, here, :] * (value - pix_ref[5, here, :]) / pix_ref[6, here, :]
            if block == 0:
                res_ref[part * half : (part + 1) * half, :] = res
            total = total + jnp.sum(res * res, axis=0, keepdims=True)
        sums.append(total)
    sum_ref[...] = (sums[0] + sums[1]) + (sums[2] + sums[3])


def residual_part(pix, low, low_got, high, high_got):
    return pl.pallas_call(
        residual_kernel,
        out_shape=(
            jax.ShapeDtypeStruct((2 * low.shape[1], LANES), jnp.float32),
            vmem_array((1, LANES), jnp.float32),
        ),
        in_specs=[VMEM_SPEC] * 5,
        out_specs=(VMEM_SPEC, VMEM_SPEC),
        compiler_params=LIMITS,
        name="residual_part",
    )(*[in_vmem(array) for array in (pix, low, low_got, high, high_got)])


def exchange_add_kernel(order, mine_ref, got_ref, out_ref):
    for i in range(4):
        out_ref[i] = mine_ref[i] + got_ref[order[i]]


def exchange_add(mine, got, order):
    return pl.pallas_call(
        functools.partial(exchange_add_kernel, order),
        out_shape=vmem_array(mine.shape, jnp.float32),
        in_specs=[VMEM_SPEC] * 2,
        out_specs=VMEM_SPEC,
        compiler_params=LIMITS,
        name="exchange_add",
    )(in_vmem(mine), in_vmem(got))


def quad_sum(value, axis, core):
    count = lax.axis_size(axis)
    low = [(2 * (i ^ 1), 2 * i) for i in range(count)]
    high = [(2 * (i ^ 2) + 1, 2 * i + 1) for i in range(count)]
    first = lax.ppermute(value, (axis, "pix"), low + high)
    second = lax.ppermute(value, (axis, "pix"), [(2 * (i ^ 3) + 1, 2 * i + 1) for i in range(count)])
    half = first + jnp.where(core == 0, value, second)
    return half + lax.ppermute(half, "pix", xor_pairs(2, 1))


def per_device(
    pixel_pos,
    pixel_view,
    observed,
    noise_scale,
    valid_mask,
    patch_pos,
    patch_depth,
    segment_ids,
    seg_strike,
    seg_dip,
    slip_models,
):
    own_pixels = pixel_pos.shape[1]
    near_pairs, far_pairs, swap = xor_pairs(4, 1), xor_pairs(4, 3), xor_pairs(2, 1)
    core = lax.axis_index("pix").astype(jnp.int32)
    piece, sites = prepare(
        core[None],
        (seg_strike, seg_dip),
        (patch_pos, patch_depth[None], segment_ids[None], jnp.transpose(slip_models, (1, 0, 2))),
        (pixel_pos, pixel_view, observed[None], noise_scale[None], valid_mask[None]),
    )

    def stack(*values):
        return jnp.concatenate(values, axis=0)

    piece = piece[None]
    two, sites = lax.optimization_barrier(
        (stack(piece, lax.ppermute(piece, "z", xor_pairs(8, 2))), stack(sites, lax.ppermute(sites, "y", near_pairs)))
    )
    sites_far = lax.ppermute(sites, "y", far_pairs)
    four = stack(two, lax.ppermute(two, "z", mirror_pairs(8)))
    four_got = lax.ppermute(four, "z", xor_pairs(8, 1))
    far_a = lax.ppermute(four, "x", far_pairs)
    near_a = lax.ppermute(four, "x", near_pairs)
    pix = pixel_columns(stack(sites, sites_far), own_pixels)
    far_b = lax.ppermute(four_got, "x", far_pairs)
    near_b = lax.ppermute(four_got, "x", near_pairs)
    own_other = lax.ppermute(stack(four, four_got), "pix", swap)
    across_a = lax.ppermute(far_a, "x", near_pairs)
    part = four.shape[0]
    count = 2 * part
    acc = unit_product(pix, (four, four_got, own_other), (((0, 0, part), (1, 0, part), (2, 0, count)),))
    near_a, near_b, far_b, acc = lax.optimization_barrier((near_a, near_b, far_b, acc))
    across_b = lax.ppermute(far_b, "x", near_pairs)
    others = lax.ppermute(stack(near_a, near_b, far_a, far_b), "pix", swap)
    acc = unit_product(
        pix,
        (near_a, near_b, far_a, far_b, others),
        (((0, 0, part), (1, 0, part), (4, 0, count)), ((2, 0, part), (3, 0, part), (4, count, count))),
        acc,
    )
    across_a, across_b, acc = lax.optimization_barrier((across_a, across_b, acc))
    across = stack(across_a, across_b)
    across_other = lax.ppermute(across, "pix", swap)
    last = (((0, 0, count), (1, 0, count)),)
    rows = 2 * own_pixels
    shape = (4, own_pixels // 2, LANES)
    low = unit_product(pix, (across, across_other), last, acc, 0, rows).reshape(shape)
    high = unit_product(pix, (across, across_other), last, acc, rows, rows).reshape(shape)
    low = exchange_add(low, lax.ppermute(low, "y", far_pairs), FAR_ORDER)
    high = exchange_add(high, lax.ppermute(high, "y", near_pairs), NEAR_ORDER)
    residual, own_sum = residual_part(
        pix, low, lax.ppermute(low, "y", near_pairs), high, lax.ppermute(high, "y", far_pairs)
    )
    total = own_sum + lax.ppermute(own_sum, "pix", swap)
    total = quad_sum(total, "x", core)
    total = quad_sum(total, "z", core)
    total = total + lax.ppermute(total, "z", mirror_pairs(8))
    pixels = own_pixels * lax.axis_size(PATCH) * lax.axis_size("pix")
    return (residual, total[0] / pixels)


def solution(mesh):
    finer = Mesh(mesh.devices.reshape(4, 8, 4, mesh.shape["pix"]), PATCH_PIX)
    placed = (
        P(None, PATCH_PIX),
        P(None, PATCH_PIX),
        P(PATCH_PIX),
        P(PATCH_PIX),
        P(PATCH_PIX),
        P(None, PATCH),
        P(PATCH),
        P(PATCH),
        P(),
        P(),
        P(PATCH, None, None),
    )
    return jax.shard_map(
        per_device,
        mesh=finer,
        in_specs=placed,
        out_specs=(P(PATCH_PIX, None), P()),
        check_vma=False,
    )
```

time: 89.2 us -> 79.9 us (0.90)
  the two profiles are of different devices: /device:TPU:38 before, /device:TPU:1 now
where the time goes in v3:
time: 79.9 us; the launch traced here: 79.7 us
  starting transfers between devices  45.2 us (57%)
  waiting for transfers between devices  21.6 us (27%)
  Pallas kernels  11.5 us (14%)
  between operations  0.81 us (1%)
    pallas_call x4, Pallas kernels, unit_product(): pl.pallas_call(functools.partial(unit_kernel, units, len(parts), acc is n...  9.07 us
    ppermute x2, starting transfers between devices, quad_sum(): lax.ppermute(value, (axis, 'pix'), [(2 * (i ^ 3) + 1, 2 * i + 1) for i in...  7.2 us
    ppermute x1, starting transfers between devices, per_device(): four = stack(two, lax.ppermute(two, 'z', mirror_pairs(8)))  4.95 us
    ppermute x2, waiting for transfers between devices, quad_sum(): lax.ppermute(value, (axis, 'pix'), [(2 * (i ^ 3) + 1, 2 * i + 1) for i in...  4.37 us
    ppermute x1, starting transfers between devices, per_device(): own_other = lax.ppermute(stack(four, four_got), 'pix', swap)  4.04 us
    ppermute x1, starting transfers between devices, per_device(): total = total + lax.ppermute(total, 'z', mirror_pairs(8))  3.76 us
    ppermute x1, starting transfers between devices, per_device(): lax.ppermute(piece, 'z', xor_pairs(8, 2))  2.99 us
    ppermute x2, starting transfers between devices, quad_sum(): first = lax.ppermute(value, (axis, 'pix'), low + high)  2.7 us
  transfers between devices with their start and end apart: 26, of which 15 were waited for; matrix products, arithmetic and copies ran while one was open for 0% of the time, Pallas kernels for 11%

profile of v3, /device:TPU:1, one launch (start us, length us, event | category | flops | bytes accessed | tf_op | source)
XLA Modules:
  0.0 79.7 jit_solution(5209562414103792787)
XLA Ops:
  0.6 1.1 %prepare.1 = (bf16[80,128]{1,0:T(8,128)(2,1)S(1)}, f32[1,8,128]{2,1,0:T(8,128)S(1)}) custom-call(s32[1]{0:T(128)} %bitcast.core_ref, f32[16]{0:T(128)} %strike_ref.1, f32[16]{0:T(128)} %dip_ref.1, f32[2,48]{1,0:T(2,128)} %pos_ref.1, f32[1,48]{1,0:T(1,128)} %bitcast.19, s32[1,48]{1,0:T(1,128)} %bitcast.20, bf16[3,48,128]{2,1,0:T(8,128)(2,1)} %bitcast.18, ...), custom_call_target="tpu_custom_call" | custom-call | tf_op jit(solution)/shard_map/prepare/pallas_call | solution.py:118
  1.7 2.1 %collective-permute-start.1 = (f32[1,8,128]{2,1,0:T(8,128)S(1)}, f32[1,8,128]{2,1,0:T(8,128)S(1)}, u32[]{:S(2)}, u32[]{:S(2)}) collective-permute-start(f32[1,8,128]{2,1,0:T(8,128)S(1)} %get-tuple-element.16), channel_id=1, source_target_pairs={{0,64},{64,0},{128,192},{192,128},{1,65},{65,1},{129,193},{193,129... | collective-permute-start | bytes 12296 | tf_op jit(solution)/shard_map/ppermute | solution.py:355
  3.8 3.0 %collective-permute-start = (bf16[1,80,128]{2,1,0:T(8,128)(2,1)S(1)}, bf16[1,80,128]{2,1,0:T(8,128)(2,1)S(1)}, u32[]{:S(2)}, u32[]{:S(2)}) collective-permute-start(bf16[1,80,128]{2,1,0:T(8,128)(2,1)S(1)} %bitcast.16), channel_id=1, source_target_pairs={{0,16},{8,24},{16,0},{24,8},{32,48},{40,56},{48,32},{56,40},{1,17}... | collective-permute-start | bytes 61448 | tf_op jit(solution)/shard_map/ppermute | solution.py:355
  6.8 0.0 collective-permute-done.1
  6.8 1.2 %collective-permute-done = bf16[1,80,128]{2,1,0:T(8,128)(2,1)S(1)} collective-permute-done((bf16[1,80,128]{2,1,0:T(8,128)(2,1)S(1)}, bf16[1,80,128]{2,1,0:T(8,128)(2,1)S(1)}, u32[]{:S(2)}, u32[]{:S(2)}) %collective-permute-start) | collective-permute-done | bytes 20512 | tf_op jit(solution)/shard_map/ppermute | solution.py:355
  8.0 4.9 %collective-permute-start.3 = (bf16[2,80,128]{2,1,0:T(8,128)(2,1)S(1)}, bf16[2,80,128]{2,1,0:T(8,128)(2,1)S(1)}, u32[]{:S(2)}, u32[]{:S(2)}) collective-permute-start(bf16[2,80,128]{2,1,0:T(8,128)(2,1)S(1)} %pad_maximum_fusion.2), channel_id=1, source_target_pairs={{0,56},{8,48},{16,40},{24,32},{32,24},{40,16},{48,8},{56,0},{1,57}... | collective-permute-start | bytes 122888 | tf_op jit(solution)/shard_map/ppermute | solution.py:358
  13.0 1.4 %collective-permute-done.3 = bf16[2,80,128]{2,1,0:T(8,128)(2,1)S(1)} collective-permute-done((bf16[2,80,128]{2,1,0:T(8,128)(2,1)S(1)}, bf16[2,80,128]{2,1,0:T(8,128)(2,1)S(1)}, u32[]{:S(2)}, u32[]{:S(2)}) %collective-permute-start.3) | collective-permute-done | bytes 40992 | tf_op jit(solution)/shard_map/ppermute | solution.py:358
  14.3 1.7 %collective-permute-start.7 = (bf16[4,80,128]{2,1,0:T(8,128)(2,1)S(1)}, bf16[4,80,128]{2,1,0:T(8,128)(2,1)S(1)}, u32[]{:S(2)}, u32[]{:S(2)}) collective-permute-start(bf16[4,80,128]{2,1,0:T(8,128)(2,1)S(1)} %constant_dynamic-update-slice_fusion.refs_0_), channel_id=1, source_target_pairs={{0,8},{8,0},{16,24},{24,16},{32,40},{40,32},{48,56},{56,48},{1,9},... | collective-permute-start | bytes 245768 | tf_op jit(solution)/shard_map/ppermute | solution.py:359
  16.1 1.8 %collective-permute-done.7.refs_1_ = bf16[4,80,128]{2,1,0:T(8,128)(2,1)S(1)} collective-permute-done((bf16[4,80,128]{2,1,0:T(8,128)(2,1)S(1)}, bf16[4,80,128]{2,1,0:T(8,128)(2,1)S(1)}, u32[]{:S(2)}, u32[]{:S(2)}) %collective-permute-start.7) | collective-permute-done | bytes 81952 | tf_op jit(solution)/shard_map/ppermute | solution.py:359
  17.9 4.0 %collective-permute-start.10 = (bf16[8,80,128]{2,1,0:T(8,128)(2,1)S(1)}, bf16[8,80,128]{2,1,0:T(8,128)(2,1)S(1)}, u32[]{:S(2)}, u32[]{:S(2)}) collective-permute-start(bf16[8,80,128]{2,1,0:T(8,128)(2,1)S(1)} %pad_maximum_fusion.1), channel_id=1, source_target_pairs={{0,1},{1,0},{2,3},{3,2},{4,5},{5,4},{6,7},{7,6},{8,9},{9,8},{10,11... | collective-permute-start | bytes 491528 | tf_op jit(solution)/shard_map/ppermute | solution.py:365
  22.0 1.9 %collective-permute-start.2 = (f32[2,8,128]{2,1,0:T(8,128)S(1)}, f32[2,8,128]{2,1,0:T(8,128)S(1)}, u32[]{:S(2)}, u32[]{:S(2)}) collective-permute-start(f32[2,8,128]{2,1,0:T(8,128)S(1)} %pad_maximum_fusion.4), channel_id=1, source_target_pairs={{0,192},{64,128},{128,64},{192,0},{1,193},{65,129},{129,65},{193,1... | collective-permute-start | bytes 24584 | tf_op jit(solution)/shard_map/ppermute | solution.py:357
  23.9 1.2 %collective-permute-start.6 = (bf16[4,80,128]{2,1,0:T(8,128)(2,1)S(1)}, bf16[4,80,128]{2,1,0:T(8,128)(2,1)S(1)}, u32[]{:S(2)}, u32[]{:S(2)}) collective-permute-start(bf16[4,80,128]{2,1,0:T(8,128)(2,1)S(1)} %constant_dynamic-update-slice_fusion.refs_0_), channel_id=1, source_target_pairs={{0,2},{2,0},{4,6},{6,4},{1,3},{3,1},{5,7},{7,5},{8,10},{10,8},{12,... | collective-permute-start | bytes 245768 | tf_op jit(solution)/shard_map/ppermute | solution.py:361
  25.1 1.8 %collective-permute-start.4 = (bf16[4,80,128]{2,1,0:T(8,128)(2,1)S(1)}, bf16[4,80,128]{2,1,0:T(8,128)(2,1)S(1)}, u32[]{:S(2)}, u32[]{:S(2)}) collective-permute-start(bf16[4,80,128]{2,1,0:T(8,128)(2,1)S(1)} %constant_dynamic-update-slice_fusion.refs_0_), channel_id=1, source_target_pairs={{0,6},{2,4},{4,2},{6,0},{1,7},{3,5},{5,3},{7,1},{8,14},{10,12},{12... | collective-permute-start | bytes 245768 | tf_op jit(solution)/shard_map/ppermute | solution.py:360
  26.9 0.3 collective-permute-start.8
  27.2 0.0 collective-permute-done.2
  27.2 0.9 %collective-permute-start.9 = (bf16[4,80,128]{2,1,0:T(8,128)(2,1)S(1)}, bf16[4,80,128]{2,1,0:T(8,128)(2,1)S(1)}, u32[]{:S(2)}, u32[]{:S(2)}) collective-permute-start(bf16[4,80,128]{2,1,0:T(8,128)(2,1)S(1)} %collective-permute-done.7.refs_1_), channel_id=1, source_target_pairs={{0,6},{2,4},{4,2},{6,0},{1,7},{3,5},{5,3},{7,1},{8,14},{10,12},{12... | collective-permute-start | bytes 245768 | tf_op jit(solution)/shard_map/ppermute | solution.py:363
  28.1 0.7 pixel_columns.1.pix_ref
  28.8 0.0 collective-permute-done.10.refs_2_
  28.8 2.2 %unit_product.4.refs_5_ = f32[384,128]{1,0:T(8,128)S(1)} custom-call(f32[8,384,128]{2,1,0:T(8,128)S(1)} %pixel_columns.1.pix_ref, bf16[4,80,128]{2,1,0:T(8,128)(2,1)S(1)} %constant_dynamic-update-slice_fusion.refs_0_, bf16[4,80,128]{2,1,0:T(8,128)(2,1)S(1)} %collective-permute-done.7.refs_1_, bf16[8,80,128]{2,1,0:T(8,128)(2,1)S(1)} %collective-permute-done.10.refs_2_), custom_call_target="tpu_custom_call" | custom-call | flops 147456000 | bytes 524288 | tf_op jit(solution)/shard_map/unit_product/pallas_call | solution.py:256
  31.1 0.0 collective-permute-done.6.refs_0_
  31.1 0.0 collective-permute-done.8.refs_1_
  31.1 0.6 collective-permute-done.9.refs_3_
  31.7 0.0 collective-permute-done.4.refs_2_
  31.8 2.5 %collective-permute-start.12 = (bf16[16,80,128]{2,1,0:T(8,128)(2,1)S(1)}, bf16[16,80,128]{2,1,0:T(8,128)(2,1)S(1)}, u32[]{:S(2)}, u32[]{:S(2)}) collective-permute-start(bf16[16,80,128]{2,1,0:T(8,128)(2,1)S(1)} %pad_maximum_fusion), channel_id=1, source_target_pairs={{0,1},{1,0},{2,3},{3,2},{4,5},{5,4},{6,7},{7,6},{8,9},{9,8},{10,11... | collective-permute-start | bytes 983048 | tf_op jit(solution)/shard_map/ppermute | solution.py:372
  34.2 0.0 collective-permute-start.5
  34.2 1.5 %collective-permute-start.11 = (bf16[4,80,128]{2,1,0:T(8,128)(2,1)S(1)}, bf16[4,80,128]{2,1,0:T(8,128)(2,1)S(1)}, u32[]{:S(2)}, u32[]{:S(2)}) collective-permute-start(bf16[4,80,128]{2,1,0:T(8,128)(2,1)S(1)} %collective-permute-done.9.refs_3_), channel_id=1, source_target_pairs={{0,2},{2,0},{4,6},{6,4},{1,3},{3,1},{5,7},{7,5},{8,10},{10,8},{12,... | collective-permute-start | bytes 245768 | tf_op jit(solution)/shard_map/ppermute | solution.py:371
  35.7 0.0 collective-permute-done.12.refs_4_
  35.7 4.4 %unit_product.5.refs_2_ = f32[384,128]{1,0:T(8,128)S(1)} custom-call(f32[8,384,128]{2,1,0:T(8,128)S(1)} %pixel_columns.1.pix_ref, bf16[4,80,128]{2,1,0:T(8,128)(2,1)S(1)} %collective-permute-done.6.refs_0_, bf16[4,80,128]{2,1,0:T(8,128)(2,1)S(1)} %collective-permute-done.8.refs_1_, bf16[4,80,128]{2,1,0:T(8,128)(2,1)S(1)} %collective-permute-done.4.refs_2_, ...), custom_call_target="tpu_custom_call" | custom-call | flops 294912000 | bytes 524288 | tf_op jit(solution)/shard_map/unit_product/pallas_call | solution.py:256
  40.1 0.0 collective-permute-done.5
  40.1 0.0 collective-permute-done.11
  40.1 0.8 %collective-permute-start.13 = (bf16[8,80,128]{2,1,0:T(8,128)(2,1)S(1)}, bf16[8,80,128]{2,1,0:T(8,128)(2,1)S(1)}, u32[]{:S(2)}, u32[]{:S(2)}) collective-permute-start(bf16[8,80,128]{2,1,0:T(8,128)(2,1)S(1)} %constant_dynamic-update-slice_fusion.2.refs_0_), channel_id=1, source_target_pairs={{0,1},{1,0},{2,3},{3,2},{4,5},{5,4},{6,7},{7,6},{8,9},{9,8},{10,11... | collective-permute-start | bytes 491528 | tf_op jit(solution)/shard_map/ppermute | solution.py:381
  40.9 1.0 %collective-permute-done.13.refs_1_ = bf16[8,80,128]{2,1,0:T(8,128)(2,1)S(1)} collective-permute-done((bf16[8,80,128]{2,1,0:T(8,128)(2,1)S(1)}, bf16[8,80,128]{2,1,0:T(8,128)(2,1)S(1)}, u32[]{:S(2)}, u32[]{:S(2)}) %collective-permute-start.13) | collective-permute-done | bytes 163872 | tf_op jit(solution)/shard_map/ppermute | solution.py:381
  42.0 1.2 %unit_product.7 = f32[192,128]{1,0:T(8,128)S(1)} custom-call(f32[8,384,128]{2,1,0:T(8,128)S(1)} %pixel_columns.1.pix_ref, bf16[8,80,128]{2,1,0:T(8,128)(2,1)S(1)} %constant_dynamic-update-slice_fusion.2.refs_0_, bf16[8,80,128]{2,1,0:T(8,128)(2,1)S(1)} %collective-permute-done.13.refs_1_, f32[384,128]{1,0:T(8,128)S(1)} %unit_product.5.refs_2_), custom_call_target="tpu_custom_call" | custom-call | flops 73728000 | bytes 524288 | tf_op jit(solution)/shard_map/unit_product/pallas_call | solution.py:256
  43.2 0.5 collective-permute-start.16
  43.7 1.2 %unit_product.6 = f32[192,128]{1,0:T(8,128)S(1)} custom-call(f32[8,384,128]{2,1,0:T(8,128)S(1)} %pixel_columns.1.pix_ref, bf16[8,80,128]{2,1,0:T(8,128)(2,1)S(1)} %constant_dynamic-update-slice_fusion.2.refs_0_, bf16[8,80,128]{2,1,0:T(8,128)(2,1)S(1)} %collective-permute-done.13.refs_1_, f32[384,128]{1,0:T(8,128)S(1)} %unit_product.5.refs_2_), custom_call_target="tpu_custom_call" | custom-call | flops 73728000 | bytes 524288 | tf_op jit(solution)/shard_map/unit_product/pallas_call | solution.py:256
  44.9 0.7 collective-permute-start.14
  45.6 1.7 %collective-permute-done.16.got_ref = f32[4,48,128]{2,1,0:T(8,128)S(1)} collective-permute-done((f32[4,48,128]{2,1,0:T(8,128)S(1)}, f32[4,48,128]{2,1,0:T(8,128)S(1)}, u32[]{:S(2)}, u32[]{:S(2)}) %collective-permute-start.16) | collective-permute-done | bytes 98336 | tf_op jit(solution)/shard_map/ppermute | solution.py:388
  47.3 0.9 %collective-permute-start.17 = (f32[4,48,128]{2,1,0:T(8,128)S(1)}, f32[4,48,128]{2,1,0:T(8,128)S(1)}, u32[]{:S(2)}, u32[]{:S(2)}) collective-permute-start(f32[4,48,128]{2,1,0:T(8,128)S(1)} %exchange_add.3.high_ref), channel_id=1, source_target_pairs={{0,192},{64,128},{128,64},{192,0},{1,193},{65,129},{129,65},{193,1... | collective-permute-start | bytes 294920 | tf_op jit(solution)/shard_map/ppermute | solution.py:390
  48.1 1.7 %collective-permute-done.14.got_ref = f32[4,48,128]{2,1,0:T(8,128)S(1)} collective-permute-done((f32[4,48,128]{2,1,0:T(8,128)S(1)}, f32[4,48,128]{2,1,0:T(8,128)S(1)}, u32[]{:S(2)}, u32[]{:S(2)}) %collective-permute-start.14) | collective-permute-done | bytes 98336 | tf_op jit(solution)/shard_map/ppermute | solution.py:387
  49.9 0.1 collective-permute-start.15
  50.0 2.1 %collective-permute-done.17.high_got_ref = f32[4,48,128]{2,1,0:T(8,128)S(1)} collective-permute-done((f32[4,48,128]{2,1,0:T(8,128)S(1)}, f32[4,48,128]{2,1,0:T(8,128)S(1)}, u32[]{:S(2)}, u32[]{:S(2)}) %collective-permute-start.17) | collective-permute-done | bytes 98336 | tf_op jit(solution)/shard_map/ppermute | solution.py:390
  52.1 1.7 %collective-permute-done.15.low_got_ref = f32[4,48,128]{2,1,0:T(8,128)S(1)} collective-permute-done((f32[4,48,128]{2,1,0:T(8,128)S(1)}, f32[4,48,128]{2,1,0:T(8,128)S(1)}, u32[]{:S(2)}, u32[]{:S(2)}) %collective-permute-start.15) | collective-permute-done | bytes 98336 | tf_op jit(solution)/shard_map/ppermute | solution.py:390
  53.7 0.7 residual_part.1
  54.4 2.7 %collective-permute-start.18 = (f32[1,128]{1,0:T(1,128)S(1)}, f32[1,128]{1,0:T(1,128)S(1)}, u32[]{:S(2)}, u32[]{:S(2)}) collective-permute-start(f32[1,128]{1,0:T(1,128)S(1)} %get-tuple-element.27), channel_id=1, source_target_pairs={{0,1},{1,0},{2,3},{3,2},{4,5},{5,4},{6,7},{7,6},{8,9},{9,8},{10,11... | collective-permute-start | bytes 1544 | tf_op jit(solution)/shard_map/ppermute | solution.py:392
  57.0 0.8 %collective-permute-done.18 = f32[1,128]{1,0:T(1,128)S(1)} collective-permute-done((f32[1,128]{1,0:T(1,128)S(1)}, f32[1,128]{1,0:T(1,128)S(1)}, u32[]{:S(2)}, u32[]{:S(2)}) %collective-permute-start.18) | collective-permute-done | bytes 544 | tf_op jit(solution)/shard_map/ppermute | solution.py:392
  57.9 0.5 collective-permute-start.19
  58.4 3.8 %collective-permute-start.20 = (f32[1,128]{1,0:T(1,128)S(1)}, f32[1,128]{1,0:T(1,128)S(1)}, u32[]{:S(2)}, u32[]{:S(2)}) collective-permute-start(f32[1,128]{1,0:T(1,128)S(1)} %add.18), channel_id=1, source_target_pairs={{7,1},{5,3},{3,5},{1,7},{15,9},{13,11},{11,13},{9,15},{23,17},{21,... | collective-permute-start | bytes 1544 | tf_op jit(solution)/shard_map/ppermute | solution.py:322
  62.2 0.0 collective-permute-done.19
  62.2 1.7 %collective-permute-done.20 = f32[1,128]{1,0:T(1,128)S(1)} collective-permute-done((f32[1,128]{1,0:T(1,128)S(1)}, f32[1,128]{1,0:T(1,128)S(1)}, u32[]{:S(2)}, u32[]{:S(2)}) %collective-permute-start.20) | collective-permute-done | bytes 544 | tf_op jit(solution)/shard_map/ppermute | solution.py:322
  63.9 0.0 collective-permute-start.21
  63.9 1.2 %collective-permute-done.21 = f32[1,128]{1,0:T(1,128)S(1)} collective-permute-done((f32[1,128]{1,0:T(1,128)S(1)}, f32[1,128]{1,0:T(1,128)S(1)}, u32[]{:S(2)}, u32[]{:S(2)}) %collective-permute-start.21) | collective-permute-done | bytes 544 | tf_op jit(solution)/shard_map/ppermute | solution.py:324
  65.1 2.2 %collective-permute-start.22 = (f32[1,128]{1,0:T(1,128)S(1)}, f32[1,128]{1,0:T(1,128)S(1)}, u32[]{:S(2)}, u32[]{:S(2)}) collective-permute-start(f32[1,128]{1,0:T(1,128)S(1)} %add.20), channel_id=1, source_target_pairs={{8,0},{0,8},{24,16},{16,24},{40,32},{32,40},{56,48},{48,56},{17,1}... | collective-permute-start | bytes 1544 | tf_op jit(solution)/shard_map/ppermute | solution.py:321
  67.2 3.4 %collective-permute-start.23 = (f32[1,128]{1,0:T(1,128)S(1)}, f32[1,128]{1,0:T(1,128)S(1)}, u32[]{:S(2)}, u32[]{:S(2)}) collective-permute-start(f32[1,128]{1,0:T(1,128)S(1)} %add.20), channel_id=1, source_target_pairs={{25,1},{17,9},{9,17},{1,25},{57,33},{49,41},{41,49},{33,57},{27,3}... | collective-permute-start | bytes 1544 | tf_op jit(solution)/shard_map/ppermute | solution.py:322
  70.7 0.0 collective-permute-done.22
  70.7 2.6 %collective-permute-done.23 = f32[1,128]{1,0:T(1,128)S(1)} collective-permute-done((f32[1,128]{1,0:T(1,128)S(1)}, f32[1,128]{1,0:T(1,128)S(1)}, u32[]{:S(2)}, u32[]{:S(2)}) %collective-permute-start.23) | collective-permute-done | bytes 544 | tf_op jit(solution)/shard_map/ppermute | solution.py:322
  73.3 0.0 collective-permute-start.24
  73.3 1.2 %collective-permute-done.24 = f32[1,128]{1,0:T(1,128)S(1)} collective-permute-done((f32[1,128]{1,0:T(1,128)S(1)}, f32[1,128]{1,0:T(1,128)S(1)}, u32[]{:S(2)}, u32[]{:S(2)}) %collective-permute-start.24) | collective-permute-done | bytes 544 | tf_op jit(solution)/shard_map/ppermute | solution.py:324
  74.5 3.8 %collective-permute-start.25 = (f32[1,128]{1,0:T(1,128)S(1)}, f32[1,128]{1,0:T(1,128)S(1)}, u32[]{:S(2)}, u32[]{:S(2)}) collective-permute-start(f32[1,128]{1,0:T(1,128)S(1)} %add.22), channel_id=1, source_target_pairs={{0,56},{8,48},{16,40},{24,32},{32,24},{40,16},{48,8},{56,0},{1,57}... | collective-permute-start | bytes 1544 | tf_op jit(solution)/shard_map/ppermute | solution.py:395
  78.3 1.0 %collective-permute-done.25 = f32[1,128]{1,0:T(1,128)S(1)} collective-permute-done((f32[1,128]{1,0:T(1,128)S(1)}, f32[1,128]{1,0:T(1,128)S(1)}, u32[]{:S(2)}, u32[]{:S(2)}) %collective-permute-start.25) | collective-permute-done | bytes 544 | tf_op jit(solution)/shard_map/ppermute | solution.py:395
  79.2 0.5 multiply_bitcast_fusion
  (16 shorter events, 0.2 us)
Async XLA Ops:
  1.7 5.1 %collective-permute-start.1 = (f32[1,8,128]{2,1,0:T(8,128)S(1)}, f32[1,8,128]{2,1,0:T(8,128)S(1)}, u32[]{:S(2)}, u32[]{:S(2)}) collective-permute-start(f32[1,8,128]{2,1,0:T(8,128)S(1)} %get-tuple-element.16), channel_id=1, source_target_pairs={{0,64},{64,0},{128,192},{192,128},{1,65},{65,1},{129,193},{193,129... | collective-permute-start | bytes 12296 | tf_op jit(solution)/shard_map/ppermute | solution.py:355
  3.8 4.2 %collective-permute-start = (bf16[1,80,128]{2,1,0:T(8,128)(2,1)S(1)}, bf16[1,80,128]{2,1,0:T(8,128)(2,1)S(1)}, u32[]{:S(2)}, u32[]{:S(2)}) collective-permute-start(bf16[1,80,128]{2,1,0:T(8,128)(2,1)S(1)} %bitcast.16), channel_id=1, source_target_pairs={{0,16},{8,24},{16,0},{24,8},{32,48},{40,56},{48,32},{56,40},{1,17}... | collective-permute-start | bytes 61448 | tf_op jit(solution)/shard_map/ppermute | solution.py:355
  8.0 6.3 %collective-permute-start.3 = (bf16[2,80,128]{2,1,0:T(8,128)(2,1)S(1)}, bf16[2,80,128]{2,1,0:T(8,128)(2,1)S(1)}, u32[]{:S(2)}, u32[]{:S(2)}) collective-permute-start(bf16[2,80,128]{2,1,0:T(8,128)(2,1)S(1)} %pad_maximum_fusion.2), channel_id=1, source_target_pairs={{0,56},{8,48},{16,40},{24,32},{32,24},{40,16},{48,8},{56,0},{1,57}... | collective-permute-start | bytes 122888 | tf_op jit(solution)/shard_map/ppermute | solution.py:358
  14.3 3.5 %collective-permute-start.7 = (bf16[4,80,128]{2,1,0:T(8,128)(2,1)S(1)}, bf16[4,80,128]{2,1,0:T(8,128)(2,1)S(1)}, u32[]{:S(2)}, u32[]{:S(2)}) collective-permute-start(bf16[4,80,128]{2,1,0:T(8,128)(2,1)S(1)} %constant_dynamic-update-slice_fusion.refs_0_), channel_id=1, source_target_pairs={{0,8},{8,0},{16,24},{24,16},{32,40},{40,32},{48,56},{56,48},{1,9},... | collective-permute-start | bytes 245768 | tf_op jit(solution)/shard_map/ppermute | solution.py:359
  17.9 10.9 %collective-permute-start.10 = (bf16[8,80,128]{2,1,0:T(8,128)(2,1)S(1)}, bf16[8,80,128]{2,1,0:T(8,128)(2,1)S(1)}, u32[]{:S(2)}, u32[]{:S(2)}) collective-permute-start(bf16[8,80,128]{2,1,0:T(8,128)(2,1)S(1)} %pad_maximum_fusion.1), channel_id=1, source_target_pairs={{0,1},{1,0},{2,3},{3,2},{4,5},{5,4},{6,7},{7,6},{8,9},{9,8},{10,11... | collective-permute-start | bytes 491528 | tf_op jit(solution)/shard_map/ppermute | solution.py:365
  22.0 5.2 %collective-permute-start.2 = (f32[2,8,128]{2,1,0:T(8,128)S(1)}, f32[2,8,128]{2,1,0:T(8,128)S(1)}, u32[]{:S(2)}, u32[]{:S(2)}) collective-permute-start(f32[2,8,128]{2,1,0:T(8,128)S(1)} %pad_maximum_fusion.4), channel_id=1, source_target_pairs={{0,192},{64,128},{128,64},{192,0},{1,193},{65,129},{129,65},{193,1... | collective-permute-start | bytes 24584 | tf_op jit(solution)/shard_map/ppermute | solution.py:357
  23.9 7.2 %collective-permute-start.6 = (bf16[4,80,128]{2,1,0:T(8,128)(2,1)S(1)}, bf16[4,80,128]{2,1,0:T(8,128)(2,1)S(1)}, u32[]{:S(2)}, u32[]{:S(2)}) collective-permute-start(bf16[4,80,128]{2,1,0:T(8,128)(2,1)S(1)} %constant_dynamic-update-slice_fusion.refs_0_), channel_id=1, source_target_pairs={{0,2},{2,0},{4,6},{6,4},{1,3},{3,1},{5,7},{7,5},{8,10},{10,8},{12,... | collective-permute-start | bytes 245768 | tf_op jit(solution)/shard_map/ppermute | solution.py:361
  25.1 6.6 %collective-permute-start.4 = (bf16[4,80,128]{2,1,0:T(8,128)(2,1)S(1)}, bf16[4,80,128]{2,1,0:T(8,128)(2,1)S(1)}, u32[]{:S(2)}, u32[]{:S(2)}) collective-permute-start(bf16[4,80,128]{2,1,0:T(8,128)(2,1)S(1)} %constant_dynamic-update-slice_fusion.refs_0_), channel_id=1, source_target_pairs={{0,6},{2,4},{4,2},{6,0},{1,7},{3,5},{5,3},{7,1},{8,14},{10,12},{12... | collective-permute-start | bytes 245768 | tf_op jit(solution)/shard_map/ppermute | solution.py:360
  26.9 4.2 %collective-permute-start.8 = (bf16[4,80,128]{2,1,0:T(8,128)(2,1)S(1)}, bf16[4,80,128]{2,1,0:T(8,128)(2,1)S(1)}, u32[]{:S(2)}, u32[]{:S(2)}) collective-permute-start(bf16[4,80,128]{2,1,0:T(8,128)(2,1)S(1)} %collective-permute-done.7.refs_1_), channel_id=1, source_target_pairs={{0,2},{2,0},{4,6},{6,4},{1,3},{3,1},{5,7},{7,5},{8,10},{10,8},{12,... | collective-permute-start | bytes 245768 | tf_op jit(solution)/shard_map/ppermute | solution.py:364
  27.2 4.5 %collective-permute-start.9 = (bf16[4,80,128]{2,1,0:T(8,128)(2,1)S(1)}, bf16[4,80,128]{2,1,0:T(8,128)(2,1)S(1)}, u32[]{:S(2)}, u32[]{:S(2)}) collective-permute-start(bf16[4,80,128]{2,1,0:T(8,128)(2,1)S(1)} %collective-permute-done.7.refs_1_), channel_id=1, source_target_pairs={{0,6},{2,4},{4,2},{6,0},{1,7},{3,5},{5,3},{7,1},{8,14},{10,12},{12... | collective-permute-start | bytes 245768 | tf_op jit(solution)/shard_map/ppermute | solution.py:363
  31.8 3.9 %collective-permute-start.12 = (bf16[16,80,128]{2,1,0:T(8,128)(2,1)S(1)}, bf16[16,80,128]{2,1,0:T(8,128)(2,1)S(1)}, u32[]{:S(2)}, u32[]{:S(2)}) collective-permute-start(bf16[16,80,128]{2,1,0:T(8,128)(2,1)S(1)} %pad_maximum_fusion), channel_id=1, source_target_pairs={{0,1},{1,0},{2,3},{3,2},{4,5},{5,4},{6,7},{7,6},{8,9},{9,8},{10,11... | collective-permute-start | bytes 983048 | tf_op jit(solution)/shard_map/ppermute | solution.py:372
  34.2 5.9 %collective-permute-start.5 = (bf16[4,80,128]{2,1,0:T(8,128)(2,1)S(1)}, bf16[4,80,128]{2,1,0:T(8,128)(2,1)S(1)}, u32[]{:S(2)}, u32[]{:S(2)}) collective-permute-start(bf16[4,80,128]{2,1,0:T(8,128)(2,1)S(1)} %collective-permute-done.4.refs_2_), channel_id=1, source_target_pairs={{0,2},{2,0},{4,6},{6,4},{1,3},{3,1},{5,7},{7,5},{8,10},{10,8},{12,... | collective-permute-start | bytes 245768 | tf_op jit(solution)/shard_map/ppermute | solution.py:366
  34.2 5.9 %collective-permute-start.11 = (bf16[4,80,128]{2,1,0:T(8,128)(2,1)S(1)}, bf16[4,80,128]{2,1,0:T(8,128)(2,1)S(1)}, u32[]{:S(2)}, u32[]{:S(2)}) collective-permute-start(bf16[4,80,128]{2,1,0:T(8,128)(2,1)S(1)} %collective-permute-done.9.refs_3_), channel_id=1, source_target_pairs={{0,2},{2,0},{4,6},{6,4},{1,3},{3,1},{5,7},{7,5},{8,10},{10,8},{12,... | collective-permute-start | bytes 245768 | tf_op jit(solution)/shard_map/ppermute | solution.py:371
  40.1 1.8 %collective-permute-start.13 = (bf16[8,80,128]{2,1,0:T(8,128)(2,1)S(1)}, bf16[8,80,128]{2,1,0:T(8,128)(2,1)S(1)}, u32[]{:S(2)}, u32[]{:S(2)}) collective-permute-start(bf16[8,80,128]{2,1,0:T(8,128)(2,1)S(1)} %constant_dynamic-update-slice_fusion.2.refs_0_), channel_id=1, source_target_pairs={{0,1},{1,0},{2,3},{3,2},{4,5},{5,4},{6,7},{7,6},{8,9},{9,8},{10,11... | collective-permute-start | bytes 491528 | tf_op jit(solution)/shard_map/ppermute | solution.py:381
  43.2 4.1 %collective-permute-start.16 = (f32[4,48,128]{2,1,0:T(8,128)S(1)}, f32[4,48,128]{2,1,0:T(8,128)S(1)}, u32[]{:S(2)}, u32[]{:S(2)}) collective-permute-start(f32[4,48,128]{2,1,0:T(8,128)S(1)} %bitcast.14), channel_id=1, source_target_pairs={{0,64},{64,0},{128,192},{192,128},{1,65},{65,1},{129,193},{193,129... | collective-permute-start | bytes 294920 | tf_op jit(solution)/shard_map/ppermute | solution.py:388
  44.9 4.9 %collective-permute-start.14 = (f32[4,48,128]{2,1,0:T(8,128)S(1)}, f32[4,48,128]{2,1,0:T(8,128)S(1)}, u32[]{:S(2)}, u32[]{:S(2)}) collective-permute-start(f32[4,48,128]{2,1,0:T(8,128)S(1)} %bitcast.12), channel_id=1, source_target_pairs={{0,192},{64,128},{128,64},{192,0},{1,193},{65,129},{129,65},{193,1... | collective-permute-start | bytes 294920 | tf_op jit(solution)/shard_map/ppermute | solution.py:387
  47.3 4.8 %collective-permute-start.17 = (f32[4,48,128]{2,1,0:T(8,128)S(1)}, f32[4,48,128]{2,1,0:T(8,128)S(1)}, u32[]{:S(2)}, u32[]{:S(2)}) collective-permute-start(f32[4,48,128]{2,1,0:T(8,128)S(1)} %exchange_add.3.high_ref), channel_id=1, source_target_pairs={{0,192},{64,128},{128,64},{192,0},{1,193},{65,129},{129,65},{193,1... | collective-permute-start | bytes 294920 | tf_op jit(solution)/shard_map/ppermute | solution.py:390
  49.9 3.8 %collective-permute-start.15 = (f32[4,48,128]{2,1,0:T(8,128)S(1)}, f32[4,48,128]{2,1,0:T(8,128)S(1)}, u32[]{:S(2)}, u32[]{:S(2)}) collective-permute-start(f32[4,48,128]{2,1,0:T(8,128)S(1)} %exchange_add.2.low_ref), channel_id=1, source_target_pairs={{0,64},{64,0},{128,192},{192,128},{1,65},{65,1},{129,193},{193,129... | collective-permute-start | bytes 294920 | tf_op jit(solution)/shard_map/ppermute | solution.py:390
  54.4 3.5 %collective-permute-start.18 = (f32[1,128]{1,0:T(1,128)S(1)}, f32[1,128]{1,0:T(1,128)S(1)}, u32[]{:S(2)}, u32[]{:S(2)}) collective-permute-start(f32[1,128]{1,0:T(1,128)S(1)} %get-tuple-element.27), channel_id=1, source_target_pairs={{0,1},{1,0},{2,3},{3,2},{4,5},{5,4},{6,7},{7,6},{8,9},{9,8},{10,11... | collective-permute-start | bytes 1544 | tf_op jit(solution)/shard_map/ppermute | solution.py:392
  57.9 4.3 %collective-permute-start.19 = (f32[1,128]{1,0:T(1,128)S(1)}, f32[1,128]{1,0:T(1,128)S(1)}, u32[]{:S(2)}, u32[]{:S(2)}) collective-permute-start(f32[1,128]{1,0:T(1,128)S(1)} %add.18), channel_id=1, source_target_pairs={{2,0},{0,2},{6,4},{4,6},{5,1},{7,3},{1,5},{3,7},{10,8},{8,10},{14,... | collective-permute-start | bytes 1544 | tf_op jit(solution)/shard_map/ppermute | solution.py:321
  58.4 5.5 %collective-permute-start.20 = (f32[1,128]{1,0:T(1,128)S(1)}, f32[1,128]{1,0:T(1,128)S(1)}, u32[]{:S(2)}, u32[]{:S(2)}) collective-permute-start(f32[1,128]{1,0:T(1,128)S(1)} %add.18), channel_id=1, source_target_pairs={{7,1},{5,3},{3,5},{1,7},{15,9},{13,11},{11,13},{9,15},{23,17},{21,... | collective-permute-start | bytes 1544 | tf_op jit(solution)/shard_map/ppermute | solution.py:322
  63.9 1.2 %collective-permute-start.21 = (f32[1,128]{1,0:T(1,128)S(1)}, f32[1,128]{1,0:T(1,128)S(1)}, u32[]{:S(2)}, u32[]{:S(2)}) collective-permute-start(f32[1,128]{1,0:T(1,128)S(1)} %fusion), channel_id=1, source_target_pairs={{0,1},{1,0},{2,3},{3,2},{4,5},{5,4},{6,7},{7,6},{8,9},{9,8},{10,11... | collective-permute-start | bytes 1544 | tf_op jit(solution)/shard_map/ppermute | solution.py:324
  65.1 5.6 %collective-permute-start.22 = (f32[1,128]{1,0:T(1,128)S(1)}, f32[1,128]{1,0:T(1,128)S(1)}, u32[]{:S(2)}, u32[]{:S(2)}) collective-permute-start(f32[1,128]{1,0:T(1,128)S(1)} %add.20), channel_id=1, source_target_pairs={{8,0},{0,8},{24,16},{16,24},{40,32},{32,40},{56,48},{48,56},{17,1}... | collective-permute-start | bytes 1544 | tf_op jit(solution)/shard_map/ppermute | solution.py:321
  67.2 6.1 %collective-permute-start.23 = (f32[1,128]{1,0:T(1,128)S(1)}, f32[1,128]{1,0:T(1,128)S(1)}, u32[]{:S(2)}, u32[]{:S(2)}) collective-permute-start(f32[1,128]{1,0:T(1,128)S(1)} %add.20), channel_id=1, source_target_pairs={{25,1},{17,9},{9,17},{1,25},{57,33},{49,41},{41,49},{33,57},{27,3}... | collective-permute-start | bytes 1544 | tf_op jit(solution)/shard_map/ppermute | solution.py:322
  73.3 1.2 %collective-permute-start.24 = (f32[1,128]{1,0:T(1,128)S(1)}, f32[1,128]{1,0:T(1,128)S(1)}, u32[]{:S(2)}, u32[]{:S(2)}) collective-permute-start(f32[1,128]{1,0:T(1,128)S(1)} %fusion.1), channel_id=1, source_target_pairs={{0,1},{1,0},{2,3},{3,2},{4,5},{5,4},{6,7},{7,6},{8,9},{9,8},{10,11... | collective-permute-start | bytes 1544 | tf_op jit(solution)/shard_map/ppermute | solution.py:324
  74.5 4.7 %collective-permute-start.25 = (f32[1,128]{1,0:T(1,128)S(1)}, f32[1,128]{1,0:T(1,128)S(1)}, u32[]{:S(2)}, u32[]{:S(2)}) collective-permute-start(f32[1,128]{1,0:T(1,128)S(1)} %add.22), channel_id=1, source_target_pairs={{0,56},{8,48},{16,40},{24,32},{32,24},{40,16},{48,8},{56,0},{1,57}... | collective-permute-start | bytes 1544 | tf_op jit(solution)/shard_map/ppermute | solution.py:395

commit v4 on v3

--- a/solution.py
+++ b/solution.py
@@ -56,7 +56,6 @@
 
 
 def prepare_kernel(
-    core_ref,
     strike_ref,
     dip_ref,
     pos_ref,
@@ -96,60 +95,64 @@
     pieces = jnp.concatenate([pieces, jnp.zeros((24, LANES - count), jnp.float32)], axis=1)
     pieces = jnp.concatenate([pieces, jnp.zeros((LANES - 24, LANES), jnp.float32)], axis=0)
     turned_ref[...] = jnp.transpose(pieces)
-    first = core_ref[0] * PIECE
-    tile = jnp.zeros((SUB, LANES), jnp.float32)
-    for group in range(GROUPS):
-        start = pl.multiple_of(first + SUB * group, SUB)
-        part = turned_ref[pl.ds(start, SUB), :]
-        tile = tile + (part if group == 0 else pltpu.roll(part, FRAME_STRIDE * group, 1))
-        for k in range(3):
-            row = (k * GROUPS + group) * SUB
-            out_ref[row : row + SUB, :] = slip_ref[k, pl.ds(start, SUB), :]
-    out_ref[SLIP_ROWS:ROWS, :] = tile.astype(jnp.bfloat16)
+    for half in range(2):
+        tile = jnp.zeros((SUB, LANES), jnp.float32)
+        for group in range(GROUPS):
+            start = half * PIECE + SUB * group
+            part = turned_ref[start : start + SUB, :]
+            tile = tile + (part if group == 0 else pltpu.roll(part, FRAME_STRIDE * group, 1))
+            for k in range(3):
+                row = (k * GROUPS + group) * SUB
+                out_ref[half, row : row + SUB, :] = slip_ref[k, start : start + SUB, :]
+        out_ref[half, SLIP_ROWS:ROWS, :] = tile.astype(jnp.bfloat16)
     site = jnp.concatenate(
         [pixel_ref[...], view_ref[...], observed_ref[...], noise_ref[...], mask_ref[...].astype(jnp.float32)], axis=0
     )
     sites_ref[0] = jnp.concatenate([site, jnp.zeros((SUB, LANES - site.shape[1]), jnp.float32)], axis=1)
 
 
-def prepare(core, tables, patches, pixels):
+def prepare(tables, patches, pixels):
     smem = pl.BlockSpec(memory_space=pltpu.SMEM)
     vectors = list(patches) + list(pixels)
     return pl.pallas_call(
         prepare_kernel,
-        out_shape=(vmem_array((ROWS, LANES), jnp.bfloat16), vmem_array((1, SUB, LANES), jnp.float32)),
-        in_specs=[smem] * 3 + [VMEM_SPEC] * len(vectors),
+        out_shape=(vmem_array((2, ROWS, LANES), jnp.bfloat16), vmem_array((1, SUB, LANES), jnp.float32)),
+        in_specs=[smem] * 2 + [VMEM_SPEC] * len(vectors),
         out_specs=(VMEM_SPEC, VMEM_SPEC),
         scratch_shapes=[pltpu.VMEM((LANES, LANES), jnp.float32)],
         compiler_params=LIMITS,
         name="prepare",
-    )(core, *[in_hbm(array) for array in list(tables) + vectors])
-
-
-def columns_kernel(width, sites_ref, pix_ref):
-    blocks = sites_ref.shape[0]
+    )(*[in_hbm(array) for array in list(tables) + vectors])
+
+
+def columns_kernel(width, first, sites_ref, *refs):
+    pix_ref = refs[-1]
     half = width // 2
-    for block in range(blocks):
+    for block in range(sites_ref.shape[0]):
         columns = jnp.transpose(sites_ref[block])[:width]
-        for f in range(SUB):
+        for f in range(7):
             column = columns[:, f : f + 1]
             if 2 <= f < 5:
                 column = column * VIEW_SCALE
+            if f == 6:
+                column = columns[:, 7:8] / column
             column = jnp.broadcast_to(column, (width, LANES))
             for part in range(2):
-                row = (part * blocks + block) * half
+                row = (part * 4 + first + block) * half
                 pix_ref[f, row : row + half, :] = column[part * half : (part + 1) * half]
 
 
-def pixel_columns(sites, width):
+def pixel_columns(sites, width, first, before=None):
+    arrays = [sites] if before is None else [sites, before]
     return pl.pallas_call(
-        functools.partial(columns_kernel, width),
-        out_shape=vmem_array((SUB, sites.shape[0] * width, LANES), jnp.float32),
-        in_specs=[VMEM_SPEC],
+        functools.partial(columns_kernel, width, first),
+        out_shape=vmem_array((7, 4 * width, LANES), jnp.float32),
+        in_specs=[VMEM_SPEC] * len(arrays),
         out_specs=VMEM_SPEC,
+        input_output_aliases={} if before is None else {1: 0},
         compiler_params=LIMITS,
         name="pixel_columns",
-    )(in_vmem(sites))
+    )(*[in_vmem(array) for array in arrays])
 
 
 def unit_kernel(units, count, has_acc, first_row, pix_ref, *refs):
@@ -158,7 +161,7 @@
     out_ref, green_ref = refs[-2:]
     pixels = out_ref.shape[0]
     step = 16
-    span = 96 if pixels % 96 == 0 else pixels
+    span = 192
 
     def gathered(unit, row, rows):
         return jnp.concatenate(
@@ -276,7 +279,7 @@
             value = mine[block] + got[order[block]]
             row = (part * 4 + block) * half
             here = slice(row, row + half)
-            res = pix_ref[7, here, :] * (value - pix_ref[5, here, :]) / pix_ref[6, here, :]
+            res = (value - pix_ref[5, here, :]) * pix_ref[6, here, :]
             if block == 0:
                 res_ref[part * half : (part + 1) * half, :] = res
             total = total + jnp.sum(res * res, axis=0, keepdims=True)
@@ -312,16 +315,6 @@
         compiler_params=LIMITS,
         name="exchange_add",
     )(in_vmem(mine), in_vmem(got))
-
-
-def quad_sum(value, axis, core):
-    count = lax.axis_size(axis)
-    low = [(2 * (i ^ 1), 2 * i) for i in range(count)]
-    high = [(2 * (i ^ 2) + 1, 2 * i + 1) for i in range(count)]
-    first = lax.ppermute(value, (axis, "pix"), low + high)
-    second = lax.ppermute(value, (axis, "pix"), [(2 * (i ^ 3) + 1, 2 * i + 1) for i in range(count)])
-    half = first + jnp.where(core == 0, value, second)
-    return half + lax.ppermute(half, "pix", xor_pairs(2, 1))
 
 
 def per_device(
@@ -341,7 +334,6 @@
     near_pairs, far_pairs, swap = xor_pairs(4, 1), xor_pairs(4, 3), xor_pairs(2, 1)
     core = lax.axis_index("pix").astype(jnp.int32)
     piece, sites = prepare(
-        core[None],
         (seg_strike, seg_dip),
         (patch_pos, patch_depth[None], segment_ids[None], jnp.transpose(slip_models, (1, 0, 2))),
         (pixel_pos, pixel_view, observed[None], noise_scale[None], valid_mask[None]),
@@ -350,16 +342,19 @@
     def stack(*values):
         return jnp.concatenate(values, axis=0)
 
-    piece = piece[None]
-    two, sites = lax.optimization_barrier(
-        (stack(piece, lax.ppermute(piece, "z", xor_pairs(8, 2))), stack(sites, lax.ppermute(sites, "y", near_pairs)))
-    )
-    sites_far = lax.ppermute(sites, "y", far_pairs)
-    four = stack(two, lax.ppermute(two, "z", mirror_pairs(8)))
+    meets = [(2 * (i ^ 2), 2 * i) for i in range(8)] + [(2 * (i ^ 5) + 1, 2 * i + 1) for i in range(8)]
+    first = lax.ppermute(piece, ("z", "pix"), meets)
+    meets = [(2 * (i ^ 1), 2 * i) for i in range(8)] + [(2 * (i ^ 6) + 1, 2 * i + 1) for i in range(8)]
+    second = lax.ppermute(piece, ("z", "pix"), meets)
+    sites_near = lax.ppermute(sites, "y", near_pairs)
+    four = jnp.where(core == 0, stack(piece, first), stack(first, second))
+    four, sites = lax.optimization_barrier((four, stack(sites, sites_near)))
     four_got = lax.ppermute(four, "z", xor_pairs(8, 1))
     far_a = lax.ppermute(four, "x", far_pairs)
     near_a = lax.ppermute(four, "x", near_pairs)
-    pix = pixel_columns(stack(sites, sites_far), own_pixels)
+    sites_far = lax.ppermute(sites, "y", far_pairs)
+    pix = pixel_columns(sites, own_pixels, 0)
+    pix = pixel_columns(sites_far, own_pixels, 2, pix)
     far_b = lax.ppermute(four_got, "x", far_pairs)
     near_b = lax.ppermute(four_got, "x", near_pairs)
     own_other = lax.ppermute(stack(four, four_got), "pix", swap)
@@ -371,14 +366,15 @@
     across_b = lax.ppermute(far_b, "x", near_pairs)
     others = lax.ppermute(stack(near_a, near_b, far_a, far_b), "pix", swap)
     acc = unit_product(
-        pix,
-        (near_a, near_b, far_a, far_b, others),
-        (((0, 0, part), (1, 0, part), (4, 0, count)), ((2, 0, part), (3, 0, part), (4, count, count))),
-        acc,
+        pix, (near_a, near_b, others), (((0, 0, part), (1, 0, part), (2, 0, count)),), acc
     )
     across_a, across_b, acc = lax.optimization_barrier((across_a, across_b, acc))
     across = stack(across_a, across_b)
     across_other = lax.ppermute(across, "pix", swap)
+    acc = unit_product(
+        pix, (far_a, far_b, others), (((0, 0, part), (1, 0, part), (2, count, count)),), acc
+    )
+    across_other, acc = lax.optimization_barrier((across_other, acc))
     last = (((0, 0, count), (1, 0, count)),)
     rows = 2 * own_pixels
     shape = (4, own_pixels // 2, LANES)
@@ -390,9 +386,17 @@
         pix, low, lax.ppermute(low, "y", near_pairs), high, lax.ppermute(high, "y", far_pairs)
     )
     total = own_sum + lax.ppermute(own_sum, "pix", swap)
-    total = quad_sum(total, "x", core)
-    total = quad_sum(total, "z", core)
-    total = total + lax.ppermute(total, "z", mirror_pairs(8))
+    for axis, pairs in [
+        ("x", near_pairs),
+        ("x", far_pairs),
+        ("z", xor_pairs(8, 1)),
+        ("z", xor_pairs(8, 2)),
+        ("z", mirror_pairs(8)),
+    ]:
+        meets = [(2 * source + 1, 2 * target + 1) for source, target in pairs]
+        meets += [(2 * i, 2 * (i ^ 1)) for i, _ in pairs]
+        total = total + lax.ppermute(total, (axis, "pix"), meets)
+    total = jnp.where(core == 1, total, lax.ppermute(total, "pix", swap))
     pixels = own_pixels * lax.axis_size(PATCH) * lax.axis_size("pix")
     return (residual, total[0] / pixels)
 

time: 79.9 us -> 76.5 us (0.957)
  starting transfers between devices: 45.2 us -> 34.3 us
  waiting for transfers between devices: 21.6 us -> 29.7 us
    ppermute x10 -> x9, starting transfers between devices: 23.7 us -> 16.5 us  [the longest x1 6.46 us: per_device(): first = lax.ppermute(piece, ('z', 'pix'), meets)]
    ppermute x10 -> x9, waiting for transfers between devices: 10.2 us -> 16.2 us  [the longest x5 10.6 us: per_device(): total = total + lax.ppermute(total, (axis, 'pix'), meets)]
    ppermute x1, starting transfers between devices: 4.04 us -> 0.09 us  [per_device(): own_other = lax.ppermute(stack(four, four_got), 'pix', swap)]
    ppermute x1, waiting for transfers between devices: 1.72 us -> 3.58 us  [per_device(): low = exchange_add(low, lax.ppermute(low, 'y', far_pairs), FAR_ORDER)]
    ppermute x1, waiting for transfers between devices: 0.01 us -> 1.76 us  [per_device(): across_b = lax.ppermute(far_b, 'x', near_pairs)]
    ppermute x1, starting transfers between devices: 0.95 us -> 2.48 us  [per_device(): far_b = lax.ppermute(four_got, 'x', far_pairs)]
    ppermute x1, starting transfers between devices: 1.82 us -> 0.34 us  [per_device(): far_a = lax.ppermute(four, 'x', far_pairs)]
    ppermute x1, waiting for transfers between devices: 1.66 us -> 0.35 us  [per_device(): high = exchange_add(high, lax.ppermute(high, 'y', near_pairs), NEAR_ORDER)]
  transfers between devices with their start and end apart: 26 -> 25, of which waited for: 15 -> 17; matrix products, arithmetic and copies ran while one was open for 0% -> 0% of each run, Pallas kernels for 11% -> 11%
where the time goes in v4:
time: 76.5 us; the launch traced here: 76.3 us
  starting transfers between devices  34.3 us (45%)
  waiting for transfers between devices  29.7 us (39%)
  Pallas kernels  10.9 us (14%)
  between operations  0.78 us (1%)
    ppermute x5, waiting for transfers between devices, per_device(): total = total + lax.ppermute(total, (axis, 'pix'), meets)  10.6 us
    pallas_call x5, Pallas kernels, unit_product(): pl.pallas_call(functools.partial(unit_kernel, units, len(parts), acc is n...  8.35 us
    ppermute x1, starting transfers between devices, per_device(): first = lax.ppermute(piece, ('z', 'pix'), meets)  6.46 us
    ppermute x5, starting transfers between devices, per_device(): total = total + lax.ppermute(total, (axis, 'pix'), meets)  4.78 us
    ppermute x1, waiting for transfers between devices, per_device(): second = lax.ppermute(piece, ('z', 'pix'), meets)  3.6 us
    ppermute x1, waiting for transfers between devices, per_device(): low = exchange_add(low, lax.ppermute(low, 'y', far_pairs), FAR_ORDER)  3.58 us
    ppermute x1, starting transfers between devices, per_device(): total = jnp.where(core == 1, total, lax.ppermute(total, 'pix', swap))  2.77 us
    ppermute x1, starting transfers between devices, per_device(): others = lax.ppermute(stack(near_a, near_b, far_a, far_b), 'pix', swap)  2.66 us
  transfers between devices with their start and end apart: 25, of which 17 were waited for; matrix products, arithmetic and copies ran while one was open for 0% of the time, Pallas kernels for 11%

profile of v4, /device:TPU:1, one launch (start us, length us, event | category | flops | bytes accessed | tf_op | source)
XLA Modules:
  0.0 76.3 jit_solution(11743954294564350499)
XLA Ops:
  0.6 1.0 %prepare.1 = (bf16[2,80,128]{2,1,0:T(8,128)(2,1)S(1)}, f32[1,8,128]{2,1,0:T(8,128)S(1)}) custom-call(f32[16]{0:T(128)} %strike_ref.1, f32[16]{0:T(128)} %dip_ref.1, f32[2,48]{1,0:T(2,128)} %pos_ref.1, f32[1,48]{1,0:T(1,128)} %bitcast.15, s32[1,48]{1,0:T(1,128)} %bitcast.16, bf16[3,48,128]{2,1,0:T(8,128)(2,1)} %bitcast.14, f32[2,96]{1,0:T(2,128)} %pixel_ref.1, ...), custom_call_target="tpu_custom_call" | custom-call | tf_op jit(solution)/shard_map/prepare/pallas_call | solution.py:117
  1.6 2.2 %collective-permute-start.2 = (f32[1,8,128]{2,1,0:T(8,128)S(1)}, f32[1,8,128]{2,1,0:T(8,128)S(1)}, u32[]{:S(2)}, u32[]{:S(2)}) collective-permute-start(f32[1,8,128]{2,1,0:T(8,128)S(1)} %get-tuple-element.18), channel_id=1, source_target_pairs={{0,64},{64,0},{128,192},{192,128},{1,65},{65,1},{129,193},{193,129... | collective-permute-start | bytes 12296 | tf_op jit(solution)/shard_map/ppermute | solution.py:349
  3.8 6.5 %collective-permute-start = (bf16[2,80,128]{2,1,0:T(8,128)(2,1)S(1)}, bf16[2,80,128]{2,1,0:T(8,128)(2,1)S(1)}, u32[]{:S(2)}, u32[]{:S(2)}) collective-permute-start(bf16[2,80,128]{2,1,0:T(8,128)(2,1)S(1)} %get-tuple-element.17), channel_id=1, source_target_pairs={{16,0},{24,8},{0,16},{8,24},{48,32},{56,40},{32,48},{40,56},{41,1}... | collective-permute-start | bytes 122888 | tf_op jit(solution)/shard_map/ppermute | solution.py:346
  10.3 0.3 collective-permute-start.1
  10.5 0.0 collective-permute-done.2
  10.6 1.1 %collective-permute-done = bf16[2,80,128]{2,1,0:T(8,128)(2,1)S(1)} collective-permute-done((bf16[2,80,128]{2,1,0:T(8,128)(2,1)S(1)}, bf16[2,80,128]{2,1,0:T(8,128)(2,1)S(1)}, u32[]{:S(2)}, u32[]{:S(2)}) %collective-permute-start) | collective-permute-done | bytes 40992 | tf_op jit(solution)/shard_map/ppermute | solution.py:346
  11.7 3.6 %collective-permute-done.1 = bf16[2,80,128]{2,1,0:T(8,128)(2,1)S(1)} collective-permute-done((bf16[2,80,128]{2,1,0:T(8,128)(2,1)S(1)}, bf16[2,80,128]{2,1,0:T(8,128)(2,1)S(1)}, u32[]{:S(2)}, u32[]{:S(2)}) %collective-permute-start.1) | collective-permute-done | bytes 40992 | tf_op jit(solution)/shard_map/ppermute | solution.py:348
  15.3 0.8 %collective-permute-start.7 = (bf16[4,80,128]{2,1,0:T(8,128)(2,1)S(1)}, bf16[4,80,128]{2,1,0:T(8,128)(2,1)S(1)}, u32[]{:S(2)}, u32[]{:S(2)}) collective-permute-start(bf16[4,80,128]{2,1,0:T(8,128)(2,1)S(1)} %maximum_select_fusion.refs_0_), channel_id=1, source_target_pairs={{0,8},{8,0},{16,24},{24,16},{32,40},{40,32},{48,56},{56,48},{1,9},... | collective-permute-start | bytes 245768 | tf_op jit(solution)/shard_map/ppermute | solution.py:352
  16.1 2.6 %collective-permute-done.7.refs_1_ = bf16[4,80,128]{2,1,0:T(8,128)(2,1)S(1)} collective-permute-done((bf16[4,80,128]{2,1,0:T(8,128)(2,1)S(1)}, bf16[4,80,128]{2,1,0:T(8,128)(2,1)S(1)}, u32[]{:S(2)}, u32[]{:S(2)}) %collective-permute-start.7) | collective-permute-done | bytes 81952 | tf_op jit(solution)/shard_map/ppermute | solution.py:352
  18.7 0.1 collective-permute-start.10
  18.8 2.0 %collective-permute-start.3 = (f32[2,8,128]{2,1,0:T(8,128)S(1)}, f32[2,8,128]{2,1,0:T(8,128)S(1)}, u32[]{:S(2)}, u32[]{:S(2)}) collective-permute-start(f32[2,8,128]{2,1,0:T(8,128)S(1)} %pad_maximum_fusion.2.sites_ref), channel_id=1, source_target_pairs={{0,192},{64,128},{128,64},{192,0},{1,193},{65,129},{129,65},{193,1... | collective-permute-start | bytes 24584 | tf_op jit(solution)/shard_map/ppermute | solution.py:355
  20.8 1.2 %collective-permute-start.6 = (bf16[4,80,128]{2,1,0:T(8,128)(2,1)S(1)}, bf16[4,80,128]{2,1,0:T(8,128)(2,1)S(1)}, u32[]{:S(2)}, u32[]{:S(2)}) collective-permute-start(bf16[4,80,128]{2,1,0:T(8,128)(2,1)S(1)} %maximum_select_fusion.refs_0_), channel_id=1, source_target_pairs={{0,2},{2,0},{4,6},{6,4},{1,3},{3,1},{5,7},{7,5},{8,10},{10,8},{12,... | collective-permute-start | bytes 245768 | tf_op jit(solution)/shard_map/ppermute | solution.py:354
  22.0 0.3 collective-permute-start.8
  22.2 2.5 %collective-permute-start.9 = (bf16[4,80,128]{2,1,0:T(8,128)(2,1)S(1)}, bf16[4,80,128]{2,1,0:T(8,128)(2,1)S(1)}, u32[]{:S(2)}, u32[]{:S(2)}) collective-permute-start(bf16[4,80,128]{2,1,0:T(8,128)(2,1)S(1)} %collective-permute-done.7.refs_1_), channel_id=1, source_target_pairs={{0,6},{2,4},{4,2},{6,0},{1,7},{3,5},{5,3},{7,1},{8,14},{10,12},{12... | collective-permute-start | bytes 245768 | tf_op jit(solution)/shard_map/ppermute | solution.py:358
  24.7 0.0 collective-permute-done.3.sites_ref
  24.7 0.3 collective-permute-start.4
  25.1 0.5 pixel_columns.2.refs_0_
  25.5 0.5 pixel_columns.3.pix_ref
  26.0 0.0 collective-permute-done.10.refs_2_
  26.0 2.1 %unit_product.5.refs_3_ = f32[384,128]{1,0:T(8,128)S(1)} custom-call(f32[7,384,128]{2,1,0:T(8,128)S(1)} %pixel_columns.3.pix_ref, bf16[4,80,128]{2,1,0:T(8,128)(2,1)S(1)} %maximum_select_fusion.refs_0_, bf16[4,80,128]{2,1,0:T(8,128)(2,1)S(1)} %collective-permute-done.7.refs_1_, bf16[8,80,128]{2,1,0:T(8,128)(2,1)S(1)} %collective-permute-done.10.refs_2_), custom_call_target="tpu_custom_call" | custom-call | flops 147456000 | bytes 524288 | tf_op jit(solution)/shard_map/unit_product/pallas_call | solution.py:259
  28.0 0.0 collective-permute-done.6.refs_0_
  28.0 0.0 collective-permute-done.8.refs_1_
  28.0 0.0 collective-permute-done.9.refs_1_
  28.1 1.3 %collective-permute-done.4.refs_0_ = bf16[4,80,128]{2,1,0:T(8,128)(2,1)S(1)} collective-permute-done((bf16[4,80,128]{2,1,0:T(8,128)(2,1)S(1)}, bf16[4,80,128]{2,1,0:T(8,128)(2,1)S(1)}, u32[]{:S(2)}, u32[]{:S(2)}) %collective-permute-start.4) | collective-permute-done | bytes 81952 | tf_op jit(solution)/shard_map/ppermute | solution.py:353
  29.4 2.7 %collective-permute-start.12 = (bf16[16,80,128]{2,1,0:T(8,128)(2,1)S(1)}, bf16[16,80,128]{2,1,0:T(8,128)(2,1)S(1)}, u32[]{:S(2)}, u32[]{:S(2)}) collective-permute-start(bf16[16,80,128]{2,1,0:T(8,128)(2,1)S(1)} %pad_maximum_fusion), channel_id=1, source_target_pairs={{0,1},{1,0},{2,3},{3,2},{4,5},{5,4},{6,7},{7,6},{8,9},{9,8},{10,11... | collective-permute-start | bytes 983048 | tf_op jit(solution)/shard_map/ppermute | solution.py:367
  32.0 0.0 collective-permute-start.5
  32.0 1.5 %collective-permute-start.11 = (bf16[4,80,128]{2,1,0:T(8,128)(2,1)S(1)}, bf16[4,80,128]{2,1,0:T(8,128)(2,1)S(1)}, u32[]{:S(2)}, u32[]{:S(2)}) collective-permute-start(bf16[4,80,128]{2,1,0:T(8,128)(2,1)S(1)} %collective-permute-done.9.refs_1_), channel_id=1, source_target_pairs={{0,2},{2,0},{4,6},{6,4},{1,3},{3,1},{5,7},{7,5},{8,10},{10,8},{12,... | collective-permute-start | bytes 245768 | tf_op jit(solution)/shard_map/ppermute | solution.py:366
  33.5 0.0 collective-permute-done.12.refs_2_
  33.5 2.1 %unit_product.6.refs_3_ = f32[384,128]{1,0:T(8,128)S(1)} custom-call(f32[7,384,128]{2,1,0:T(8,128)S(1)} %pixel_columns.3.pix_ref, bf16[4,80,128]{2,1,0:T(8,128)(2,1)S(1)} %collective-permute-done.6.refs_0_, bf16[4,80,128]{2,1,0:T(8,128)(2,1)S(1)} %collective-permute-done.8.refs_1_, bf16[16,80,128]{2,1,0:T(8,128)(2,1)S(1)} %collective-permute-done.12.refs_2_, ...), custom_call_target="tpu_custom_call" | custom-call | flops 147456000 | bytes 524288 | tf_op jit(solution)/shard_map/unit_product/pallas_call | solution.py:259
  35.6 0.4 collective-permute-done.5
  35.9 1.8 %collective-permute-done.11 = bf16[4,80,128]{2,1,0:T(8,128)(2,1)S(1)} collective-permute-done((bf16[4,80,128]{2,1,0:T(8,128)(2,1)S(1)}, bf16[4,80,128]{2,1,0:T(8,128)(2,1)S(1)}, u32[]{:S(2)}, u32[]{:S(2)}) %collective-permute-start.11) | collective-permute-done | bytes 81952 | tf_op jit(solution)/shard_map/ppermute | solution.py:366
  37.7 1.2 %collective-permute-start.13 = (bf16[8,80,128]{2,1,0:T(8,128)(2,1)S(1)}, bf16[8,80,128]{2,1,0:T(8,128)(2,1)S(1)}, u32[]{:S(2)}, u32[]{:S(2)}) collective-permute-start(bf16[8,80,128]{2,1,0:T(8,128)(2,1)S(1)} %constant_dynamic-update-slice_fusion.refs_0_), channel_id=1, source_target_pairs={{0,1},{1,0},{2,3},{3,2},{4,5},{5,4},{6,7},{7,6},{8,9},{9,8},{10,11... | collective-permute-start | bytes 491528 | tf_op jit(solution)/shard_map/ppermute | solution.py:373
  38.9 2.1 %unit_product.7.refs_2_ = f32[384,128]{1,0:T(8,128)S(1)} custom-call(f32[7,384,128]{2,1,0:T(8,128)S(1)} %pixel_columns.3.pix_ref, bf16[4,80,128]{2,1,0:T(8,128)(2,1)S(1)} %collective-permute-done.4.refs_0_, bf16[4,80,128]{2,1,0:T(8,128)(2,1)S(1)} %collective-permute-done.9.refs_1_, bf16[16,80,128]{2,1,0:T(8,128)(2,1)S(1)} %collective-permute-done.12.refs_2_, ...), custom_call_target="tpu_custom_call" | custom-call | flops 147456000 | bytes 524288 | tf_op jit(solution)/shard_map/unit_product/pallas_call | solution.py:259
  41.0 0.0 collective-permute-done.13.refs_1_
  41.0 1.1 %unit_product.8 = f32[192,128]{1,0:T(8,128)S(1)} custom-call(f32[7,384,128]{2,1,0:T(8,128)S(1)} %pixel_columns.3.pix_ref, bf16[8,80,128]{2,1,0:T(8,128)(2,1)S(1)} %constant_dynamic-update-slice_fusion.refs_0_, bf16[8,80,128]{2,1,0:T(8,128)(2,1)S(1)} %collective-permute-done.13.refs_1_, f32[384,128]{1,0:T(8,128)S(1)} %unit_product.7.refs_2_), custom_call_target="tpu_custom_call" | custom-call | flops 73728000 | bytes 524288 | tf_op jit(solution)/shard_map/unit_product/pallas_call | solution.py:259
  42.1 0.9 %collective-permute-start.14 = (f32[4,48,128]{2,1,0:T(8,128)S(1)}, f32[4,48,128]{2,1,0:T(8,128)S(1)}, u32[]{:S(2)}, u32[]{:S(2)}) collective-permute-start(f32[4,48,128]{2,1,0:T(8,128)S(1)} %bitcast.12), channel_id=1, source_target_pairs={{0,192},{64,128},{128,64},{192,0},{1,193},{65,129},{129,65},{193,1... | collective-permute-start | bytes 294920 | tf_op jit(solution)/shard_map/ppermute | solution.py:383
  43.0 1.1 %unit_product.9 = f32[192,128]{1,0:T(8,128)S(1)} custom-call(f32[7,384,128]{2,1,0:T(8,128)S(1)} %pixel_columns.3.pix_ref, bf16[8,80,128]{2,1,0:T(8,128)(2,1)S(1)} %constant_dynamic-update-slice_fusion.refs_0_, bf16[8,80,128]{2,1,0:T(8,128)(2,1)S(1)} %collective-permute-done.13.refs_1_, f32[384,128]{1,0:T(8,128)S(1)} %unit_product.7.refs_2_), custom_call_target="tpu_custom_call" | custom-call | flops 73728000 | bytes 524288 | tf_op jit(solution)/shard_map/unit_product/pallas_call | solution.py:259
  44.1 0.1 collective-permute-start.16
  44.2 3.6 %collective-permute-done.14.got_ref = f32[4,48,128]{2,1,0:T(8,128)S(1)} collective-permute-done((f32[4,48,128]{2,1,0:T(8,128)S(1)}, f32[4,48,128]{2,1,0:T(8,128)S(1)}, u32[]{:S(2)}, u32[]{:S(2)}) %collective-permute-start.14) | collective-permute-done | bytes 98336 | tf_op jit(solution)/shard_map/ppermute | solution.py:383
  47.8 0.1 collective-permute-start.15
  47.9 0.3 collective-permute-done.16.got_ref
  48.2 2.0 %collective-permute-start.17 = (f32[4,48,128]{2,1,0:T(8,128)S(1)}, f32[4,48,128]{2,1,0:T(8,128)S(1)}, u32[]{:S(2)}, u32[]{:S(2)}) collective-permute-start(f32[4,48,128]{2,1,0:T(8,128)S(1)} %exchange_add.3.high_ref), channel_id=1, source_target_pairs={{0,192},{64,128},{128,64},{192,0},{1,193},{65,129},{129,65},{193,1... | collective-permute-start | bytes 294920 | tf_op jit(solution)/shard_map/ppermute | solution.py:386
  50.2 1.1 %collective-permute-done.15.low_got_ref = f32[4,48,128]{2,1,0:T(8,128)S(1)} collective-permute-done((f32[4,48,128]{2,1,0:T(8,128)S(1)}, f32[4,48,128]{2,1,0:T(8,128)S(1)}, u32[]{:S(2)}, u32[]{:S(2)}) %collective-permute-start.15) | collective-permute-done | bytes 98336 | tf_op jit(solution)/shard_map/ppermute | solution.py:386
  51.3 1.7 %collective-permute-done.17.high_got_ref = f32[4,48,128]{2,1,0:T(8,128)S(1)} collective-permute-done((f32[4,48,128]{2,1,0:T(8,128)S(1)}, f32[4,48,128]{2,1,0:T(8,128)S(1)}, u32[]{:S(2)}, u32[]{:S(2)}) %collective-permute-start.17) | collective-permute-done | bytes 98336 | tf_op jit(solution)/shard_map/ppermute | solution.py:386
  53.0 0.7 residual_part.1
  53.6 2.3 %collective-permute-start.18 = (f32[1,128]{1,0:T(1,128)S(1)}, f32[1,128]{1,0:T(1,128)S(1)}, u32[]{:S(2)}, u32[]{:S(2)}) collective-permute-start(f32[1,128]{1,0:T(1,128)S(1)} %get-tuple-element.31), channel_id=1, source_target_pairs={{0,1},{1,0},{2,3},{3,2},{4,5},{5,4},{6,7},{7,6},{8,9},{9,8},{10,11... | collective-permute-start | bytes 1544 | tf_op jit(solution)/shard_map/ppermute | solution.py:388
  55.9 0.8 %collective-permute-done.18 = f32[1,128]{1,0:T(1,128)S(1)} collective-permute-done((f32[1,128]{1,0:T(1,128)S(1)}, f32[1,128]{1,0:T(1,128)S(1)}, u32[]{:S(2)}, u32[]{:S(2)}) %collective-permute-start.18) | collective-permute-done | bytes 544 | tf_op jit(solution)/shard_map/ppermute | solution.py:388
  56.8 0.0 collective-permute-start.19
  56.8 2.4 %collective-permute-done.19 = f32[1,128]{1,0:T(1,128)S(1)} collective-permute-done((f32[1,128]{1,0:T(1,128)S(1)}, f32[1,128]{1,0:T(1,128)S(1)}, u32[]{:S(2)}, u32[]{:S(2)}) %collective-permute-start.19) | collective-permute-done | bytes 544 | tf_op jit(solution)/shard_map/ppermute | solution.py:398
  59.2 1.5 %collective-permute-start.20 = (f32[1,128]{1,0:T(1,128)S(1)}, f32[1,128]{1,0:T(1,128)S(1)}, u32[]{:S(2)}, u32[]{:S(2)}) collective-permute-start(f32[1,128]{1,0:T(1,128)S(1)} %add.19), channel_id=1, source_target_pairs={{1,7},{3,5},{5,3},{7,1},{0,2},{2,0},{4,6},{6,4},{9,15},{11,13},{13... | collective-permute-start | bytes 1544 | tf_op jit(solution)/shard_map/ppermute | solution.py:398
  60.7 2.1 %collective-permute-done.20 = f32[1,128]{1,0:T(1,128)S(1)} collective-permute-done((f32[1,128]{1,0:T(1,128)S(1)}, f32[1,128]{1,0:T(1,128)S(1)}, u32[]{:S(2)}, u32[]{:S(2)}) %collective-permute-start.20) | collective-permute-done | bytes 544 | tf_op jit(solution)/shard_map/ppermute | solution.py:398
  62.8 0.7 collective-permute-start.21
  63.5 1.7 %collective-permute-done.21 = f32[1,128]{1,0:T(1,128)S(1)} collective-permute-done((f32[1,128]{1,0:T(1,128)S(1)}, f32[1,128]{1,0:T(1,128)S(1)}, u32[]{:S(2)}, u32[]{:S(2)}) %collective-permute-start.21) | collective-permute-done | bytes 544 | tf_op jit(solution)/shard_map/ppermute | solution.py:398
  65.3 1.3 %collective-permute-start.22 = (f32[1,128]{1,0:T(1,128)S(1)}, f32[1,128]{1,0:T(1,128)S(1)}, u32[]{:S(2)}, u32[]{:S(2)}) collective-permute-start(f32[1,128]{1,0:T(1,128)S(1)} %add.21), channel_id=1, source_target_pairs={{1,17},{9,25},{17,1},{25,9},{33,49},{41,57},{49,33},{57,41},{0,8},... | collective-permute-start | bytes 1544 | tf_op jit(solution)/shard_map/ppermute | solution.py:398
  66.5 2.0 %collective-permute-done.22 = f32[1,128]{1,0:T(1,128)S(1)} collective-permute-done((f32[1,128]{1,0:T(1,128)S(1)}, f32[1,128]{1,0:T(1,128)S(1)}, u32[]{:S(2)}, u32[]{:S(2)}) %collective-permute-start.22) | collective-permute-done | bytes 544 | tf_op jit(solution)/shard_map/ppermute | solution.py:398
  68.6 1.3 %collective-permute-start.23 = (f32[1,128]{1,0:T(1,128)S(1)}, f32[1,128]{1,0:T(1,128)S(1)}, u32[]{:S(2)}, u32[]{:S(2)}) collective-permute-start(f32[1,128]{1,0:T(1,128)S(1)} %add.22), channel_id=1, source_target_pairs={{1,57},{9,49},{17,41},{25,33},{33,25},{41,17},{49,9},{57,1},{0,8},... | collective-permute-start | bytes 1544 | tf_op jit(solution)/shard_map/ppermute | solution.py:398
  69.9 2.3 %collective-permute-done.23 = f32[1,128]{1,0:T(1,128)S(1)} collective-permute-done((f32[1,128]{1,0:T(1,128)S(1)}, f32[1,128]{1,0:T(1,128)S(1)}, u32[]{:S(2)}, u32[]{:S(2)}) %collective-permute-start.23) | collective-permute-done | bytes 544 | tf_op jit(solution)/shard_map/ppermute | solution.py:398
  72.2 2.8 %collective-permute-start.24 = (f32[1,128]{1,0:T(1,128)S(1)}, f32[1,128]{1,0:T(1,128)S(1)}, u32[]{:S(2)}, u32[]{:S(2)}) collective-permute-start(f32[1,128]{1,0:T(1,128)S(1)} %add.23), channel_id=1, source_target_pairs={{0,1},{1,0},{2,3},{3,2},{4,5},{5,4},{6,7},{7,6},{8,9},{9,8},{10,11... | collective-permute-start | bytes 1544 | tf_op jit(solution)/shard_map/ppermute | solution.py:399
  75.0 0.8 %collective-permute-done.24 = f32[1,128]{1,0:T(1,128)S(1)} collective-permute-done((f32[1,128]{1,0:T(1,128)S(1)}, f32[1,128]{1,0:T(1,128)S(1)}, u32[]{:S(2)}, u32[]{:S(2)}) %collective-permute-start.24) | collective-permute-done | bytes 544 | tf_op jit(solution)/shard_map/ppermute | solution.py:399
  75.8 0.5 fusion.1
  (14 shorter events, 0.1 us)
Async XLA Ops:
  1.6 8.9 %collective-permute-start.2 = (f32[1,8,128]{2,1,0:T(8,128)S(1)}, f32[1,8,128]{2,1,0:T(8,128)S(1)}, u32[]{:S(2)}, u32[]{:S(2)}) collective-permute-start(f32[1,8,128]{2,1,0:T(8,128)S(1)} %get-tuple-element.18), channel_id=1, source_target_pairs={{0,64},{64,0},{128,192},{192,128},{1,65},{65,1},{129,193},{193,129... | collective-permute-start | bytes 12296 | tf_op jit(solution)/shard_map/ppermute | solution.py:349
  3.8 7.9 %collective-permute-start = (bf16[2,80,128]{2,1,0:T(8,128)(2,1)S(1)}, bf16[2,80,128]{2,1,0:T(8,128)(2,1)S(1)}, u32[]{:S(2)}, u32[]{:S(2)}) collective-permute-start(bf16[2,80,128]{2,1,0:T(8,128)(2,1)S(1)} %get-tuple-element.17), channel_id=1, source_target_pairs={{16,0},{24,8},{0,16},{8,24},{48,32},{56,40},{32,48},{40,56},{41,1}... | collective-permute-start | bytes 122888 | tf_op jit(solution)/shard_map/ppermute | solution.py:346
  10.3 5.0 %collective-permute-start.1 = (bf16[2,80,128]{2,1,0:T(8,128)(2,1)S(1)}, bf16[2,80,128]{2,1,0:T(8,128)(2,1)S(1)}, u32[]{:S(2)}, u32[]{:S(2)}) collective-permute-start(bf16[2,80,128]{2,1,0:T(8,128)(2,1)S(1)} %get-tuple-element.17), channel_id=1, source_target_pairs={{8,0},{0,8},{24,16},{16,24},{40,32},{32,40},{56,48},{48,56},{49,1}... | collective-permute-start | bytes 122888 | tf_op jit(solution)/shard_map/ppermute | solution.py:348
  15.3 3.4 %collective-permute-start.7 = (bf16[4,80,128]{2,1,0:T(8,128)(2,1)S(1)}, bf16[4,80,128]{2,1,0:T(8,128)(2,1)S(1)}, u32[]{:S(2)}, u32[]{:S(2)}) collective-permute-start(bf16[4,80,128]{2,1,0:T(8,128)(2,1)S(1)} %maximum_select_fusion.refs_0_), channel_id=1, source_target_pairs={{0,8},{8,0},{16,24},{24,16},{32,40},{40,32},{48,56},{56,48},{1,9},... | collective-permute-start | bytes 245768 | tf_op jit(solution)/shard_map/ppermute | solution.py:352
  18.7 7.3 %collective-permute-start.10 = (bf16[8,80,128]{2,1,0:T(8,128)(2,1)S(1)}, bf16[8,80,128]{2,1,0:T(8,128)(2,1)S(1)}, u32[]{:S(2)}, u32[]{:S(2)}) collective-permute-start(bf16[8,80,128]{2,1,0:T(8,128)(2,1)S(1)} %pad_maximum_fusion.1), channel_id=1, source_target_pairs={{0,1},{1,0},{2,3},{3,2},{4,5},{5,4},{6,7},{7,6},{8,9},{9,8},{10,11... | collective-permute-start | bytes 491528 | tf_op jit(solution)/shard_map/ppermute | solution.py:360
  18.8 5.9 %collective-permute-start.3 = (f32[2,8,128]{2,1,0:T(8,128)S(1)}, f32[2,8,128]{2,1,0:T(8,128)S(1)}, u32[]{:S(2)}, u32[]{:S(2)}) collective-permute-start(f32[2,8,128]{2,1,0:T(8,128)S(1)} %pad_maximum_fusion.2.sites_ref), channel_id=1, source_target_pairs={{0,192},{64,128},{128,64},{192,0},{1,193},{65,129},{129,65},{193,1... | collective-permute-start | bytes 24584 | tf_op jit(solution)/shard_map/ppermute | solution.py:355
  20.8 7.3 %collective-permute-start.6 = (bf16[4,80,128]{2,1,0:T(8,128)(2,1)S(1)}, bf16[4,80,128]{2,1,0:T(8,128)(2,1)S(1)}, u32[]{:S(2)}, u32[]{:S(2)}) collective-permute-start(bf16[4,80,128]{2,1,0:T(8,128)(2,1)S(1)} %maximum_select_fusion.refs_0_), channel_id=1, source_target_pairs={{0,2},{2,0},{4,6},{6,4},{1,3},{3,1},{5,7},{7,5},{8,10},{10,8},{12,... | collective-permute-start | bytes 245768 | tf_op jit(solution)/shard_map/ppermute | solution.py:354
  22.0 6.1 %collective-permute-start.8 = (bf16[4,80,128]{2,1,0:T(8,128)(2,1)S(1)}, bf16[4,80,128]{2,1,0:T(8,128)(2,1)S(1)}, u32[]{:S(2)}, u32[]{:S(2)}) collective-permute-start(bf16[4,80,128]{2,1,0:T(8,128)(2,1)S(1)} %collective-permute-done.7.refs_1_), channel_id=1, source_target_pairs={{0,2},{2,0},{4,6},{6,4},{1,3},{3,1},{5,7},{7,5},{8,10},{10,8},{12,... | collective-permute-start | bytes 245768 | tf_op jit(solution)/shard_map/ppermute | solution.py:359
  22.2 5.8 %collective-permute-start.9 = (bf16[4,80,128]{2,1,0:T(8,128)(2,1)S(1)}, bf16[4,80,128]{2,1,0:T(8,128)(2,1)S(1)}, u32[]{:S(2)}, u32[]{:S(2)}) collective-permute-start(bf16[4,80,128]{2,1,0:T(8,128)(2,1)S(1)} %collective-permute-done.7.refs_1_), channel_id=1, source_target_pairs={{0,6},{2,4},{4,2},{6,0},{1,7},{3,5},{5,3},{7,1},{8,14},{10,12},{12... | collective-permute-start | bytes 245768 | tf_op jit(solution)/shard_map/ppermute | solution.py:358
  24.7 4.6 %collective-permute-start.4 = (bf16[4,80,128]{2,1,0:T(8,128)(2,1)S(1)}, bf16[4,80,128]{2,1,0:T(8,128)(2,1)S(1)}, u32[]{:S(2)}, u32[]{:S(2)}) collective-permute-start(bf16[4,80,128]{2,1,0:T(8,128)(2,1)S(1)} %maximum_select_fusion.refs_0_), channel_id=1, source_target_pairs={{0,6},{2,4},{4,2},{6,0},{1,7},{3,5},{5,3},{7,1},{8,14},{10,12},{12... | collective-permute-start | bytes 245768 | tf_op jit(solution)/shard_map/ppermute | solution.py:353
  29.4 4.1 %collective-permute-start.12 = (bf16[16,80,128]{2,1,0:T(8,128)(2,1)S(1)}, bf16[16,80,128]{2,1,0:T(8,128)(2,1)S(1)}, u32[]{:S(2)}, u32[]{:S(2)}) collective-permute-start(bf16[16,80,128]{2,1,0:T(8,128)(2,1)S(1)} %pad_maximum_fusion), channel_id=1, source_target_pairs={{0,1},{1,0},{2,3},{3,2},{4,5},{5,4},{6,7},{7,6},{8,9},{9,8},{10,11... | collective-permute-start | bytes 983048 | tf_op jit(solution)/shard_map/ppermute | solution.py:367
  32.0 3.9 %collective-permute-start.5 = (bf16[4,80,128]{2,1,0:T(8,128)(2,1)S(1)}, bf16[4,80,128]{2,1,0:T(8,128)(2,1)S(1)}, u32[]{:S(2)}, u32[]{:S(2)}) collective-permute-start(bf16[4,80,128]{2,1,0:T(8,128)(2,1)S(1)} %collective-permute-done.4.refs_0_), channel_id=1, source_target_pairs={{0,2},{2,0},{4,6},{6,4},{1,3},{3,1},{5,7},{7,5},{8,10},{10,8},{12,... | collective-permute-start | bytes 245768 | tf_op jit(solution)/shard_map/ppermute | solution.py:361
  32.0 5.7 %collective-permute-start.11 = (bf16[4,80,128]{2,1,0:T(8,128)(2,1)S(1)}, bf16[4,80,128]{2,1,0:T(8,128)(2,1)S(1)}, u32[]{:S(2)}, u32[]{:S(2)}) collective-permute-start(bf16[4,80,128]{2,1,0:T(8,128)(2,1)S(1)} %collective-permute-done.9.refs_1_), channel_id=1, source_target_pairs={{0,2},{2,0},{4,6},{6,4},{1,3},{3,1},{5,7},{7,5},{8,10},{10,8},{12,... | collective-permute-start | bytes 245768 | tf_op jit(solution)/shard_map/ppermute | solution.py:366
  37.7 3.3 %collective-permute-start.13 = (bf16[8,80,128]{2,1,0:T(8,128)(2,1)S(1)}, bf16[8,80,128]{2,1,0:T(8,128)(2,1)S(1)}, u32[]{:S(2)}, u32[]{:S(2)}) collective-permute-start(bf16[8,80,128]{2,1,0:T(8,128)(2,1)S(1)} %constant_dynamic-update-slice_fusion.refs_0_), channel_id=1, source_target_pairs={{0,1},{1,0},{2,3},{3,2},{4,5},{5,4},{6,7},{7,6},{8,9},{9,8},{10,11... | collective-permute-start | bytes 491528 | tf_op jit(solution)/shard_map/ppermute | solution.py:373
  42.1 5.6 %collective-permute-start.14 = (f32[4,48,128]{2,1,0:T(8,128)S(1)}, f32[4,48,128]{2,1,0:T(8,128)S(1)}, u32[]{:S(2)}, u32[]{:S(2)}) collective-permute-start(f32[4,48,128]{2,1,0:T(8,128)S(1)} %bitcast.12), channel_id=1, source_target_pairs={{0,192},{64,128},{128,64},{192,0},{1,193},{65,129},{129,65},{193,1... | collective-permute-start | bytes 294920 | tf_op jit(solution)/shard_map/ppermute | solution.py:383
  44.1 4.1 %collective-permute-start.16 = (f32[4,48,128]{2,1,0:T(8,128)S(1)}, f32[4,48,128]{2,1,0:T(8,128)S(1)}, u32[]{:S(2)}, u32[]{:S(2)}) collective-permute-start(f32[4,48,128]{2,1,0:T(8,128)S(1)} %bitcast.10), channel_id=1, source_target_pairs={{0,64},{64,0},{128,192},{192,128},{1,65},{65,1},{129,193},{193,129... | collective-permute-start | bytes 294920 | tf_op jit(solution)/shard_map/ppermute | solution.py:384
  47.8 3.6 %collective-permute-start.15 = (f32[4,48,128]{2,1,0:T(8,128)S(1)}, f32[4,48,128]{2,1,0:T(8,128)S(1)}, u32[]{:S(2)}, u32[]{:S(2)}) collective-permute-start(f32[4,48,128]{2,1,0:T(8,128)S(1)} %exchange_add.2.low_ref), channel_id=1, source_target_pairs={{0,64},{64,0},{128,192},{192,128},{1,65},{65,1},{129,193},{193,129... | collective-permute-start | bytes 294920 | tf_op jit(solution)/shard_map/ppermute | solution.py:386
  48.2 4.8 %collective-permute-start.17 = (f32[4,48,128]{2,1,0:T(8,128)S(1)}, f32[4,48,128]{2,1,0:T(8,128)S(1)}, u32[]{:S(2)}, u32[]{:S(2)}) collective-permute-start(f32[4,48,128]{2,1,0:T(8,128)S(1)} %exchange_add.3.high_ref), channel_id=1, source_target_pairs={{0,192},{64,128},{128,64},{192,0},{1,193},{65,129},{129,65},{193,1... | collective-permute-start | bytes 294920 | tf_op jit(solution)/shard_map/ppermute | solution.py:386
  53.6 3.1 %collective-permute-start.18 = (f32[1,128]{1,0:T(1,128)S(1)}, f32[1,128]{1,0:T(1,128)S(1)}, u32[]{:S(2)}, u32[]{:S(2)}) collective-permute-start(f32[1,128]{1,0:T(1,128)S(1)} %get-tuple-element.31), channel_id=1, source_target_pairs={{0,1},{1,0},{2,3},{3,2},{4,5},{5,4},{6,7},{7,6},{8,9},{9,8},{10,11... | collective-permute-start | bytes 1544 | tf_op jit(solution)/shard_map/ppermute | solution.py:388
  56.8 2.4 %collective-permute-start.19 = (f32[1,128]{1,0:T(1,128)S(1)}, f32[1,128]{1,0:T(1,128)S(1)}, u32[]{:S(2)}, u32[]{:S(2)}) collective-permute-start(f32[1,128]{1,0:T(1,128)S(1)} %add.18), channel_id=1, source_target_pairs={{1,3},{3,1},{5,7},{7,5},{0,2},{2,0},{4,6},{6,4},{9,11},{11,9},{13,... | collective-permute-start | bytes 1544 | tf_op jit(solution)/shard_map/ppermute | solution.py:398
  59.2 3.6 %collective-permute-start.20 = (f32[1,128]{1,0:T(1,128)S(1)}, f32[1,128]{1,0:T(1,128)S(1)}, u32[]{:S(2)}, u32[]{:S(2)}) collective-permute-start(f32[1,128]{1,0:T(1,128)S(1)} %add.19), channel_id=1, source_target_pairs={{1,7},{3,5},{5,3},{7,1},{0,2},{2,0},{4,6},{6,4},{9,15},{11,13},{13... | collective-permute-start | bytes 1544 | tf_op jit(solution)/shard_map/ppermute | solution.py:398
  62.8 2.4 %collective-permute-start.21 = (f32[1,128]{1,0:T(1,128)S(1)}, f32[1,128]{1,0:T(1,128)S(1)}, u32[]{:S(2)}, u32[]{:S(2)}) collective-permute-start(f32[1,128]{1,0:T(1,128)S(1)} %add.20), channel_id=1, source_target_pairs={{1,9},{9,1},{17,25},{25,17},{33,41},{41,33},{49,57},{57,49},{0,8},... | collective-permute-start | bytes 1544 | tf_op jit(solution)/shard_map/ppermute | solution.py:398
  65.3 3.3 %collective-permute-start.22 = (f32[1,128]{1,0:T(1,128)S(1)}, f32[1,128]{1,0:T(1,128)S(1)}, u32[]{:S(2)}, u32[]{:S(2)}) collective-permute-start(f32[1,128]{1,0:T(1,128)S(1)} %add.21), channel_id=1, source_target_pairs={{1,17},{9,25},{17,1},{25,9},{33,49},{41,57},{49,33},{57,41},{0,8},... | collective-permute-start | bytes 1544 | tf_op jit(solution)/shard_map/ppermute | solution.py:398
  68.6 3.6 %collective-permute-start.23 = (f32[1,128]{1,0:T(1,128)S(1)}, f32[1,128]{1,0:T(1,128)S(1)}, u32[]{:S(2)}, u32[]{:S(2)}) collective-permute-start(f32[1,128]{1,0:T(1,128)S(1)} %add.22), channel_id=1, source_target_pairs={{1,57},{9,49},{17,41},{25,33},{33,25},{41,17},{49,9},{57,1},{0,8},... | collective-permute-start | bytes 1544 | tf_op jit(solution)/shard_map/ppermute | solution.py:398
  72.2 3.6 %collective-permute-start.24 = (f32[1,128]{1,0:T(1,128)S(1)}, f32[1,128]{1,0:T(1,128)S(1)}, u32[]{:S(2)}, u32[]{:S(2)}) collective-permute-start(f32[1,128]{1,0:T(1,128)S(1)} %add.23), channel_id=1, source_target_pairs={{0,1},{1,0},{2,3},{3,2},{4,5},{5,4},{6,7},{7,6},{8,9},{9,8},{10,11... | collective-permute-start | bytes 1544 | tf_op jit(solution)/shard_map/ppermute | solution.py:399

commit v5 on v4

--- a/solution.py
+++ b/solution.py
@@ -22,6 +22,14 @@
 FRAME_STRIDE = 40
 NEAR_ORDER = (1, 0, 3, 2)
 FAR_ORDER = (2, 3, 0, 1)
+FIRST_SHARE = 7
+
+
+def shares(width):
+    first = width * FIRST_SHARE // 12
+    return ((0, first, 0), (first, width - first, 4 * first))
+
+
 VIEW_SCALE = 3.0 / (2.0 * math.pi)
 
 
@@ -127,7 +135,6 @@
 
 def columns_kernel(width, first, sites_ref, *refs):
     pix_ref = refs[-1]
-    half = width // 2
     for block in range(sites_ref.shape[0]):
         columns = jnp.transpose(sites_ref[block])[:width]
         for f in range(7):
@@ -137,9 +144,9 @@
             if f == 6:
                 column = columns[:, 7:8] / column
             column = jnp.broadcast_to(column, (width, LANES))
-            for part in range(2):
-                row = (part * 4 + first + block) * half
-                pix_ref[f, row : row + half, :] = column[part * half : (part + 1) * half]
+            for start, size, offset in shares(width):
+                row = offset + (first + block) * size
+                pix_ref[f, row : row + size, :] = column[start : start + size]
 
 
 def pixel_columns(sites, width, first, before=None):
@@ -161,7 +168,7 @@
     out_ref, green_ref = refs[-2:]
     pixels = out_ref.shape[0]
     step = 16
-    span = 192
+    span = pixels // 2
 
     def gathered(unit, row, rows):
         return jnp.concatenate(
@@ -269,19 +276,17 @@
 
 
 def residual_kernel(pix_ref, low_ref, low_got_ref, high_ref, high_got_ref, res_ref, sum_ref):
-    half = low_ref.shape[1]
+    width = low_ref.shape[1] + high_ref.shape[1]
+    parts = (low_ref, low_got_ref, NEAR_ORDER), (high_ref, high_got_ref, FAR_ORDER)
     sums = []
     for block in range(4):
         total = jnp.zeros((1, LANES), jnp.float32)
-        for part, (mine, got, order) in enumerate(
-            [(low_ref, low_got_ref, NEAR_ORDER), (high_ref, high_got_ref, FAR_ORDER)]
-        ):
+        for (start, size, offset), (mine, got, order) in zip(shares(width), parts):
             value = mine[block] + got[order[block]]
-            row = (part * 4 + block) * half
-            here = slice(row, row + half)
+            here = slice(offset + block * size, offset + (block + 1) * size)
             res = (value - pix_ref[5, here, :]) * pix_ref[6, here, :]
             if block == 0:
-                res_ref[part * half : (part + 1) * half, :] = res
+                res_ref[start : start + size, :] = res
             total = total + jnp.sum(res * res, axis=0, keepdims=True)
         sums.append(total)
     sum_ref[...] = (sums[0] + sums[1]) + (sums[2] + sums[3])
@@ -291,7 +296,7 @@
     return pl.pallas_call(
         residual_kernel,
         out_shape=(
-            jax.ShapeDtypeStruct((2 * low.shape[1], LANES), jnp.float32),
+            jax.ShapeDtypeStruct((low.shape[1] + high.shape[1], LANES), jnp.float32),
             vmem_array((1, LANES), jnp.float32),
         ),
         in_specs=[VMEM_SPEC] * 5,
@@ -362,7 +367,6 @@
     part = four.shape[0]
     count = 2 * part
     acc = unit_product(pix, (four, four_got, own_other), (((0, 0, part), (1, 0, part), (2, 0, count)),))
-    near_a, near_b, far_b, acc = lax.optimization_barrier((near_a, near_b, far_b, acc))
     across_b = lax.ppermute(far_b, "x", near_pairs)
     others = lax.ppermute(stack(near_a, near_b, far_a, far_b), "pix", swap)
     acc = unit_product(
@@ -376,26 +380,31 @@
     )
     across_other, acc = lax.optimization_barrier((across_other, acc))
     last = (((0, 0, count), (1, 0, count)),)
-    rows = 2 * own_pixels
-    shape = (4, own_pixels // 2, LANES)
-    low = unit_product(pix, (across, across_other), last, acc, 0, rows).reshape(shape)
-    high = unit_product(pix, (across, across_other), last, acc, rows, rows).reshape(shape)
+
+    def last_product(share):
+        _, size, offset = share
+        value = unit_product(pix, (across, across_other), last, acc, offset, 4 * size)
+        return value.reshape(4, size, LANES)
+
+    first_share, second_share = shares(own_pixels)
+    low = last_product(first_share)
+    high = last_product(second_share)
     low = exchange_add(low, lax.ppermute(low, "y", far_pairs), FAR_ORDER)
     high = exchange_add(high, lax.ppermute(high, "y", near_pairs), NEAR_ORDER)
-    residual, own_sum = residual_part(
-        pix, low, lax.ppermute(low, "y", near_pairs), high, lax.ppermute(high, "y", far_pairs)
-    )
+    low_got = lax.ppermute(low, "y", near_pairs)
+    high_got = lax.ppermute(high, "y", far_pairs)
+    residual, own_sum = residual_part(pix, low, low_got, high, high_got)
     total = own_sum + lax.ppermute(own_sum, "pix", swap)
-    for axis, pairs in [
-        ("x", near_pairs),
-        ("x", far_pairs),
-        ("z", xor_pairs(8, 1)),
-        ("z", xor_pairs(8, 2)),
-        ("z", mirror_pairs(8)),
-    ]:
+    meets = [(2 * (i ^ 1), 2 * i) for i in range(4)] + [(2 * (i ^ 2) + 1, 2 * i + 1) for i in range(4)]
+    first = lax.ppermute(total, ("x", "pix"), meets)
+    meets = [(2 * (i ^ 1), 2 * i) for i in range(4)] + [(2 * (i ^ 3) + 1, 2 * i + 1) for i in range(4)]
+    second = lax.ppermute(total, ("x", "pix"), meets)
+    total = first + jnp.where(core == 0, total, second)
+    total = total + lax.ppermute(total, "pix", swap)
+    for pairs in [xor_pairs(8, 1), xor_pairs(8, 2), mirror_pairs(8)]:
         meets = [(2 * source + 1, 2 * target + 1) for source, target in pairs]
         meets += [(2 * i, 2 * (i ^ 1)) for i, _ in pairs]
-        total = total + lax.ppermute(total, (axis, "pix"), meets)
+        total = total + lax.ppermute(total, ("z", "pix"), meets)
     total = jnp.where(core == 1, total, lax.ppermute(total, "pix", swap))
     pixels = own_pixels * lax.axis_size(PATCH) * lax.axis_size("pix")
     return (residual, total[0] / pixels)

time: 76.5 us -> 74.2 us (0.970)
  waiting for transfers between devices: 29.7 us -> 26.6 us
    ppermute x1, starting transfers between devices: 2.66 us -> 0.09 us  [per_device(): others = lax.ppermute(stack(near_a, near_b, far_a, far_b), 'pix', swap)]
    ppermute x1, waiting for transfers between devices: 2.59 us -> 0.4 us  [per_device(): four_got = lax.ppermute(four, 'z', xor_pairs(8, 1))]
    ppermute x1, starting transfers between devices: 0.34 us -> 2.48 us  [per_device(): far_a = lax.ppermute(four, 'x', far_pairs)]
    ppermute x7 -> x8, waiting for transfers between devices: 13.4 us -> 11.6 us  [the longest x3 5.03 us: per_device(): total = total + lax.ppermute(total, ('z', 'pix'), meets)]
    ppermute x1, waiting for transfers between devices: 1.76 us -> 0.01 us  [per_device(): across_b = lax.ppermute(far_b, 'x', near_pairs)]
    ppermute x1, waiting for transfers between devices: 0.01 us -> 1.36 us  [per_device(): sites_far = lax.ppermute(sites, 'y', far_pairs)]
    ppermute x1, waiting for transfers between devices: 0.01 us -> 1.32 us  [per_device(): far_b = lax.ppermute(four_got, 'x', far_pairs)]
    ppermute x1, waiting for transfers between devices: 0.01 us -> 1.27 us  [per_device(): near_b = lax.ppermute(four_got, 'x', near_pairs)]
  transfers between devices with their start and end apart: 25 -> 26, of which waited for: 17 -> 18; matrix products, arithmetic and copies ran while one was open for 0% -> 0% of each run, Pallas kernels for 11% -> 11%
where the time goes in v5:
time: 74.2 us; the launch traced here: 74 us
  starting transfers between devices  34.7 us (47%)
  waiting for transfers between devices  26.6 us (36%)
  Pallas kernels  11.4 us (15%)
  between operations  0.8 us (1%)
    pallas_call x5, Pallas kernels, unit_product(): pl.pallas_call(functools.partial(unit_kernel, units, len(parts), acc is n...  8.8 us
    ppermute x1, starting transfers between devices, per_device(): first = lax.ppermute(piece, ('z', 'pix'), meets)  6.46 us
    ppermute x3, waiting for transfers between devices, per_device(): total = total + lax.ppermute(total, ('z', 'pix'), meets)  5.03 us
    ppermute x3, starting transfers between devices, per_device(): total = total + lax.ppermute(total, ('z', 'pix'), meets)  4.33 us
    ppermute x1, waiting for transfers between devices, per_device(): second = lax.ppermute(piece, ('z', 'pix'), meets)  3.6 us
    ppermute x1, waiting for transfers between devices, per_device(): high_got = lax.ppermute(high, 'y', far_pairs)  3.44 us
    ppermute x1, waiting for transfers between devices, per_device(): low = exchange_add(low, lax.ppermute(low, 'y', far_pairs), FAR_ORDER)  2.71 us
    ppermute x1, starting transfers between devices, per_device(): far_a = lax.ppermute(four, 'x', far_pairs)  2.48 us
  transfers between devices with their start and end apart: 26, of which 18 were waited for; matrix products, arithmetic and copies ran while one was open for 0% of the time, Pallas kernels for 11%

profile of v5, /device:TPU:1, one launch (start us, length us, event | category | flops | bytes accessed | tf_op | source)
XLA Modules:
  0.0 74.0 jit_solution(5232987960086674559)
XLA Ops:
  0.6 1.0 %prepare.1 = (bf16[2,80,128]{2,1,0:T(8,128)(2,1)S(1)}, f32[1,8,128]{2,1,0:T(8,128)S(1)}) custom-call(f32[16]{0:T(128)} %strike_ref.1, f32[16]{0:T(128)} %dip_ref.1, f32[2,48]{1,0:T(2,128)} %pos_ref.1, f32[1,48]{1,0:T(1,128)} %bitcast.15, s32[1,48]{1,0:T(1,128)} %bitcast.16, bf16[3,48,128]{2,1,0:T(8,128)(2,1)} %bitcast.14, f32[2,96]{1,0:T(2,128)} %pixel_ref.1, ...), custom_call_target="tpu_custom_call" | custom-call | tf_op jit(solution)/shard_map/prepare/pallas_call | solution.py:125
  1.6 2.2 %collective-permute-start.2 = (f32[1,8,128]{2,1,0:T(8,128)S(1)}, f32[1,8,128]{2,1,0:T(8,128)S(1)}, u32[]{:S(2)}, u32[]{:S(2)}) collective-permute-start(f32[1,8,128]{2,1,0:T(8,128)S(1)} %get-tuple-element.14), channel_id=1, source_target_pairs={{0,64},{64,0},{128,192},{192,128},{1,65},{65,1},{129,193},{193,129... | collective-permute-start | bytes 12296 | tf_op jit(solution)/shard_map/ppermute | solution.py:354
  3.8 6.5 %collective-permute-start = (bf16[2,80,128]{2,1,0:T(8,128)(2,1)S(1)}, bf16[2,80,128]{2,1,0:T(8,128)(2,1)S(1)}, u32[]{:S(2)}, u32[]{:S(2)}) collective-permute-start(bf16[2,80,128]{2,1,0:T(8,128)(2,1)S(1)} %get-tuple-element.13), channel_id=1, source_target_pairs={{16,0},{24,8},{0,16},{8,24},{48,32},{56,40},{32,48},{40,56},{41,1}... | collective-permute-start | bytes 122888 | tf_op jit(solution)/shard_map/ppermute | solution.py:351
  10.3 0.3 collective-permute-start.1
  10.5 0.0 collective-permute-done.2
  10.6 1.1 %collective-permute-done = bf16[2,80,128]{2,1,0:T(8,128)(2,1)S(1)} collective-permute-done((bf16[2,80,128]{2,1,0:T(8,128)(2,1)S(1)}, bf16[2,80,128]{2,1,0:T(8,128)(2,1)S(1)}, u32[]{:S(2)}, u32[]{:S(2)}) %collective-permute-start) | collective-permute-done | bytes 40992 | tf_op jit(solution)/shard_map/ppermute | solution.py:351
  11.7 3.6 %collective-permute-done.1 = bf16[2,80,128]{2,1,0:T(8,128)(2,1)S(1)} collective-permute-done((bf16[2,80,128]{2,1,0:T(8,128)(2,1)S(1)}, bf16[2,80,128]{2,1,0:T(8,128)(2,1)S(1)}, u32[]{:S(2)}, u32[]{:S(2)}) %collective-permute-start.1) | collective-permute-done | bytes 40992 | tf_op jit(solution)/shard_map/ppermute | solution.py:353
  15.3 0.8 %collective-permute-start.6 = (bf16[4,80,128]{2,1,0:T(8,128)(2,1)S(1)}, bf16[4,80,128]{2,1,0:T(8,128)(2,1)S(1)}, u32[]{:S(2)}, u32[]{:S(2)}) collective-permute-start(bf16[4,80,128]{2,1,0:T(8,128)(2,1)S(1)} %maximum_select_fusion.refs_0_), channel_id=1, source_target_pairs={{0,8},{8,0},{16,24},{24,16},{32,40},{40,32},{48,56},{56,48},{1,9},... | collective-permute-start | bytes 245768 | tf_op jit(solution)/shard_map/ppermute | solution.py:357
  16.1 2.5 %collective-permute-start.4 = (bf16[4,80,128]{2,1,0:T(8,128)(2,1)S(1)}, bf16[4,80,128]{2,1,0:T(8,128)(2,1)S(1)}, u32[]{:S(2)}, u32[]{:S(2)}) collective-permute-start(bf16[4,80,128]{2,1,0:T(8,128)(2,1)S(1)} %maximum_select_fusion.refs_0_), channel_id=1, source_target_pairs={{0,6},{2,4},{4,2},{6,0},{1,7},{3,5},{5,3},{7,1},{8,14},{10,12},{12... | collective-permute-start | bytes 245768 | tf_op jit(solution)/shard_map/ppermute | solution.py:358
  18.5 0.0 collective-permute-start.9
  18.5 0.4 collective-permute-done.6.refs_1_
  18.9 2.5 %collective-permute-start.7 = (bf16[4,80,128]{2,1,0:T(8,128)(2,1)S(1)}, bf16[4,80,128]{2,1,0:T(8,128)(2,1)S(1)}, u32[]{:S(2)}, u32[]{:S(2)}) collective-permute-start(bf16[4,80,128]{2,1,0:T(8,128)(2,1)S(1)} %collective-permute-done.6.refs_1_), channel_id=1, source_target_pairs={{0,6},{2,4},{4,2},{6,0},{1,7},{3,5},{5,3},{7,1},{8,14},{10,12},{12... | collective-permute-start | bytes 245768 | tf_op jit(solution)/shard_map/ppermute | solution.py:363
  21.4 0.0 collective-permute-start.10
  21.4 0.0 collective-permute-done.4.refs_0_
  21.4 0.7 collective-permute-done.9.refs_0_
  22.1 1.3 %collective-permute-done.7.refs_1_ = bf16[4,80,128]{2,1,0:T(8,128)(2,1)S(1)} collective-permute-done((bf16[4,80,128]{2,1,0:T(8,128)(2,1)S(1)}, bf16[4,80,128]{2,1,0:T(8,128)(2,1)S(1)}, u32[]{:S(2)}, u32[]{:S(2)}) %collective-permute-start.7) | collective-permute-done | bytes 81952 | tf_op jit(solution)/shard_map/ppermute | solution.py:363
  23.5 1.3 %collective-permute-done.10.refs_1_ = bf16[4,80,128]{2,1,0:T(8,128)(2,1)S(1)} collective-permute-done((bf16[4,80,128]{2,1,0:T(8,128)(2,1)S(1)}, bf16[4,80,128]{2,1,0:T(8,128)(2,1)S(1)}, u32[]{:S(2)}, u32[]{:S(2)}) %collective-permute-start.10) | collective-permute-done | bytes 81952 | tf_op jit(solution)/shard_map/ppermute | solution.py:364
  24.8 0.1 collective-permute-start.11
  24.9 0.6 collective-permute-start.12
  25.5 0.0 collective-permute-start.5
  25.5 1.5 %collective-permute-start.8 = (bf16[4,80,128]{2,1,0:T(8,128)(2,1)S(1)}, bf16[4,80,128]{2,1,0:T(8,128)(2,1)S(1)}, u32[]{:S(2)}, u32[]{:S(2)}) collective-permute-start(bf16[4,80,128]{2,1,0:T(8,128)(2,1)S(1)} %collective-permute-done.7.refs_1_), channel_id=1, source_target_pairs={{0,2},{2,0},{4,6},{6,4},{1,3},{3,1},{5,7},{7,5},{8,10},{10,8},{12,... | collective-permute-start | bytes 245768 | tf_op jit(solution)/shard_map/ppermute | solution.py:370
  26.9 1.9 %collective-permute-start.3 = (f32[2,8,128]{2,1,0:T(8,128)S(1)}, f32[2,8,128]{2,1,0:T(8,128)S(1)}, u32[]{:S(2)}, u32[]{:S(2)}) collective-permute-start(f32[2,8,128]{2,1,0:T(8,128)S(1)} %pad_maximum_fusion.2.sites_ref), channel_id=1, source_target_pairs={{0,192},{64,128},{128,64},{192,0},{1,193},{65,129},{129,65},{193,1... | collective-permute-start | bytes 24584 | tf_op jit(solution)/shard_map/ppermute | solution.py:360
  28.8 0.5 pixel_columns.2.refs_0_
  29.3 1.4 %collective-permute-done.3.sites_ref = f32[2,8,128]{2,1,0:T(8,128)S(1)} collective-permute-done((f32[2,8,128]{2,1,0:T(8,128)S(1)}, f32[2,8,128]{2,1,0:T(8,128)S(1)}, u32[]{:S(2)}, u32[]{:S(2)}) %collective-permute-start.3) | collective-permute-done | bytes 8224 | tf_op jit(solution)/shard_map/ppermute | solution.py:360
  30.7 0.5 pixel_columns.3.pix_ref
  31.1 0.0 collective-permute-done.12.refs_2_
  31.1 2.1 %unit_product.5.refs_3_ = f32[384,128]{1,0:T(8,128)S(1)} custom-call(f32[7,384,128]{2,1,0:T(8,128)S(1)} %pixel_columns.3.pix_ref, bf16[4,80,128]{2,1,0:T(8,128)(2,1)S(1)} %maximum_select_fusion.refs_0_, bf16[4,80,128]{2,1,0:T(8,128)(2,1)S(1)} %collective-permute-done.6.refs_1_, bf16[8,80,128]{2,1,0:T(8,128)(2,1)S(1)} %collective-permute-done.12.refs_2_), custom_call_target="tpu_custom_call" | custom-call | flops 147456000 | bytes 524288 | tf_op jit(solution)/shard_map/unit_product/pallas_call | solution.py:266
  33.2 0.0 collective-permute-done.11.refs_2_
  33.2 2.1 %unit_product.6.refs_3_ = f32[384,128]{1,0:T(8,128)S(1)} custom-call(f32[7,384,128]{2,1,0:T(8,128)S(1)} %pixel_columns.3.pix_ref, bf16[4,80,128]{2,1,0:T(8,128)(2,1)S(1)} %collective-permute-done.9.refs_0_, bf16[4,80,128]{2,1,0:T(8,128)(2,1)S(1)} %collective-permute-done.10.refs_1_, bf16[16,80,128]{2,1,0:T(8,128)(2,1)S(1)} %collective-permute-done.11.refs_2_, ...), custom_call_target="tpu_custom_call" | custom-call | flops 147456000 | bytes 524288 | tf_op jit(solution)/shard_map/unit_product/pallas_call | solution.py:266
  35.3 0.0 collective-permute-done.5
  35.3 0.0 collective-permute-done.8
  35.3 2.1 %collective-permute-start.13 = (bf16[8,80,128]{2,1,0:T(8,128)(2,1)S(1)}, bf16[8,80,128]{2,1,0:T(8,128)(2,1)S(1)}, u32[]{:S(2)}, u32[]{:S(2)}) collective-permute-start(bf16[8,80,128]{2,1,0:T(8,128)(2,1)S(1)} %constant_dynamic-update-slice_fusion.refs_0_), channel_id=1, source_target_pairs={{0,1},{1,0},{2,3},{3,2},{4,5},{5,4},{6,7},{7,6},{8,9},{9,8},{10,11... | collective-permute-start | bytes 491528 | tf_op jit(solution)/shard_map/ppermute | solution.py:377
  37.4 2.1 %unit_product.7.refs_2_ = f32[384,128]{1,0:T(8,128)S(1)} custom-call(f32[7,384,128]{2,1,0:T(8,128)S(1)} %pixel_columns.3.pix_ref, bf16[4,80,128]{2,1,0:T(8,128)(2,1)S(1)} %collective-permute-done.4.refs_0_, bf16[4,80,128]{2,1,0:T(8,128)(2,1)S(1)} %collective-permute-done.7.refs_1_, bf16[16,80,128]{2,1,0:T(8,128)(2,1)S(1)} %collective-permute-done.11.refs_2_, ...), custom_call_target="tpu_custom_call" | custom-call | flops 147456000 | bytes 524288 | tf_op jit(solution)/shard_map/unit_product/pallas_call | solution.py:266
  39.5 0.0 collective-permute-done.13.refs_1_
  39.5 1.4 %unit_product.8 = f32[224,128]{1,0:T(8,128)S(1)} custom-call(f32[7,384,128]{2,1,0:T(8,128)S(1)} %pixel_columns.3.pix_ref, bf16[8,80,128]{2,1,0:T(8,128)(2,1)S(1)} %constant_dynamic-update-slice_fusion.refs_0_, bf16[8,80,128]{2,1,0:T(8,128)(2,1)S(1)} %collective-permute-done.13.refs_1_, f32[384,128]{1,0:T(8,128)S(1)} %unit_product.7.refs_2_), custom_call_target="tpu_custom_call" | custom-call | flops 86016000 | bytes 524288 | tf_op jit(solution)/shard_map/unit_product/pallas_call | solution.py:266
  40.9 2.0 %collective-permute-start.14 = (f32[4,56,128]{2,1,0:T(8,128)S(1)}, f32[4,56,128]{2,1,0:T(8,128)S(1)}, u32[]{:S(2)}, u32[]{:S(2)}) collective-permute-start(f32[4,56,128]{2,1,0:T(8,128)S(1)} %bitcast.10), channel_id=1, source_target_pairs={{0,192},{64,128},{128,64},{192,0},{1,193},{65,129},{129,65},{193,1... | collective-permute-start | bytes 344072 | tf_op jit(solution)/shard_map/ppermute | solution.py:392
  42.9 1.2 %unit_product.9 = f32[160,128]{1,0:T(8,128)S(1)} custom-call(f32[7,384,128]{2,1,0:T(8,128)S(1)} %pixel_columns.3.pix_ref, bf16[8,80,128]{2,1,0:T(8,128)(2,1)S(1)} %constant_dynamic-update-slice_fusion.refs_0_, bf16[8,80,128]{2,1,0:T(8,128)(2,1)S(1)} %collective-permute-done.13.refs_1_, f32[384,128]{1,0:T(8,128)S(1)} %unit_product.7.refs_2_), custom_call_target="tpu_custom_call" | custom-call | flops 61440000 | bytes 524288 | tf_op jit(solution)/shard_map/unit_product/pallas_call | solution.py:266
  44.1 0.1 collective-permute-start.16
  44.2 2.7 %collective-permute-done.14.got_ref = f32[4,56,128]{2,1,0:T(8,128)S(1)} collective-permute-done((f32[4,56,128]{2,1,0:T(8,128)S(1)}, f32[4,56,128]{2,1,0:T(8,128)S(1)}, u32[]{:S(2)}, u32[]{:S(2)}) %collective-permute-start.14) | collective-permute-done | bytes 114720 | tf_op jit(solution)/shard_map/ppermute | solution.py:392
  46.9 0.1 collective-permute-start.15
  47.0 0.9 %collective-permute-done.16.got_ref = f32[4,40,128]{2,1,0:T(8,128)S(1)} collective-permute-done((f32[4,40,128]{2,1,0:T(8,128)S(1)}, f32[4,40,128]{2,1,0:T(8,128)S(1)}, u32[]{:S(2)}, u32[]{:S(2)}) %collective-permute-start.16) | collective-permute-done | bytes 81952 | tf_op jit(solution)/shard_map/ppermute | solution.py:393
  47.9 1.2 %collective-permute-start.17 = (f32[4,40,128]{2,1,0:T(8,128)S(1)}, f32[4,40,128]{2,1,0:T(8,128)S(1)}, u32[]{:S(2)}, u32[]{:S(2)}) collective-permute-start(f32[4,40,128]{2,1,0:T(8,128)S(1)} %exchange_add.3.high_ref), channel_id=1, source_target_pairs={{0,192},{64,128},{128,64},{192,0},{1,193},{65,129},{129,65},{193,1... | collective-permute-start | bytes 245768 | tf_op jit(solution)/shard_map/ppermute | solution.py:395
  49.0 3.4 %collective-permute-done.17.high_got_ref = f32[4,40,128]{2,1,0:T(8,128)S(1)} collective-permute-done((f32[4,40,128]{2,1,0:T(8,128)S(1)}, f32[4,40,128]{2,1,0:T(8,128)S(1)}, u32[]{:S(2)}, u32[]{:S(2)}) %collective-permute-start.17) | collective-permute-done | bytes 81952 | tf_op jit(solution)/shard_map/ppermute | solution.py:395
  52.5 0.0 collective-permute-done.15.low_got_ref
  52.5 0.7 residual_part.1
  53.1 2.3 %collective-permute-start.18 = (f32[1,128]{1,0:T(1,128)S(1)}, f32[1,128]{1,0:T(1,128)S(1)}, u32[]{:S(2)}, u32[]{:S(2)}) collective-permute-start(f32[1,128]{1,0:T(1,128)S(1)} %get-tuple-element.23), channel_id=1, source_target_pairs={{0,1},{1,0},{2,3},{3,2},{4,5},{5,4},{6,7},{7,6},{8,9},{9,8},{10,11... | collective-permute-start | bytes 1544 | tf_op jit(solution)/shard_map/ppermute | solution.py:397
  55.5 0.8 %collective-permute-done.18 = f32[1,128]{1,0:T(1,128)S(1)} collective-permute-done((f32[1,128]{1,0:T(1,128)S(1)}, f32[1,128]{1,0:T(1,128)S(1)}, u32[]{:S(2)}, u32[]{:S(2)}) %collective-permute-start.18) | collective-permute-done | bytes 544 | tf_op jit(solution)/shard_map/ppermute | solution.py:397
  56.3 0.8 %collective-permute-start.19 = (f32[1,128]{1,0:T(1,128)S(1)}, f32[1,128]{1,0:T(1,128)S(1)}, u32[]{:S(2)}, u32[]{:S(2)}) collective-permute-start(f32[1,128]{1,0:T(1,128)S(1)} %add.18), channel_id=1, source_target_pairs={{2,0},{0,2},{6,4},{4,6},{5,1},{7,3},{1,5},{3,7},{10,8},{8,10},{14,... | collective-permute-start | bytes 1544 | tf_op jit(solution)/shard_map/ppermute | solution.py:399
  57.0 1.6 %collective-permute-start.20 = (f32[1,128]{1,0:T(1,128)S(1)}, f32[1,128]{1,0:T(1,128)S(1)}, u32[]{:S(2)}, u32[]{:S(2)}) collective-permute-start(f32[1,128]{1,0:T(1,128)S(1)} %add.18), channel_id=1, source_target_pairs={{2,0},{0,2},{6,4},{4,6},{7,1},{5,3},{3,5},{1,7},{10,8},{8,10},{14,... | collective-permute-start | bytes 1544 | tf_op jit(solution)/shard_map/ppermute | solution.py:401
  58.7 1.5 %collective-permute-done.19 = f32[1,128]{1,0:T(1,128)S(1)} collective-permute-done((f32[1,128]{1,0:T(1,128)S(1)}, f32[1,128]{1,0:T(1,128)S(1)}, u32[]{:S(2)}, u32[]{:S(2)}) %collective-permute-start.19) | collective-permute-done | bytes 544 | tf_op jit(solution)/shard_map/ppermute | solution.py:399
  60.2 0.5 collective-permute-done.20
  60.7 0.0 collective-permute-start.21
  60.7 1.2 %collective-permute-done.21 = f32[1,128]{1,0:T(1,128)S(1)} collective-permute-done((f32[1,128]{1,0:T(1,128)S(1)}, f32[1,128]{1,0:T(1,128)S(1)}, u32[]{:S(2)}, u32[]{:S(2)}) %collective-permute-start.21) | collective-permute-done | bytes 544 | tf_op jit(solution)/shard_map/ppermute | solution.py:403
  61.8 0.7 collective-permute-start.22
  62.5 1.7 %collective-permute-done.22 = f32[1,128]{1,0:T(1,128)S(1)} collective-permute-done((f32[1,128]{1,0:T(1,128)S(1)}, f32[1,128]{1,0:T(1,128)S(1)}, u32[]{:S(2)}, u32[]{:S(2)}) %collective-permute-start.22) | collective-permute-done | bytes 544 | tf_op jit(solution)/shard_map/ppermute | solution.py:407
  64.3 1.0 %collective-permute-start.23 = (f32[1,128]{1,0:T(1,128)S(1)}, f32[1,128]{1,0:T(1,128)S(1)}, u32[]{:S(2)}, u32[]{:S(2)}) collective-permute-start(f32[1,128]{1,0:T(1,128)S(1)} %add.21), channel_id=1, source_target_pairs={{1,17},{9,25},{17,1},{25,9},{33,49},{41,57},{49,33},{57,41},{0,8},... | collective-permute-start | bytes 1544 | tf_op jit(solution)/shard_map/ppermute | solution.py:407
  65.3 2.3 %collective-permute-done.23 = f32[1,128]{1,0:T(1,128)S(1)} collective-permute-done((f32[1,128]{1,0:T(1,128)S(1)}, f32[1,128]{1,0:T(1,128)S(1)}, u32[]{:S(2)}, u32[]{:S(2)}) %collective-permute-start.23) | collective-permute-done | bytes 544 | tf_op jit(solution)/shard_map/ppermute | solution.py:407
  67.6 2.6 %collective-permute-start.24 = (f32[1,128]{1,0:T(1,128)S(1)}, f32[1,128]{1,0:T(1,128)S(1)}, u32[]{:S(2)}, u32[]{:S(2)}) collective-permute-start(f32[1,128]{1,0:T(1,128)S(1)} %add.22), channel_id=1, source_target_pairs={{1,57},{9,49},{17,41},{25,33},{33,25},{41,17},{49,9},{57,1},{0,8},... | collective-permute-start | bytes 1544 | tf_op jit(solution)/shard_map/ppermute | solution.py:407
  70.2 1.0 %collective-permute-done.24 = f32[1,128]{1,0:T(1,128)S(1)} collective-permute-done((f32[1,128]{1,0:T(1,128)S(1)}, f32[1,128]{1,0:T(1,128)S(1)}, u32[]{:S(2)}, u32[]{:S(2)}) %collective-permute-start.24) | collective-permute-done | bytes 544 | tf_op jit(solution)/shard_map/ppermute | solution.py:407
  71.2 1.5 %collective-permute-start.25 = (f32[1,128]{1,0:T(1,128)S(1)}, f32[1,128]{1,0:T(1,128)S(1)}, u32[]{:S(2)}, u32[]{:S(2)}) collective-permute-start(f32[1,128]{1,0:T(1,128)S(1)} %add.23), channel_id=1, source_target_pairs={{0,1},{1,0},{2,3},{3,2},{4,5},{5,4},{6,7},{7,6},{8,9},{9,8},{10,11... | collective-permute-start | bytes 1544 | tf_op jit(solution)/shard_map/ppermute | solution.py:408
  72.7 0.8 %collective-permute-done.25 = f32[1,128]{1,0:T(1,128)S(1)} collective-permute-done((f32[1,128]{1,0:T(1,128)S(1)}, f32[1,128]{1,0:T(1,128)S(1)}, u32[]{:S(2)}, u32[]{:S(2)}) %collective-permute-start.25) | collective-permute-done | bytes 544 | tf_op jit(solution)/shard_map/ppermute | solution.py:408
  73.5 0.5 fusion.1
  (14 shorter events, 0.2 us)
Async XLA Ops:
  1.6 8.9 %collective-permute-start.2 = (f32[1,8,128]{2,1,0:T(8,128)S(1)}, f32[1,8,128]{2,1,0:T(8,128)S(1)}, u32[]{:S(2)}, u32[]{:S(2)}) collective-permute-start(f32[1,8,128]{2,1,0:T(8,128)S(1)} %get-tuple-element.14), channel_id=1, source_target_pairs={{0,64},{64,0},{128,192},{192,128},{1,65},{65,1},{129,193},{193,129... | collective-permute-start | bytes 12296 | tf_op jit(solution)/shard_map/ppermute | solution.py:354
  3.8 7.9 %collective-permute-start = (bf16[2,80,128]{2,1,0:T(8,128)(2,1)S(1)}, bf16[2,80,128]{2,1,0:T(8,128)(2,1)S(1)}, u32[]{:S(2)}, u32[]{:S(2)}) collective-permute-start(bf16[2,80,128]{2,1,0:T(8,128)(2,1)S(1)} %get-tuple-element.13), channel_id=1, source_target_pairs={{16,0},{24,8},{0,16},{8,24},{48,32},{56,40},{32,48},{40,56},{41,1}... | collective-permute-start | bytes 122888 | tf_op jit(solution)/shard_map/ppermute | solution.py:351
  10.3 5.0 %collective-permute-start.1 = (bf16[2,80,128]{2,1,0:T(8,128)(2,1)S(1)}, bf16[2,80,128]{2,1,0:T(8,128)(2,1)S(1)}, u32[]{:S(2)}, u32[]{:S(2)}) collective-permute-start(bf16[2,80,128]{2,1,0:T(8,128)(2,1)S(1)} %get-tuple-element.13), channel_id=1, source_target_pairs={{8,0},{0,8},{24,16},{16,24},{40,32},{32,40},{56,48},{48,56},{49,1}... | collective-permute-start | bytes 122888 | tf_op jit(solution)/shard_map/ppermute | solution.py:353
  15.3 3.7 %collective-permute-start.6 = (bf16[4,80,128]{2,1,0:T(8,128)(2,1)S(1)}, bf16[4,80,128]{2,1,0:T(8,128)(2,1)S(1)}, u32[]{:S(2)}, u32[]{:S(2)}) collective-permute-start(bf16[4,80,128]{2,1,0:T(8,128)(2,1)S(1)} %maximum_select_fusion.refs_0_), channel_id=1, source_target_pairs={{0,8},{8,0},{16,24},{24,16},{32,40},{40,32},{48,56},{56,48},{1,9},... | collective-permute-start | bytes 245768 | tf_op jit(solution)/shard_map/ppermute | solution.py:357
  16.1 5.4 %collective-permute-start.4 = (bf16[4,80,128]{2,1,0:T(8,128)(2,1)S(1)}, bf16[4,80,128]{2,1,0:T(8,128)(2,1)S(1)}, u32[]{:S(2)}, u32[]{:S(2)}) collective-permute-start(bf16[4,80,128]{2,1,0:T(8,128)(2,1)S(1)} %maximum_select_fusion.refs_0_), channel_id=1, source_target_pairs={{0,6},{2,4},{4,2},{6,0},{1,7},{3,5},{5,3},{7,1},{8,14},{10,12},{12... | collective-permute-start | bytes 245768 | tf_op jit(solution)/shard_map/ppermute | solution.py:358
  18.5 3.6 %collective-permute-start.9 = (bf16[4,80,128]{2,1,0:T(8,128)(2,1)S(1)}, bf16[4,80,128]{2,1,0:T(8,128)(2,1)S(1)}, u32[]{:S(2)}, u32[]{:S(2)}) collective-permute-start(bf16[4,80,128]{2,1,0:T(8,128)(2,1)S(1)} %maximum_select_fusion.refs_0_), channel_id=1, source_target_pairs={{0,2},{2,0},{4,6},{6,4},{1,3},{3,1},{5,7},{7,5},{8,10},{10,8},{12,... | collective-permute-start | bytes 245768 | tf_op jit(solution)/shard_map/ppermute | solution.py:359
  18.9 4.5 %collective-permute-start.7 = (bf16[4,80,128]{2,1,0:T(8,128)(2,1)S(1)}, bf16[4,80,128]{2,1,0:T(8,128)(2,1)S(1)}, u32[]{:S(2)}, u32[]{:S(2)}) collective-permute-start(bf16[4,80,128]{2,1,0:T(8,128)(2,1)S(1)} %collective-permute-done.6.refs_1_), channel_id=1, source_target_pairs={{0,6},{2,4},{4,2},{6,0},{1,7},{3,5},{5,3},{7,1},{8,14},{10,12},{12... | collective-permute-start | bytes 245768 | tf_op jit(solution)/shard_map/ppermute | solution.py:363
  21.4 3.3 %collective-permute-start.10 = (bf16[4,80,128]{2,1,0:T(8,128)(2,1)S(1)}, bf16[4,80,128]{2,1,0:T(8,128)(2,1)S(1)}, u32[]{:S(2)}, u32[]{:S(2)}) collective-permute-start(bf16[4,80,128]{2,1,0:T(8,128)(2,1)S(1)} %collective-permute-done.6.refs_1_), channel_id=1, source_target_pairs={{0,2},{2,0},{4,6},{6,4},{1,3},{3,1},{5,7},{7,5},{8,10},{10,8},{12,... | collective-permute-start | bytes 245768 | tf_op jit(solution)/shard_map/ppermute | solution.py:364
  24.8 8.4 %collective-permute-start.11 = (bf16[16,80,128]{2,1,0:T(8,128)(2,1)S(1)}, bf16[16,80,128]{2,1,0:T(8,128)(2,1)S(1)}, u32[]{:S(2)}, u32[]{:S(2)}) collective-permute-start(bf16[16,80,128]{2,1,0:T(8,128)(2,1)S(1)} %pad_maximum_fusion), channel_id=1, source_target_pairs={{0,1},{1,0},{2,3},{3,2},{4,5},{5,4},{6,7},{7,6},{8,9},{9,8},{10,11... | collective-permute-start | bytes 983048 | tf_op jit(solution)/shard_map/ppermute | solution.py:371
  24.9 6.2 %collective-permute-start.12 = (bf16[8,80,128]{2,1,0:T(8,128)(2,1)S(1)}, bf16[8,80,128]{2,1,0:T(8,128)(2,1)S(1)}, u32[]{:S(2)}, u32[]{:S(2)}) collective-permute-start(bf16[8,80,128]{2,1,0:T(8,128)(2,1)S(1)} %pad_maximum_fusion.1), channel_id=1, source_target_pairs={{0,1},{1,0},{2,3},{3,2},{4,5},{5,4},{6,7},{7,6},{8,9},{9,8},{10,11... | collective-permute-start | bytes 491528 | tf_op jit(solution)/shard_map/ppermute | solution.py:365
  25.5 9.8 %collective-permute-start.5 = (bf16[4,80,128]{2,1,0:T(8,128)(2,1)S(1)}, bf16[4,80,128]{2,1,0:T(8,128)(2,1)S(1)}, u32[]{:S(2)}, u32[]{:S(2)}) collective-permute-start(bf16[4,80,128]{2,1,0:T(8,128)(2,1)S(1)} %collective-permute-done.4.refs_0_), channel_id=1, source_target_pairs={{0,2},{2,0},{4,6},{6,4},{1,3},{3,1},{5,7},{7,5},{8,10},{10,8},{12,... | collective-permute-start | bytes 245768 | tf_op jit(solution)/shard_map/ppermute | solution.py:366
  25.5 9.8 %collective-permute-start.8 = (bf16[4,80,128]{2,1,0:T(8,128)(2,1)S(1)}, bf16[4,80,128]{2,1,0:T(8,128)(2,1)S(1)}, u32[]{:S(2)}, u32[]{:S(2)}) collective-permute-start(bf16[4,80,128]{2,1,0:T(8,128)(2,1)S(1)} %collective-permute-done.7.refs_1_), channel_id=1, source_target_pairs={{0,2},{2,0},{4,6},{6,4},{1,3},{3,1},{5,7},{7,5},{8,10},{10,8},{12,... | collective-permute-start | bytes 245768 | tf_op jit(solution)/shard_map/ppermute | solution.py:370
  26.9 3.7 %collective-permute-start.3 = (f32[2,8,128]{2,1,0:T(8,128)S(1)}, f32[2,8,128]{2,1,0:T(8,128)S(1)}, u32[]{:S(2)}, u32[]{:S(2)}) collective-permute-start(f32[2,8,128]{2,1,0:T(8,128)S(1)} %pad_maximum_fusion.2.sites_ref), channel_id=1, source_target_pairs={{0,192},{64,128},{128,64},{192,0},{1,193},{65,129},{129,65},{193,1... | collective-permute-start | bytes 24584 | tf_op jit(solution)/shard_map/ppermute | solution.py:360
  35.3 4.2 %collective-permute-start.13 = (bf16[8,80,128]{2,1,0:T(8,128)(2,1)S(1)}, bf16[8,80,128]{2,1,0:T(8,128)(2,1)S(1)}, u32[]{:S(2)}, u32[]{:S(2)}) collective-permute-start(bf16[8,80,128]{2,1,0:T(8,128)(2,1)S(1)} %constant_dynamic-update-slice_fusion.refs_0_), channel_id=1, source_target_pairs={{0,1},{1,0},{2,3},{3,2},{4,5},{5,4},{6,7},{7,6},{8,9},{9,8},{10,11... | collective-permute-start | bytes 491528 | tf_op jit(solution)/shard_map/ppermute | solution.py:377
  40.9 6.0 %collective-permute-start.14 = (f32[4,56,128]{2,1,0:T(8,128)S(1)}, f32[4,56,128]{2,1,0:T(8,128)S(1)}, u32[]{:S(2)}, u32[]{:S(2)}) collective-permute-start(f32[4,56,128]{2,1,0:T(8,128)S(1)} %bitcast.10), channel_id=1, source_target_pairs={{0,192},{64,128},{128,64},{192,0},{1,193},{65,129},{129,65},{193,1... | collective-permute-start | bytes 344072 | tf_op jit(solution)/shard_map/ppermute | solution.py:392
  44.1 3.8 %collective-permute-start.16 = (f32[4,40,128]{2,1,0:T(8,128)S(1)}, f32[4,40,128]{2,1,0:T(8,128)S(1)}, u32[]{:S(2)}, u32[]{:S(2)}) collective-permute-start(f32[4,40,128]{2,1,0:T(8,128)S(1)} %bitcast.12), channel_id=1, source_target_pairs={{0,64},{64,0},{128,192},{192,128},{1,65},{65,1},{129,193},{193,129... | collective-permute-start | bytes 245768 | tf_op jit(solution)/shard_map/ppermute | solution.py:393
  46.9 5.6 %collective-permute-start.15 = (f32[4,56,128]{2,1,0:T(8,128)S(1)}, f32[4,56,128]{2,1,0:T(8,128)S(1)}, u32[]{:S(2)}, u32[]{:S(2)}) collective-permute-start(f32[4,56,128]{2,1,0:T(8,128)S(1)} %exchange_add.2.low_ref), channel_id=1, source_target_pairs={{0,64},{64,0},{128,192},{192,128},{1,65},{65,1},{129,193},{193,129... | collective-permute-start | bytes 344072 | tf_op jit(solution)/shard_map/ppermute | solution.py:394
  47.9 4.6 %collective-permute-start.17 = (f32[4,40,128]{2,1,0:T(8,128)S(1)}, f32[4,40,128]{2,1,0:T(8,128)S(1)}, u32[]{:S(2)}, u32[]{:S(2)}) collective-permute-start(f32[4,40,128]{2,1,0:T(8,128)S(1)} %exchange_add.3.high_ref), channel_id=1, source_target_pairs={{0,192},{64,128},{128,64},{192,0},{1,193},{65,129},{129,65},{193,1... | collective-permute-start | bytes 245768 | tf_op jit(solution)/shard_map/ppermute | solution.py:395
  53.1 3.1 %collective-permute-start.18 = (f32[1,128]{1,0:T(1,128)S(1)}, f32[1,128]{1,0:T(1,128)S(1)}, u32[]{:S(2)}, u32[]{:S(2)}) collective-permute-start(f32[1,128]{1,0:T(1,128)S(1)} %get-tuple-element.23), channel_id=1, source_target_pairs={{0,1},{1,0},{2,3},{3,2},{4,5},{5,4},{6,7},{7,6},{8,9},{9,8},{10,11... | collective-permute-start | bytes 1544 | tf_op jit(solution)/shard_map/ppermute | solution.py:397
  56.3 3.9 %collective-permute-start.19 = (f32[1,128]{1,0:T(1,128)S(1)}, f32[1,128]{1,0:T(1,128)S(1)}, u32[]{:S(2)}, u32[]{:S(2)}) collective-permute-start(f32[1,128]{1,0:T(1,128)S(1)} %add.18), channel_id=1, source_target_pairs={{2,0},{0,2},{6,4},{4,6},{5,1},{7,3},{1,5},{3,7},{10,8},{8,10},{14,... | collective-permute-start | bytes 1544 | tf_op jit(solution)/shard_map/ppermute | solution.py:399
  57.0 3.6 %collective-permute-start.20 = (f32[1,128]{1,0:T(1,128)S(1)}, f32[1,128]{1,0:T(1,128)S(1)}, u32[]{:S(2)}, u32[]{:S(2)}) collective-permute-start(f32[1,128]{1,0:T(1,128)S(1)} %add.18), channel_id=1, source_target_pairs={{2,0},{0,2},{6,4},{4,6},{7,1},{5,3},{3,5},{1,7},{10,8},{8,10},{14,... | collective-permute-start | bytes 1544 | tf_op jit(solution)/shard_map/ppermute | solution.py:401
  60.7 1.2 %collective-permute-start.21 = (f32[1,128]{1,0:T(1,128)S(1)}, f32[1,128]{1,0:T(1,128)S(1)}, u32[]{:S(2)}, u32[]{:S(2)}) collective-permute-start(f32[1,128]{1,0:T(1,128)S(1)} %fusion.2), channel_id=1, source_target_pairs={{0,1},{1,0},{2,3},{3,2},{4,5},{5,4},{6,7},{7,6},{8,9},{9,8},{10,11... | collective-permute-start | bytes 1544 | tf_op jit(solution)/shard_map/ppermute | solution.py:403
  61.8 2.4 %collective-permute-start.22 = (f32[1,128]{1,0:T(1,128)S(1)}, f32[1,128]{1,0:T(1,128)S(1)}, u32[]{:S(2)}, u32[]{:S(2)}) collective-permute-start(f32[1,128]{1,0:T(1,128)S(1)} %add.20), channel_id=1, source_target_pairs={{1,9},{9,1},{17,25},{25,17},{33,41},{41,33},{49,57},{57,49},{0,8},... | collective-permute-start | bytes 1544 | tf_op jit(solution)/shard_map/ppermute | solution.py:407
  64.3 3.3 %collective-permute-start.23 = (f32[1,128]{1,0:T(1,128)S(1)}, f32[1,128]{1,0:T(1,128)S(1)}, u32[]{:S(2)}, u32[]{:S(2)}) collective-permute-start(f32[1,128]{1,0:T(1,128)S(1)} %add.21), channel_id=1, source_target_pairs={{1,17},{9,25},{17,1},{25,9},{33,49},{41,57},{49,33},{57,41},{0,8},... | collective-permute-start | bytes 1544 | tf_op jit(solution)/shard_map/ppermute | solution.py:407
  67.6 3.6 %collective-permute-start.24 = (f32[1,128]{1,0:T(1,128)S(1)}, f32[1,128]{1,0:T(1,128)S(1)}, u32[]{:S(2)}, u32[]{:S(2)}) collective-permute-start(f32[1,128]{1,0:T(1,128)S(1)} %add.22), channel_id=1, source_target_pairs={{1,57},{9,49},{17,41},{25,33},{33,25},{41,17},{49,9},{57,1},{0,8},... | collective-permute-start | bytes 1544 | tf_op jit(solution)/shard_map/ppermute | solution.py:407
  71.2 2.3 %collective-permute-start.25 = (f32[1,128]{1,0:T(1,128)S(1)}, f32[1,128]{1,0:T(1,128)S(1)}, u32[]{:S(2)}, u32[]{:S(2)}) collective-permute-start(f32[1,128]{1,0:T(1,128)S(1)} %add.23), channel_id=1, source_target_pairs={{0,1},{1,0},{2,3},{3,2},{4,5},{5,4},{6,7},{7,6},{8,9},{9,8},{10,11... | collective-permute-start | bytes 1544 | tf_op jit(solution)/shard_map/ppermute | solution.py:408

commit v6 on v5

--- a/solution.py
+++ b/solution.py
@@ -22,7 +22,7 @@
 FRAME_STRIDE = 40
 NEAR_ORDER = (1, 0, 3, 2)
 FAR_ORDER = (2, 3, 0, 1)
-FIRST_SHARE = 7
+FIRST_SHARE = 8
 
 
 def shares(width):
@@ -275,35 +275,34 @@
     )(*[in_vmem(array) for array in arrays])
 
 
-def residual_kernel(pix_ref, low_ref, low_got_ref, high_ref, high_got_ref, res_ref, sum_ref):
+def residuals(block, pix_ref, low_ref, low_got_ref, high_ref, high_got_ref):
     width = low_ref.shape[1] + high_ref.shape[1]
     parts = (low_ref, low_got_ref, NEAR_ORDER), (high_ref, high_got_ref, FAR_ORDER)
+    for (start, size, offset), (mine, got, order) in zip(shares(width), parts):
+        value = mine[block] + got[order[block]]
+        here = slice(offset + block * size, offset + (block + 1) * size)
+        yield start, size, (value - pix_ref[5, here, :]) * pix_ref[6, here, :]
+
+
+def square_sum_kernel(*refs):
     sums = []
     for block in range(4):
         total = jnp.zeros((1, LANES), jnp.float32)
-        for (start, size, offset), (mine, got, order) in zip(shares(width), parts):
-            value = mine[block] + got[order[block]]
-            here = slice(offset + block * size, offset + (block + 1) * size)
-            res = (value - pix_ref[5, here, :]) * pix_ref[6, here, :]
-            if block == 0:
-                res_ref[start : start + size, :] = res
+        for _, _, res in residuals(block, *refs[:-1]):
             total = total + jnp.sum(res * res, axis=0, keepdims=True)
         sums.append(total)
-    sum_ref[...] = (sums[0] + sums[1]) + (sums[2] + sums[3])
-
-
-def residual_part(pix, low, low_got, high, high_got):
+    refs[-1][...] = (sums[0] + sums[1]) + (sums[2] + sums[3])
+
+
+def own_residual_kernel(*refs):
+    for start, size, res in residuals(0, *refs[:-1]):
+        refs[-1][start : start + size, :] = res
+
+
+def on_sums(kernel, shape, arrays):
     return pl.pallas_call(
-        residual_kernel,
-        out_shape=(
-            jax.ShapeDtypeStruct((low.shape[1] + high.shape[1], LANES), jnp.float32),
-            vmem_array((1, LANES), jnp.float32),
-        ),
-        in_specs=[VMEM_SPEC] * 5,
-        out_specs=(VMEM_SPEC, VMEM_SPEC),
-        compiler_params=LIMITS,
-        name="residual_part",
-    )(*[in_vmem(array) for array in (pix, low, low_got, high, high_got)])
+        kernel, out_shape=shape, in_specs=[VMEM_SPEC] * len(arrays), out_specs=VMEM_SPEC, compiler_params=LIMITS
+    )(*[in_vmem(array) for array in arrays])
 
 
 def exchange_add_kernel(order, mine_ref, got_ref, out_ref):
@@ -393,7 +392,10 @@
     high = exchange_add(high, lax.ppermute(high, "y", near_pairs), NEAR_ORDER)
     low_got = lax.ppermute(low, "y", near_pairs)
     high_got = lax.ppermute(high, "y", far_pairs)
-    residual, own_sum = residual_part(pix, low, low_got, high, high_got)
+    sums = pix, low, low_got, high, high_got
+    own_sum = on_sums(square_sum_kernel, vmem_array((1, LANES), jnp.float32), sums)
+    shape = jax.ShapeDtypeStruct((own_pixels, LANES), jnp.float32)
+    residual = on_sums(own_residual_kernel, shape, sums)
     total = own_sum + lax.ppermute(own_sum, "pix", swap)
     meets = [(2 * (i ^ 1), 2 * i) for i in range(4)] + [(2 * (i ^ 2) + 1, 2 * i + 1) for i in range(4)]
     first = lax.ppermute(total, ("x", "pix"), meets)

time: 74.2 us -> 73.1 us (0.985)
  waiting for transfers between devices: 26.6 us -> 24.8 us
  starting transfers between devices: 34.7 us -> 35.5 us
    ppermute x1, waiting for transfers between devices: 3.44 us -> 2.52 us  [per_device(): high_got = lax.ppermute(high, 'y', far_pairs)]
  transfers between devices with their start and end apart: 26 -> 26, of which waited for: 18 -> 18; matrix products, arithmetic and copies ran while one was open for 0% -> 0% of each run, Pallas kernels for 11% -> 12%
where the time goes in v6:
time: 73.1 us; the launch traced here: 73 us
  starting transfers between devices  35.5 us (49%)
  waiting for transfers between devices  24.8 us (34%)
  Pallas kernels  11.3 us (15%)
  between operations  0.8 us (1%)
    pallas_call x5, Pallas kernels, unit_product(): pl.pallas_call(functools.partial(unit_kernel, units, len(parts), acc is n...  8.73 us
    ppermute x1, starting transfers between devices, per_device(): first = lax.ppermute(piece, ('z', 'pix'), meets)  6.46 us
    ppermute x3, waiting for transfers between devices, per_device(): total = total + lax.ppermute(total, ('z', 'pix'), meets)  5.05 us
    ppermute x3, starting transfers between devices, per_device(): total = total + lax.ppermute(total, ('z', 'pix'), meets)  4.32 us
    ppermute x1, waiting for transfers between devices, per_device(): second = lax.ppermute(piece, ('z', 'pix'), meets)  3.6 us
    ppermute x1, waiting for transfers between devices, per_device(): low = exchange_add(low, lax.ppermute(low, 'y', far_pairs), FAR_ORDER)  3.17 us
    ppermute x1, waiting for transfers between devices, per_device(): high_got = lax.ppermute(high, 'y', far_pairs)  2.52 us
    ppermute x1, starting transfers between devices, per_device(): far_a = lax.ppermute(four, 'x', far_pairs)  2.48 us
  transfers between devices with their start and end apart: 26, of which 18 were waited for; matrix products, arithmetic and copies ran while one was open for 0% of the time, Pallas kernels for 12%

profile of v6, /device:TPU:1, one launch (start us, length us, event | category | flops | bytes accessed | tf_op | source)
XLA Modules:
  0.0 73.0 jit_solution(15757617098626716980)
XLA Ops:
  0.6 1.0 %prepare.1 = (bf16[2,80,128]{2,1,0:T(8,128)(2,1)S(1)}, f32[1,8,128]{2,1,0:T(8,128)S(1)}) custom-call(f32[16]{0:T(128)} %strike_ref.1, f32[16]{0:T(128)} %dip_ref.1, f32[2,48]{1,0:T(2,128)} %pos_ref.1, f32[1,48]{1,0:T(1,128)} %bitcast.15, s32[1,48]{1,0:T(1,128)} %bitcast.16, bf16[3,48,128]{2,1,0:T(8,128)(2,1)} %bitcast.14, f32[2,96]{1,0:T(2,128)} %pixel_ref.1, ...), custom_call_target="tpu_custom_call" | custom-call | tf_op jit(solution)/shard_map/prepare/pallas_call | solution.py:125
  1.6 2.2 %collective-permute-start.2 = (f32[1,8,128]{2,1,0:T(8,128)S(1)}, f32[1,8,128]{2,1,0:T(8,128)S(1)}, u32[]{:S(2)}, u32[]{:S(2)}) collective-permute-start(f32[1,8,128]{2,1,0:T(8,128)S(1)} %get-tuple-element.12), channel_id=1, source_target_pairs={{0,64},{64,0},{128,192},{192,128},{1,65},{65,1},{129,193},{193,129... | collective-permute-start | bytes 12296 | tf_op jit(solution)/shard_map/ppermute | solution.py:353
  3.8 6.5 %collective-permute-start = (bf16[2,80,128]{2,1,0:T(8,128)(2,1)S(1)}, bf16[2,80,128]{2,1,0:T(8,128)(2,1)S(1)}, u32[]{:S(2)}, u32[]{:S(2)}) collective-permute-start(bf16[2,80,128]{2,1,0:T(8,128)(2,1)S(1)} %get-tuple-element.11), channel_id=1, source_target_pairs={{16,0},{24,8},{0,16},{8,24},{48,32},{56,40},{32,48},{40,56},{41,1}... | collective-permute-start | bytes 122888 | tf_op jit(solution)/shard_map/ppermute | solution.py:350
  10.3 0.3 collective-permute-start.1
  10.5 0.0 collective-permute-done.2
  10.6 1.1 %collective-permute-done = bf16[2,80,128]{2,1,0:T(8,128)(2,1)S(1)} collective-permute-done((bf16[2,80,128]{2,1,0:T(8,128)(2,1)S(1)}, bf16[2,80,128]{2,1,0:T(8,128)(2,1)S(1)}, u32[]{:S(2)}, u32[]{:S(2)}) %collective-permute-start) | collective-permute-done | bytes 40992 | tf_op jit(solution)/shard_map/ppermute | solution.py:350
  11.7 3.6 %collective-permute-done.1 = bf16[2,80,128]{2,1,0:T(8,128)(2,1)S(1)} collective-permute-done((bf16[2,80,128]{2,1,0:T(8,128)(2,1)S(1)}, bf16[2,80,128]{2,1,0:T(8,128)(2,1)S(1)}, u32[]{:S(2)}, u32[]{:S(2)}) %collective-permute-start.1) | collective-permute-done | bytes 40992 | tf_op jit(solution)/shard_map/ppermute | solution.py:352
  15.3 0.8 %collective-permute-start.6 = (bf16[4,80,128]{2,1,0:T(8,128)(2,1)S(1)}, bf16[4,80,128]{2,1,0:T(8,128)(2,1)S(1)}, u32[]{:S(2)}, u32[]{:S(2)}) collective-permute-start(bf16[4,80,128]{2,1,0:T(8,128)(2,1)S(1)} %maximum_select_fusion.refs_0_), channel_id=1, source_target_pairs={{0,8},{8,0},{16,24},{24,16},{32,40},{40,32},{48,56},{56,48},{1,9},... | collective-permute-start | bytes 245768 | tf_op jit(solution)/shard_map/ppermute | solution.py:356
  16.1 2.5 %collective-permute-start.4 = (bf16[4,80,128]{2,1,0:T(8,128)(2,1)S(1)}, bf16[4,80,128]{2,1,0:T(8,128)(2,1)S(1)}, u32[]{:S(2)}, u32[]{:S(2)}) collective-permute-start(bf16[4,80,128]{2,1,0:T(8,128)(2,1)S(1)} %maximum_select_fusion.refs_0_), channel_id=1, source_target_pairs={{0,6},{2,4},{4,2},{6,0},{1,7},{3,5},{5,3},{7,1},{8,14},{10,12},{12... | collective-permute-start | bytes 245768 | tf_op jit(solution)/shard_map/ppermute | solution.py:357
  18.5 0.0 collective-permute-start.9
  18.5 0.4 collective-permute-done.6.refs_1_
  18.9 2.5 %collective-permute-start.7 = (bf16[4,80,128]{2,1,0:T(8,128)(2,1)S(1)}, bf16[4,80,128]{2,1,0:T(8,128)(2,1)S(1)}, u32[]{:S(2)}, u32[]{:S(2)}) collective-permute-start(bf16[4,80,128]{2,1,0:T(8,128)(2,1)S(1)} %collective-permute-done.6.refs_1_), channel_id=1, source_target_pairs={{0,6},{2,4},{4,2},{6,0},{1,7},{3,5},{5,3},{7,1},{8,14},{10,12},{12... | collective-permute-start | bytes 245768 | tf_op jit(solution)/shard_map/ppermute | solution.py:362
  21.4 0.0 collective-permute-start.10
  21.4 0.0 collective-permute-done.4.refs_0_
  21.4 0.7 collective-permute-done.9.refs_0_
  22.1 1.3 %collective-permute-done.7.refs_1_ = bf16[4,80,128]{2,1,0:T(8,128)(2,1)S(1)} collective-permute-done((bf16[4,80,128]{2,1,0:T(8,128)(2,1)S(1)}, bf16[4,80,128]{2,1,0:T(8,128)(2,1)S(1)}, u32[]{:S(2)}, u32[]{:S(2)}) %collective-permute-start.7) | collective-permute-done | bytes 81952 | tf_op jit(solution)/shard_map/ppermute | solution.py:362
  23.5 1.3 %collective-permute-done.10.refs_1_ = bf16[4,80,128]{2,1,0:T(8,128)(2,1)S(1)} collective-permute-done((bf16[4,80,128]{2,1,0:T(8,128)(2,1)S(1)}, bf16[4,80,128]{2,1,0:T(8,128)(2,1)S(1)}, u32[]{:S(2)}, u32[]{:S(2)}) %collective-permute-start.10) | collective-permute-done | bytes 81952 | tf_op jit(solution)/shard_map/ppermute | solution.py:363
  24.8 0.1 collective-permute-start.11
  24.9 0.6 collective-permute-start.12
  25.5 0.0 collective-permute-start.5
  25.5 1.5 %collective-permute-start.8 = (bf16[4,80,128]{2,1,0:T(8,128)(2,1)S(1)}, bf16[4,80,128]{2,1,0:T(8,128)(2,1)S(1)}, u32[]{:S(2)}, u32[]{:S(2)}) collective-permute-start(bf16[4,80,128]{2,1,0:T(8,128)(2,1)S(1)} %collective-permute-done.7.refs_1_), channel_id=1, source_target_pairs={{0,2},{2,0},{4,6},{6,4},{1,3},{3,1},{5,7},{7,5},{8,10},{10,8},{12,... | collective-permute-start | bytes 245768 | tf_op jit(solution)/shard_map/ppermute | solution.py:369
  26.9 1.9 %collective-permute-start.3 = (f32[2,8,128]{2,1,0:T(8,128)S(1)}, f32[2,8,128]{2,1,0:T(8,128)S(1)}, u32[]{:S(2)}, u32[]{:S(2)}) collective-permute-start(f32[2,8,128]{2,1,0:T(8,128)S(1)} %pad_maximum_fusion.2.sites_ref), channel_id=1, source_target_pairs={{0,192},{64,128},{128,64},{192,0},{1,193},{65,129},{129,65},{193,1... | collective-permute-start | bytes 24584 | tf_op jit(solution)/shard_map/ppermute | solution.py:359
  28.8 0.5 pixel_columns.2.refs_0_
  29.3 1.4 %collective-permute-done.3.sites_ref = f32[2,8,128]{2,1,0:T(8,128)S(1)} collective-permute-done((f32[2,8,128]{2,1,0:T(8,128)S(1)}, f32[2,8,128]{2,1,0:T(8,128)S(1)}, u32[]{:S(2)}, u32[]{:S(2)}) %collective-permute-start.3) | collective-permute-done | bytes 8224 | tf_op jit(solution)/shard_map/ppermute | solution.py:359
  30.7 0.5 pixel_columns.3.pix_ref.refs_0_
  31.1 0.0 collective-permute-done.12.refs_2_
  31.1 2.1 %unit_product.5.refs_3_ = f32[384,128]{1,0:T(8,128)S(1)} custom-call(f32[7,384,128]{2,1,0:T(8,128)S(1)} %pixel_columns.3.pix_ref.refs_0_, bf16[4,80,128]{2,1,0:T(8,128)(2,1)S(1)} %maximum_select_fusion.refs_0_, bf16[4,80,128]{2,1,0:T(8,128)(2,1)S(1)} %collective-permute-done.6.refs_1_, bf16[8,80,128]{2,1,0:T(8,128)(2,1)S(1)} %collective-permute-done.12.refs_2_), custom_call_target="tpu_custom_call" | custom-call | flops 147456000 | bytes 524288 | tf_op jit(solution)/shard_map/unit_product/pallas_call | solution.py:266
  33.2 0.0 collective-permute-done.11.refs_2_
  33.2 2.1 %unit_product.6.refs_3_ = f32[384,128]{1,0:T(8,128)S(1)} custom-call(f32[7,384,128]{2,1,0:T(8,128)S(1)} %pixel_columns.3.pix_ref.refs_0_, bf16[4,80,128]{2,1,0:T(8,128)(2,1)S(1)} %collective-permute-done.9.refs_0_, bf16[4,80,128]{2,1,0:T(8,128)(2,1)S(1)} %collective-permute-done.10.refs_1_, bf16[16,80,128]{2,1,0:T(8,128)(2,1)S(1)} %collective-permute-done.11.refs_2_, ...), custom_call_target="tpu_custom_call" | custom-call | flops 147456000 | bytes 524288 | tf_op jit(solution)/shard_map/unit_product/pallas_call | solution.py:266
  35.3 0.0 collective-permute-done.5
  35.3 0.0 collective-permute-done.8
  35.3 2.1 %collective-permute-start.13 = (bf16[8,80,128]{2,1,0:T(8,128)(2,1)S(1)}, bf16[8,80,128]{2,1,0:T(8,128)(2,1)S(1)}, u32[]{:S(2)}, u32[]{:S(2)}) collective-permute-start(bf16[8,80,128]{2,1,0:T(8,128)(2,1)S(1)} %constant_dynamic-update-slice_fusion.refs_0_), channel_id=1, source_target_pairs={{0,1},{1,0},{2,3},{3,2},{4,5},{5,4},{6,7},{7,6},{8,9},{9,8},{10,11... | collective-permute-start | bytes 491528 | tf_op jit(solution)/shard_map/ppermute | solution.py:376
  37.4 2.1 %unit_product.7.refs_2_ = f32[384,128]{1,0:T(8,128)S(1)} custom-call(f32[7,384,128]{2,1,0:T(8,128)S(1)} %pixel_columns.3.pix_ref.refs_0_, bf16[4,80,128]{2,1,0:T(8,128)(2,1)S(1)} %collective-permute-done.4.refs_0_, bf16[4,80,128]{2,1,0:T(8,128)(2,1)S(1)} %collective-permute-done.7.refs_1_, bf16[16,80,128]{2,1,0:T(8,128)(2,1)S(1)} %collective-permute-done.11.refs_2_, ...), custom_call_target="tpu_custom_call" | custom-call | flops 147456000 | bytes 524288 | tf_op jit(solution)/shard_map/unit_product/pallas_call | solution.py:266
  39.5 0.0 collective-permute-done.13.refs_1_
  39.5 1.5 %unit_product.8 = f32[256,128]{1,0:T(8,128)S(1)} custom-call(f32[7,384,128]{2,1,0:T(8,128)S(1)} %pixel_columns.3.pix_ref.refs_0_, bf16[8,80,128]{2,1,0:T(8,128)(2,1)S(1)} %constant_dynamic-update-slice_fusion.refs_0_, bf16[8,80,128]{2,1,0:T(8,128)(2,1)S(1)} %collective-permute-done.13.refs_1_, f32[384,128]{1,0:T(8,128)S(1)} %unit_product.7.refs_2_), custom_call_target="tpu_custom_call" | custom-call | flops 98304000 | bytes 524288 | tf_op jit(solution)/shard_map/unit_product/pallas_call | solution.py:266
  41.0 2.0 %collective-permute-start.14 = (f32[4,64,128]{2,1,0:T(8,128)S(1)}, f32[4,64,128]{2,1,0:T(8,128)S(1)}, u32[]{:S(2)}, u32[]{:S(2)}) collective-permute-start(f32[4,64,128]{2,1,0:T(8,128)S(1)} %bitcast.10), channel_id=1, source_target_pairs={{0,192},{64,128},{128,64},{192,0},{1,193},{65,129},{129,65},{193,1... | collective-permute-start | bytes 393224 | tf_op jit(solution)/shard_map/ppermute | solution.py:391
  42.9 1.1 %unit_product.9 = f32[128,128]{1,0:T(8,128)S(1)} custom-call(f32[7,384,128]{2,1,0:T(8,128)S(1)} %pixel_columns.3.pix_ref.refs_0_, bf16[8,80,128]{2,1,0:T(8,128)(2,1)S(1)} %constant_dynamic-update-slice_fusion.refs_0_, bf16[8,80,128]{2,1,0:T(8,128)(2,1)S(1)} %collective-permute-done.13.refs_1_, f32[384,128]{1,0:T(8,128)S(1)} %unit_product.7.refs_2_), custom_call_target="tpu_custom_call" | custom-call | flops 49152000 | bytes 524288 | tf_op jit(solution)/shard_map/unit_product/pallas_call | solution.py:266
  44.0 0.1 collective-permute-start.16
  44.1 3.2 %collective-permute-done.14.got_ref = f32[4,64,128]{2,1,0:T(8,128)S(1)} collective-permute-done((f32[4,64,128]{2,1,0:T(8,128)S(1)}, f32[4,64,128]{2,1,0:T(8,128)S(1)}, u32[]{:S(2)}, u32[]{:S(2)}) %collective-permute-start.14) | collective-permute-done | bytes 131104 | tf_op jit(solution)/shard_map/ppermute | solution.py:391
  47.3 0.1 collective-permute-start.15
  47.4 0.1 collective-permute-done.16.got_ref
  47.5 1.9 %collective-permute-start.17 = (f32[4,32,128]{2,1,0:T(8,128)S(1)}, f32[4,32,128]{2,1,0:T(8,128)S(1)}, u32[]{:S(2)}, u32[]{:S(2)}) collective-permute-start(f32[4,32,128]{2,1,0:T(8,128)S(1)} %exchange_add.3.refs_3_), channel_id=1, source_target_pairs={{0,192},{64,128},{128,64},{192,0},{1,193},{65,129},{129,65},{193,1... | collective-permute-start | bytes 196616 | tf_op jit(solution)/shard_map/ppermute | solution.py:394
  49.4 2.5 %collective-permute-done.17.refs_4_ = f32[4,32,128]{2,1,0:T(8,128)S(1)} collective-permute-done((f32[4,32,128]{2,1,0:T(8,128)S(1)}, f32[4,32,128]{2,1,0:T(8,128)S(1)}, u32[]{:S(2)}, u32[]{:S(2)}) %collective-permute-start.17) | collective-permute-done | bytes 65568 | tf_op jit(solution)/shard_map/ppermute | solution.py:394
  51.9 0.0 collective-permute-done.15.refs_2_
  51.9 0.1 shard_map.123
  52.0 2.4 %collective-permute-start.18 = (f32[1,128]{1,0:T(1,128)S(1)}, f32[1,128]{1,0:T(1,128)S(1)}, u32[]{:S(2)}, u32[]{:S(2)}) collective-permute-start(f32[1,128]{1,0:T(1,128)S(1)} %shard_map.123), channel_id=1, source_target_pairs={{0,1},{1,0},{2,3},{3,2},{4,5},{5,4},{6,7},{7,6},{8,9},{9,8},{10,11... | collective-permute-start | bytes 1544 | tf_op jit(solution)/shard_map/ppermute | solution.py:399
  54.4 0.8 %collective-permute-done.18 = f32[1,128]{1,0:T(1,128)S(1)} collective-permute-done((f32[1,128]{1,0:T(1,128)S(1)}, f32[1,128]{1,0:T(1,128)S(1)}, u32[]{:S(2)}, u32[]{:S(2)}) %collective-permute-start.18) | collective-permute-done | bytes 544 | tf_op jit(solution)/shard_map/ppermute | solution.py:399
  55.2 0.8 %collective-permute-start.19 = (f32[1,128]{1,0:T(1,128)S(1)}, f32[1,128]{1,0:T(1,128)S(1)}, u32[]{:S(2)}, u32[]{:S(2)}) collective-permute-start(f32[1,128]{1,0:T(1,128)S(1)} %add.18), channel_id=1, source_target_pairs={{2,0},{0,2},{6,4},{4,6},{5,1},{7,3},{1,5},{3,7},{10,8},{8,10},{14,... | collective-permute-start | bytes 1544 | tf_op jit(solution)/shard_map/ppermute | solution.py:401
  56.0 1.6 %collective-permute-start.20 = (f32[1,128]{1,0:T(1,128)S(1)}, f32[1,128]{1,0:T(1,128)S(1)}, u32[]{:S(2)}, u32[]{:S(2)}) collective-permute-start(f32[1,128]{1,0:T(1,128)S(1)} %add.18), channel_id=1, source_target_pairs={{2,0},{0,2},{6,4},{4,6},{7,1},{5,3},{3,5},{1,7},{10,8},{8,10},{14,... | collective-permute-start | bytes 1544 | tf_op jit(solution)/shard_map/ppermute | solution.py:403
  57.6 1.5 %collective-permute-done.19 = f32[1,128]{1,0:T(1,128)S(1)} collective-permute-done((f32[1,128]{1,0:T(1,128)S(1)}, f32[1,128]{1,0:T(1,128)S(1)}, u32[]{:S(2)}, u32[]{:S(2)}) %collective-permute-start.19) | collective-permute-done | bytes 544 | tf_op jit(solution)/shard_map/ppermute | solution.py:401
  59.1 0.5 collective-permute-done.20
  59.6 0.0 collective-permute-start.21
  59.6 1.2 %collective-permute-done.21 = f32[1,128]{1,0:T(1,128)S(1)} collective-permute-done((f32[1,128]{1,0:T(1,128)S(1)}, f32[1,128]{1,0:T(1,128)S(1)}, u32[]{:S(2)}, u32[]{:S(2)}) %collective-permute-start.21) | collective-permute-done | bytes 544 | tf_op jit(solution)/shard_map/ppermute | solution.py:405
  60.8 0.7 collective-permute-start.22
  61.5 1.7 %collective-permute-done.22 = f32[1,128]{1,0:T(1,128)S(1)} collective-permute-done((f32[1,128]{1,0:T(1,128)S(1)}, f32[1,128]{1,0:T(1,128)S(1)}, u32[]{:S(2)}, u32[]{:S(2)}) %collective-permute-start.22) | collective-permute-done | bytes 544 | tf_op jit(solution)/shard_map/ppermute | solution.py:409
  63.2 1.0 %collective-permute-start.23 = (f32[1,128]{1,0:T(1,128)S(1)}, f32[1,128]{1,0:T(1,128)S(1)}, u32[]{:S(2)}, u32[]{:S(2)}) collective-permute-start(f32[1,128]{1,0:T(1,128)S(1)} %add.21), channel_id=1, source_target_pairs={{1,17},{9,25},{17,1},{25,9},{33,49},{41,57},{49,33},{57,41},{0,8},... | collective-permute-start | bytes 1544 | tf_op jit(solution)/shard_map/ppermute | solution.py:409
  64.2 2.3 %collective-permute-done.23 = f32[1,128]{1,0:T(1,128)S(1)} collective-permute-done((f32[1,128]{1,0:T(1,128)S(1)}, f32[1,128]{1,0:T(1,128)S(1)}, u32[]{:S(2)}, u32[]{:S(2)}) %collective-permute-start.23) | collective-permute-done | bytes 544 | tf_op jit(solution)/shard_map/ppermute | solution.py:409
  66.5 2.6 %collective-permute-start.24 = (f32[1,128]{1,0:T(1,128)S(1)}, f32[1,128]{1,0:T(1,128)S(1)}, u32[]{:S(2)}, u32[]{:S(2)}) collective-permute-start(f32[1,128]{1,0:T(1,128)S(1)} %add.22), channel_id=1, source_target_pairs={{1,57},{9,49},{17,41},{25,33},{33,25},{41,17},{49,9},{57,1},{0,8},... | collective-permute-start | bytes 1544 | tf_op jit(solution)/shard_map/ppermute | solution.py:409
  69.1 1.1 %collective-permute-done.24 = f32[1,128]{1,0:T(1,128)S(1)} collective-permute-done((f32[1,128]{1,0:T(1,128)S(1)}, f32[1,128]{1,0:T(1,128)S(1)}, u32[]{:S(2)}, u32[]{:S(2)}) %collective-permute-start.24) | collective-permute-done | bytes 544 | tf_op jit(solution)/shard_map/ppermute | solution.py:409
  70.1 1.5 %collective-permute-start.25 = (f32[1,128]{1,0:T(1,128)S(1)}, f32[1,128]{1,0:T(1,128)S(1)}, u32[]{:S(2)}, u32[]{:S(2)}) collective-permute-start(f32[1,128]{1,0:T(1,128)S(1)} %add.23), channel_id=1, source_target_pairs={{0,1},{1,0},{2,3},{3,2},{4,5},{5,4},{6,7},{7,6},{8,9},{9,8},{10,11... | collective-permute-start | bytes 1544 | tf_op jit(solution)/shard_map/ppermute | solution.py:410
  71.7 0.6 shard_map.122
  72.3 0.2 collective-permute-done.25
  72.5 0.5 fusion.1
  (14 shorter events, 0.1 us)
Async XLA Ops:
  1.6 8.9 %collective-permute-start.2 = (f32[1,8,128]{2,1,0:T(8,128)S(1)}, f32[1,8,128]{2,1,0:T(8,128)S(1)}, u32[]{:S(2)}, u32[]{:S(2)}) collective-permute-start(f32[1,8,128]{2,1,0:T(8,128)S(1)} %get-tuple-element.12), channel_id=1, source_target_pairs={{0,64},{64,0},{128,192},{192,128},{1,65},{65,1},{129,193},{193,129... | collective-permute-start | bytes 12296 | tf_op jit(solution)/shard_map/ppermute | solution.py:353
  3.8 7.9 %collective-permute-start = (bf16[2,80,128]{2,1,0:T(8,128)(2,1)S(1)}, bf16[2,80,128]{2,1,0:T(8,128)(2,1)S(1)}, u32[]{:S(2)}, u32[]{:S(2)}) collective-permute-start(bf16[2,80,128]{2,1,0:T(8,128)(2,1)S(1)} %get-tuple-element.11), channel_id=1, source_target_pairs={{16,0},{24,8},{0,16},{8,24},{48,32},{56,40},{32,48},{40,56},{41,1}... | collective-permute-start | bytes 122888 | tf_op jit(solution)/shard_map/ppermute | solution.py:350
  10.3 5.0 %collective-permute-start.1 = (bf16[2,80,128]{2,1,0:T(8,128)(2,1)S(1)}, bf16[2,80,128]{2,1,0:T(8,128)(2,1)S(1)}, u32[]{:S(2)}, u32[]{:S(2)}) collective-permute-start(bf16[2,80,128]{2,1,0:T(8,128)(2,1)S(1)} %get-tuple-element.11), channel_id=1, source_target_pairs={{8,0},{0,8},{24,16},{16,24},{40,32},{32,40},{56,48},{48,56},{49,1}... | collective-permute-start | bytes 122888 | tf_op jit(solution)/shard_map/ppermute | solution.py:352
  15.3 3.7 %collective-permute-start.6 = (bf16[4,80,128]{2,1,0:T(8,128)(2,1)S(1)}, bf16[4,80,128]{2,1,0:T(8,128)(2,1)S(1)}, u32[]{:S(2)}, u32[]{:S(2)}) collective-permute-start(bf16[4,80,128]{2,1,0:T(8,128)(2,1)S(1)} %maximum_select_fusion.refs_0_), channel_id=1, source_target_pairs={{0,8},{8,0},{16,24},{24,16},{32,40},{40,32},{48,56},{56,48},{1,9},... | collective-permute-start | bytes 245768 | tf_op jit(solution)/shard_map/ppermute | solution.py:356
  16.1 5.4 %collective-permute-start.4 = (bf16[4,80,128]{2,1,0:T(8,128)(2,1)S(1)}, bf16[4,80,128]{2,1,0:T(8,128)(2,1)S(1)}, u32[]{:S(2)}, u32[]{:S(2)}) collective-permute-start(bf16[4,80,128]{2,1,0:T(8,128)(2,1)S(1)} %maximum_select_fusion.refs_0_), channel_id=1, source_target_pairs={{0,6},{2,4},{4,2},{6,0},{1,7},{3,5},{5,3},{7,1},{8,14},{10,12},{12... | collective-permute-start | bytes 245768 | tf_op jit(solution)/shard_map/ppermute | solution.py:357
  18.5 3.6 %collective-permute-start.9 = (bf16[4,80,128]{2,1,0:T(8,128)(2,1)S(1)}, bf16[4,80,128]{2,1,0:T(8,128)(2,1)S(1)}, u32[]{:S(2)}, u32[]{:S(2)}) collective-permute-start(bf16[4,80,128]{2,1,0:T(8,128)(2,1)S(1)} %maximum_select_fusion.refs_0_), channel_id=1, source_target_pairs={{0,2},{2,0},{4,6},{6,4},{1,3},{3,1},{5,7},{7,5},{8,10},{10,8},{12,... | collective-permute-start | bytes 245768 | tf_op jit(solution)/shard_map/ppermute | solution.py:358
  18.9 4.5 %collective-permute-start.7 = (bf16[4,80,128]{2,1,0:T(8,128)(2,1)S(1)}, bf16[4,80,128]{2,1,0:T(8,128)(2,1)S(1)}, u32[]{:S(2)}, u32[]{:S(2)}) collective-permute-start(bf16[4,80,128]{2,1,0:T(8,128)(2,1)S(1)} %collective-permute-done.6.refs_1_), channel_id=1, source_target_pairs={{0,6},{2,4},{4,2},{6,0},{1,7},{3,5},{5,3},{7,1},{8,14},{10,12},{12... | collective-permute-start | bytes 245768 | tf_op jit(solution)/shard_map/ppermute | solution.py:362
  21.4 3.3 %collective-permute-start.10 = (bf16[4,80,128]{2,1,0:T(8,128)(2,1)S(1)}, bf16[4,80,128]{2,1,0:T(8,128)(2,1)S(1)}, u32[]{:S(2)}, u32[]{:S(2)}) collective-permute-start(bf16[4,80,128]{2,1,0:T(8,128)(2,1)S(1)} %collective-permute-done.6.refs_1_), channel_id=1, source_target_pairs={{0,2},{2,0},{4,6},{6,4},{1,3},{3,1},{5,7},{7,5},{8,10},{10,8},{12,... | collective-permute-start | bytes 245768 | tf_op jit(solution)/shard_map/ppermute | solution.py:363
  24.8 8.4 %collective-permute-start.11 = (bf16[16,80,128]{2,1,0:T(8,128)(2,1)S(1)}, bf16[16,80,128]{2,1,0:T(8,128)(2,1)S(1)}, u32[]{:S(2)}, u32[]{:S(2)}) collective-permute-start(bf16[16,80,128]{2,1,0:T(8,128)(2,1)S(1)} %pad_maximum_fusion), channel_id=1, source_target_pairs={{0,1},{1,0},{2,3},{3,2},{4,5},{5,4},{6,7},{7,6},{8,9},{9,8},{10,11... | collective-permute-start | bytes 983048 | tf_op jit(solution)/shard_map/ppermute | solution.py:370
  24.9 6.2 %collective-permute-start.12 = (bf16[8,80,128]{2,1,0:T(8,128)(2,1)S(1)}, bf16[8,80,128]{2,1,0:T(8,128)(2,1)S(1)}, u32[]{:S(2)}, u32[]{:S(2)}) collective-permute-start(bf16[8,80,128]{2,1,0:T(8,128)(2,1)S(1)} %pad_maximum_fusion.1), channel_id=1, source_target_pairs={{0,1},{1,0},{2,3},{3,2},{4,5},{5,4},{6,7},{7,6},{8,9},{9,8},{10,11... | collective-permute-start | bytes 491528 | tf_op jit(solution)/shard_map/ppermute | solution.py:364
  25.5 9.8 %collective-permute-start.5 = (bf16[4,80,128]{2,1,0:T(8,128)(2,1)S(1)}, bf16[4,80,128]{2,1,0:T(8,128)(2,1)S(1)}, u32[]{:S(2)}, u32[]{:S(2)}) collective-permute-start(bf16[4,80,128]{2,1,0:T(8,128)(2,1)S(1)} %collective-permute-done.4.refs_0_), channel_id=1, source_target_pairs={{0,2},{2,0},{4,6},{6,4},{1,3},{3,1},{5,7},{7,5},{8,10},{10,8},{12,... | collective-permute-start | bytes 245768 | tf_op jit(solution)/shard_map/ppermute | solution.py:365
  25.5 9.8 %collective-permute-start.8 = (bf16[4,80,128]{2,1,0:T(8,128)(2,1)S(1)}, bf16[4,80,128]{2,1,0:T(8,128)(2,1)S(1)}, u32[]{:S(2)}, u32[]{:S(2)}) collective-permute-start(bf16[4,80,128]{2,1,0:T(8,128)(2,1)S(1)} %collective-permute-done.7.refs_1_), channel_id=1, source_target_pairs={{0,2},{2,0},{4,6},{6,4},{1,3},{3,1},{5,7},{7,5},{8,10},{10,8},{12,... | collective-permute-start | bytes 245768 | tf_op jit(solution)/shard_map/ppermute | solution.py:369
  26.9 3.7 %collective-permute-start.3 = (f32[2,8,128]{2,1,0:T(8,128)S(1)}, f32[2,8,128]{2,1,0:T(8,128)S(1)}, u32[]{:S(2)}, u32[]{:S(2)}) collective-permute-start(f32[2,8,128]{2,1,0:T(8,128)S(1)} %pad_maximum_fusion.2.sites_ref), channel_id=1, source_target_pairs={{0,192},{64,128},{128,64},{192,0},{1,193},{65,129},{129,65},{193,1... | collective-permute-start | bytes 24584 | tf_op jit(solution)/shard_map/ppermute | solution.py:359
  35.3 4.2 %collective-permute-start.13 = (bf16[8,80,128]{2,1,0:T(8,128)(2,1)S(1)}, bf16[8,80,128]{2,1,0:T(8,128)(2,1)S(1)}, u32[]{:S(2)}, u32[]{:S(2)}) collective-permute-start(bf16[8,80,128]{2,1,0:T(8,128)(2,1)S(1)} %constant_dynamic-update-slice_fusion.refs_0_), channel_id=1, source_target_pairs={{0,1},{1,0},{2,3},{3,2},{4,5},{5,4},{6,7},{7,6},{8,9},{9,8},{10,11... | collective-permute-start | bytes 491528 | tf_op jit(solution)/shard_map/ppermute | solution.py:376
  41.0 6.3 %collective-permute-start.14 = (f32[4,64,128]{2,1,0:T(8,128)S(1)}, f32[4,64,128]{2,1,0:T(8,128)S(1)}, u32[]{:S(2)}, u32[]{:S(2)}) collective-permute-start(f32[4,64,128]{2,1,0:T(8,128)S(1)} %bitcast.10), channel_id=1, source_target_pairs={{0,192},{64,128},{128,64},{192,0},{1,193},{65,129},{129,65},{193,1... | collective-permute-start | bytes 393224 | tf_op jit(solution)/shard_map/ppermute | solution.py:391
  44.0 3.5 %collective-permute-start.16 = (f32[4,32,128]{2,1,0:T(8,128)S(1)}, f32[4,32,128]{2,1,0:T(8,128)S(1)}, u32[]{:S(2)}, u32[]{:S(2)}) collective-permute-start(f32[4,32,128]{2,1,0:T(8,128)S(1)} %bitcast.12), channel_id=1, source_target_pairs={{0,64},{64,0},{128,192},{192,128},{1,65},{65,1},{129,193},{193,129... | collective-permute-start | bytes 196616 | tf_op jit(solution)/shard_map/ppermute | solution.py:392
  47.3 4.6 %collective-permute-start.15 = (f32[4,64,128]{2,1,0:T(8,128)S(1)}, f32[4,64,128]{2,1,0:T(8,128)S(1)}, u32[]{:S(2)}, u32[]{:S(2)}) collective-permute-start(f32[4,64,128]{2,1,0:T(8,128)S(1)} %exchange_add.2.refs_1_), channel_id=1, source_target_pairs={{0,64},{64,0},{128,192},{192,128},{1,65},{65,1},{129,193},{193,129... | collective-permute-start | bytes 393224 | tf_op jit(solution)/shard_map/ppermute | solution.py:393
  47.5 4.4 %collective-permute-start.17 = (f32[4,32,128]{2,1,0:T(8,128)S(1)}, f32[4,32,128]{2,1,0:T(8,128)S(1)}, u32[]{:S(2)}, u32[]{:S(2)}) collective-permute-start(f32[4,32,128]{2,1,0:T(8,128)S(1)} %exchange_add.3.refs_3_), channel_id=1, source_target_pairs={{0,192},{64,128},{128,64},{192,0},{1,193},{65,129},{129,65},{193,1... | collective-permute-start | bytes 196616 | tf_op jit(solution)/shard_map/ppermute | solution.py:394
  52.0 3.2 %collective-permute-start.18 = (f32[1,128]{1,0:T(1,128)S(1)}, f32[1,128]{1,0:T(1,128)S(1)}, u32[]{:S(2)}, u32[]{:S(2)}) collective-permute-start(f32[1,128]{1,0:T(1,128)S(1)} %shard_map.123), channel_id=1, source_target_pairs={{0,1},{1,0},{2,3},{3,2},{4,5},{5,4},{6,7},{7,6},{8,9},{9,8},{10,11... | collective-permute-start | bytes 1544 | tf_op jit(solution)/shard_map/ppermute | solution.py:399
  55.2 3.9 %collective-permute-start.19 = (f32[1,128]{1,0:T(1,128)S(1)}, f32[1,128]{1,0:T(1,128)S(1)}, u32[]{:S(2)}, u32[]{:S(2)}) collective-permute-start(f32[1,128]{1,0:T(1,128)S(1)} %add.18), channel_id=1, source_target_pairs={{2,0},{0,2},{6,4},{4,6},{5,1},{7,3},{1,5},{3,7},{10,8},{8,10},{14,... | collective-permute-start | bytes 1544 | tf_op jit(solution)/shard_map/ppermute | solution.py:401
  56.0 3.6 %collective-permute-start.20 = (f32[1,128]{1,0:T(1,128)S(1)}, f32[1,128]{1,0:T(1,128)S(1)}, u32[]{:S(2)}, u32[]{:S(2)}) collective-permute-start(f32[1,128]{1,0:T(1,128)S(1)} %add.18), channel_id=1, source_target_pairs={{2,0},{0,2},{6,4},{4,6},{7,1},{5,3},{3,5},{1,7},{10,8},{8,10},{14,... | collective-permute-start | bytes 1544 | tf_op jit(solution)/shard_map/ppermute | solution.py:403
  59.6 1.2 %collective-permute-start.21 = (f32[1,128]{1,0:T(1,128)S(1)}, f32[1,128]{1,0:T(1,128)S(1)}, u32[]{:S(2)}, u32[]{:S(2)}) collective-permute-start(f32[1,128]{1,0:T(1,128)S(1)} %fusion.2), channel_id=1, source_target_pairs={{0,1},{1,0},{2,3},{3,2},{4,5},{5,4},{6,7},{7,6},{8,9},{9,8},{10,11... | collective-permute-start | bytes 1544 | tf_op jit(solution)/shard_map/ppermute | solution.py:405
  60.8 2.4 %collective-permute-start.22 = (f32[1,128]{1,0:T(1,128)S(1)}, f32[1,128]{1,0:T(1,128)S(1)}, u32[]{:S(2)}, u32[]{:S(2)}) collective-permute-start(f32[1,128]{1,0:T(1,128)S(1)} %add.20), channel_id=1, source_target_pairs={{1,9},{9,1},{17,25},{25,17},{33,41},{41,33},{49,57},{57,49},{0,8},... | collective-permute-start | bytes 1544 | tf_op jit(solution)/shard_map/ppermute | solution.py:409
  63.2 3.3 %collective-permute-start.23 = (f32[1,128]{1,0:T(1,128)S(1)}, f32[1,128]{1,0:T(1,128)S(1)}, u32[]{:S(2)}, u32[]{:S(2)}) collective-permute-start(f32[1,128]{1,0:T(1,128)S(1)} %add.21), channel_id=1, source_target_pairs={{1,17},{9,25},{17,1},{25,9},{33,49},{41,57},{49,33},{57,41},{0,8},... | collective-permute-start | bytes 1544 | tf_op jit(solution)/shard_map/ppermute | solution.py:409
  66.5 3.6 %collective-permute-start.24 = (f32[1,128]{1,0:T(1,128)S(1)}, f32[1,128]{1,0:T(1,128)S(1)}, u32[]{:S(2)}, u32[]{:S(2)}) collective-permute-start(f32[1,128]{1,0:T(1,128)S(1)} %add.22), channel_id=1, source_target_pairs={{1,57},{9,49},{17,41},{25,33},{33,25},{41,17},{49,9},{57,1},{0,8},... | collective-permute-start | bytes 1544 | tf_op jit(solution)/shard_map/ppermute | solution.py:409
  70.1 2.3 %collective-permute-start.25 = (f32[1,128]{1,0:T(1,128)S(1)}, f32[1,128]{1,0:T(1,128)S(1)}, u32[]{:S(2)}, u32[]{:S(2)}) collective-permute-start(f32[1,128]{1,0:T(1,128)S(1)} %add.23), channel_id=1, source_target_pairs={{0,1},{1,0},{2,3},{3,2},{4,5},{5,4},{6,7},{7,6},{8,9},{9,8},{10,11... | collective-permute-start | bytes 1544 | tf_op jit(solution)/shard_map/ppermute | solution.py:410

commit v7 on v6

--- a/solution.py
+++ b/solution.py
@@ -22,7 +22,7 @@
 FRAME_STRIDE = 40
 NEAR_ORDER = (1, 0, 3, 2)
 FAR_ORDER = (2, 3, 0, 1)
-FIRST_SHARE = 8
+FIRST_SHARE = 7
 
 
 def shares(width):
@@ -277,7 +277,7 @@
 
 def residuals(block, pix_ref, low_ref, low_got_ref, high_ref, high_got_ref):
     width = low_ref.shape[1] + high_ref.shape[1]
-    parts = (low_ref, low_got_ref, NEAR_ORDER), (high_ref, high_got_ref, FAR_ORDER)
+    parts = (low_ref, low_got_ref, FAR_ORDER), (high_ref, high_got_ref, NEAR_ORDER)
     for (start, size, offset), (mine, got, order) in zip(shares(width), parts):
         value = mine[block] + got[order[block]]
         here = slice(offset + block * size, offset + (block + 1) * size)
@@ -388,10 +388,10 @@
     first_share, second_share = shares(own_pixels)
     low = last_product(first_share)
     high = last_product(second_share)
-    low = exchange_add(low, lax.ppermute(low, "y", far_pairs), FAR_ORDER)
-    high = exchange_add(high, lax.ppermute(high, "y", near_pairs), NEAR_ORDER)
-    low_got = lax.ppermute(low, "y", near_pairs)
-    high_got = lax.ppermute(high, "y", far_pairs)
+    low = exchange_add(low, lax.ppermute(low, "y", near_pairs), NEAR_ORDER)
+    high = exchange_add(high, lax.ppermute(high, "y", far_pairs), FAR_ORDER)
+    low_got = lax.ppermute(low, "y", far_pairs)
+    high_got = lax.ppermute(high, "y", near_pairs)
     sums = pix, low, low_got, high, high_got
     own_sum = on_sums(square_sum_kernel, vmem_array((1, LANES), jnp.float32), sums)
     shape = jax.ShapeDtypeStruct((own_pixels, LANES), jnp.float32)

time: 73.1 us -> 72.2 us (0.988)
  waiting for transfers between devices: 24.8 us -> 24 us
  transfers between devices with their start and end apart: 26 -> 26, of which waited for: 18 -> 17; matrix products, arithmetic and copies ran while one was open for 0% -> 0% of each run, Pallas kernels for 12% -> 12%
where the time goes in v7:
time: 72.2 us; the launch traced here: 72.1 us
  starting transfers between devices  35.3 us (49%)
  waiting for transfers between devices  24 us (33%)
  Pallas kernels  11.3 us (16%)
  between operations  0.8 us (1%)
    pallas_call x5, Pallas kernels, unit_product(): pl.pallas_call(functools.partial(unit_kernel, units, len(parts), acc is n...  8.76 us
    ppermute x1, starting transfers between devices, per_device(): first = lax.ppermute(piece, ('z', 'pix'), meets)  6.46 us
    ppermute x3, waiting for transfers between devices, per_device(): total = total + lax.ppermute(total, ('z', 'pix'), meets)  5.04 us
    ppermute x3, starting transfers between devices, per_device(): total = total + lax.ppermute(total, ('z', 'pix'), meets)  4.33 us
    ppermute x1, waiting for transfers between devices, per_device(): second = lax.ppermute(piece, ('z', 'pix'), meets)  3.6 us
    ppermute x1, waiting for transfers between devices, per_device(): high_got = lax.ppermute(high, 'y', near_pairs)  3.57 us
    ppermute x1, starting transfers between devices, per_device(): far_a = lax.ppermute(four, 'x', far_pairs)  2.48 us
    ppermute x1, starting transfers between devices, per_device(): far_b = lax.ppermute(four_got, 'x', far_pairs)  2.48 us
  transfers between devices with their start and end apart: 26, of which 17 were waited for; matrix products, arithmetic and copies ran while one was open for 0% of the time, Pallas kernels for 12%

profile of v7, /device:TPU:1, one launch (start us, length us, event | category | flops | bytes accessed | tf_op | source)
XLA Modules:
  0.0 72.1 jit_solution(8570003216558778414)
XLA Ops:
  0.6 1.0 %prepare.1 = (bf16[2,80,128]{2,1,0:T(8,128)(2,1)S(1)}, f32[1,8,128]{2,1,0:T(8,128)S(1)}) custom-call(f32[16]{0:T(128)} %strike_ref.1, f32[16]{0:T(128)} %dip_ref.1, f32[2,48]{1,0:T(2,128)} %pos_ref.1, f32[1,48]{1,0:T(1,128)} %bitcast.15, s32[1,48]{1,0:T(1,128)} %bitcast.16, bf16[3,48,128]{2,1,0:T(8,128)(2,1)} %bitcast.14, f32[2,96]{1,0:T(2,128)} %pixel_ref.1, ...), custom_call_target="tpu_custom_call" | custom-call | tf_op jit(solution)/shard_map/prepare/pallas_call | solution.py:125
  1.6 2.2 %collective-permute-start.2 = (f32[1,8,128]{2,1,0:T(8,128)S(1)}, f32[1,8,128]{2,1,0:T(8,128)S(1)}, u32[]{:S(2)}, u32[]{:S(2)}) collective-permute-start(f32[1,8,128]{2,1,0:T(8,128)S(1)} %get-tuple-element.12), channel_id=1, source_target_pairs={{0,64},{64,0},{128,192},{192,128},{1,65},{65,1},{129,193},{193,129... | collective-permute-start | bytes 12296 | tf_op jit(solution)/shard_map/ppermute | solution.py:353
  3.8 6.5 %collective-permute-start = (bf16[2,80,128]{2,1,0:T(8,128)(2,1)S(1)}, bf16[2,80,128]{2,1,0:T(8,128)(2,1)S(1)}, u32[]{:S(2)}, u32[]{:S(2)}) collective-permute-start(bf16[2,80,128]{2,1,0:T(8,128)(2,1)S(1)} %get-tuple-element.11), channel_id=1, source_target_pairs={{16,0},{24,8},{0,16},{8,24},{48,32},{56,40},{32,48},{40,56},{41,1}... | collective-permute-start | bytes 122888 | tf_op jit(solution)/shard_map/ppermute | solution.py:350
  10.3 0.3 collective-permute-start.1
  10.5 0.0 collective-permute-done.2
  10.6 1.1 %collective-permute-done = bf16[2,80,128]{2,1,0:T(8,128)(2,1)S(1)} collective-permute-done((bf16[2,80,128]{2,1,0:T(8,128)(2,1)S(1)}, bf16[2,80,128]{2,1,0:T(8,128)(2,1)S(1)}, u32[]{:S(2)}, u32[]{:S(2)}) %collective-permute-start) | collective-permute-done | bytes 40992 | tf_op jit(solution)/shard_map/ppermute | solution.py:350
  11.7 3.6 %collective-permute-done.1 = bf16[2,80,128]{2,1,0:T(8,128)(2,1)S(1)} collective-permute-done((bf16[2,80,128]{2,1,0:T(8,128)(2,1)S(1)}, bf16[2,80,128]{2,1,0:T(8,128)(2,1)S(1)}, u32[]{:S(2)}, u32[]{:S(2)}) %collective-permute-start.1) | collective-permute-done | bytes 40992 | tf_op jit(solution)/shard_map/ppermute | solution.py:352
  15.3 0.8 %collective-permute-start.6 = (bf16[4,80,128]{2,1,0:T(8,128)(2,1)S(1)}, bf16[4,80,128]{2,1,0:T(8,128)(2,1)S(1)}, u32[]{:S(2)}, u32[]{:S(2)}) collective-permute-start(bf16[4,80,128]{2,1,0:T(8,128)(2,1)S(1)} %maximum_select_fusion.refs_0_), channel_id=1, source_target_pairs={{0,8},{8,0},{16,24},{24,16},{32,40},{40,32},{48,56},{56,48},{1,9},... | collective-permute-start | bytes 245768 | tf_op jit(solution)/shard_map/ppermute | solution.py:356
  16.1 2.5 %collective-permute-start.4 = (bf16[4,80,128]{2,1,0:T(8,128)(2,1)S(1)}, bf16[4,80,128]{2,1,0:T(8,128)(2,1)S(1)}, u32[]{:S(2)}, u32[]{:S(2)}) collective-permute-start(bf16[4,80,128]{2,1,0:T(8,128)(2,1)S(1)} %maximum_select_fusion.refs_0_), channel_id=1, source_target_pairs={{0,6},{2,4},{4,2},{6,0},{1,7},{3,5},{5,3},{7,1},{8,14},{10,12},{12... | collective-permute-start | bytes 245768 | tf_op jit(solution)/shard_map/ppermute | solution.py:357
  18.5 0.0 collective-permute-start.9
  18.5 0.4 collective-permute-done.6.refs_1_
  18.9 2.5 %collective-permute-start.7 = (bf16[4,80,128]{2,1,0:T(8,128)(2,1)S(1)}, bf16[4,80,128]{2,1,0:T(8,128)(2,1)S(1)}, u32[]{:S(2)}, u32[]{:S(2)}) collective-permute-start(bf16[4,80,128]{2,1,0:T(8,128)(2,1)S(1)} %collective-permute-done.6.refs_1_), channel_id=1, source_target_pairs={{0,6},{2,4},{4,2},{6,0},{1,7},{3,5},{5,3},{7,1},{8,14},{10,12},{12... | collective-permute-start | bytes 245768 | tf_op jit(solution)/shard_map/ppermute | solution.py:362
  21.4 0.0 collective-permute-start.10
  21.4 0.0 collective-permute-done.4.refs_0_
  21.4 0.7 collective-permute-done.9.refs_0_
  22.1 1.3 %collective-permute-done.7.refs_1_ = bf16[4,80,128]{2,1,0:T(8,128)(2,1)S(1)} collective-permute-done((bf16[4,80,128]{2,1,0:T(8,128)(2,1)S(1)}, bf16[4,80,128]{2,1,0:T(8,128)(2,1)S(1)}, u32[]{:S(2)}, u32[]{:S(2)}) %collective-permute-start.7) | collective-permute-done | bytes 81952 | tf_op jit(solution)/shard_map/ppermute | solution.py:362
  23.5 1.3 %collective-permute-done.10.refs_1_ = bf16[4,80,128]{2,1,0:T(8,128)(2,1)S(1)} collective-permute-done((bf16[4,80,128]{2,1,0:T(8,128)(2,1)S(1)}, bf16[4,80,128]{2,1,0:T(8,128)(2,1)S(1)}, u32[]{:S(2)}, u32[]{:S(2)}) %collective-permute-start.10) | collective-permute-done | bytes 81952 | tf_op jit(solution)/shard_map/ppermute | solution.py:363
  24.8 0.1 collective-permute-start.11
  24.9 0.6 collective-permute-start.12
  25.5 0.0 collective-permute-start.5
  25.5 1.5 %collective-permute-start.8 = (bf16[4,80,128]{2,1,0:T(8,128)(2,1)S(1)}, bf16[4,80,128]{2,1,0:T(8,128)(2,1)S(1)}, u32[]{:S(2)}, u32[]{:S(2)}) collective-permute-start(bf16[4,80,128]{2,1,0:T(8,128)(2,1)S(1)} %collective-permute-done.7.refs_1_), channel_id=1, source_target_pairs={{0,2},{2,0},{4,6},{6,4},{1,3},{3,1},{5,7},{7,5},{8,10},{10,8},{12,... | collective-permute-start | bytes 245768 | tf_op jit(solution)/shard_map/ppermute | solution.py:369
  26.9 1.9 %collective-permute-start.3 = (f32[2,8,128]{2,1,0:T(8,128)S(1)}, f32[2,8,128]{2,1,0:T(8,128)S(1)}, u32[]{:S(2)}, u32[]{:S(2)}) collective-permute-start(f32[2,8,128]{2,1,0:T(8,128)S(1)} %pad_maximum_fusion.2.sites_ref), channel_id=1, source_target_pairs={{0,192},{64,128},{128,64},{192,0},{1,193},{65,129},{129,65},{193,1... | collective-permute-start | bytes 24584 | tf_op jit(solution)/shard_map/ppermute | solution.py:359
  28.8 0.5 pixel_columns.2.refs_0_
  29.3 1.4 %collective-permute-done.3.sites_ref = f32[2,8,128]{2,1,0:T(8,128)S(1)} collective-permute-done((f32[2,8,128]{2,1,0:T(8,128)S(1)}, f32[2,8,128]{2,1,0:T(8,128)S(1)}, u32[]{:S(2)}, u32[]{:S(2)}) %collective-permute-start.3) | collective-permute-done | bytes 8224 | tf_op jit(solution)/shard_map/ppermute | solution.py:359
  30.7 0.5 pixel_columns.3.pix_ref.refs_0_
  31.1 0.0 collective-permute-done.12.refs_2_
  31.1 2.1 %unit_product.5.refs_3_ = f32[384,128]{1,0:T(8,128)S(1)} custom-call(f32[7,384,128]{2,1,0:T(8,128)S(1)} %pixel_columns.3.pix_ref.refs_0_, bf16[4,80,128]{2,1,0:T(8,128)(2,1)S(1)} %maximum_select_fusion.refs_0_, bf16[4,80,128]{2,1,0:T(8,128)(2,1)S(1)} %collective-permute-done.6.refs_1_, bf16[8,80,128]{2,1,0:T(8,128)(2,1)S(1)} %collective-permute-done.12.refs_2_), custom_call_target="tpu_custom_call" | custom-call | flops 147456000 | bytes 524288 | tf_op jit(solution)/shard_map/unit_product/pallas_call | solution.py:266
  33.2 0.0 collective-permute-done.11.refs_2_
  33.2 2.1 %unit_product.6.refs_3_ = f32[384,128]{1,0:T(8,128)S(1)} custom-call(f32[7,384,128]{2,1,0:T(8,128)S(1)} %pixel_columns.3.pix_ref.refs_0_, bf16[4,80,128]{2,1,0:T(8,128)(2,1)S(1)} %collective-permute-done.9.refs_0_, bf16[4,80,128]{2,1,0:T(8,128)(2,1)S(1)} %collective-permute-done.10.refs_1_, bf16[16,80,128]{2,1,0:T(8,128)(2,1)S(1)} %collective-permute-done.11.refs_2_, ...), custom_call_target="tpu_custom_call" | custom-call | flops 147456000 | bytes 524288 | tf_op jit(solution)/shard_map/unit_product/pallas_call | solution.py:266
  35.3 0.0 collective-permute-done.5
  35.3 0.0 collective-permute-done.8
  35.3 2.1 %collective-permute-start.13 = (bf16[8,80,128]{2,1,0:T(8,128)(2,1)S(1)}, bf16[8,80,128]{2,1,0:T(8,128)(2,1)S(1)}, u32[]{:S(2)}, u32[]{:S(2)}) collective-permute-start(bf16[8,80,128]{2,1,0:T(8,128)(2,1)S(1)} %constant_dynamic-update-slice_fusion.refs_0_), channel_id=1, source_target_pairs={{0,1},{1,0},{2,3},{3,2},{4,5},{5,4},{6,7},{7,6},{8,9},{9,8},{10,11... | collective-permute-start | bytes 491528 | tf_op jit(solution)/shard_map/ppermute | solution.py:376
  37.4 2.1 %unit_product.7.refs_2_ = f32[384,128]{1,0:T(8,128)S(1)} custom-call(f32[7,384,128]{2,1,0:T(8,128)S(1)} %pixel_columns.3.pix_ref.refs_0_, bf16[4,80,128]{2,1,0:T(8,128)(2,1)S(1)} %collective-permute-done.4.refs_0_, bf16[4,80,128]{2,1,0:T(8,128)(2,1)S(1)} %collective-permute-done.7.refs_1_, bf16[16,80,128]{2,1,0:T(8,128)(2,1)S(1)} %collective-permute-done.11.refs_2_, ...), custom_call_target="tpu_custom_call" | custom-call | flops 147456000 | bytes 524288 | tf_op jit(solution)/shard_map/unit_product/pallas_call | solution.py:266
  39.5 0.0 collective-permute-done.13.refs_1_
  39.5 1.4 %unit_product.8 = f32[224,128]{1,0:T(8,128)S(1)} custom-call(f32[7,384,128]{2,1,0:T(8,128)S(1)} %pixel_columns.3.pix_ref.refs_0_, bf16[8,80,128]{2,1,0:T(8,128)(2,1)S(1)} %constant_dynamic-update-slice_fusion.refs_0_, bf16[8,80,128]{2,1,0:T(8,128)(2,1)S(1)} %collective-permute-done.13.refs_1_, f32[384,128]{1,0:T(8,128)S(1)} %unit_product.7.refs_2_), custom_call_target="tpu_custom_call" | custom-call | flops 86016000 | bytes 524288 | tf_op jit(solution)/shard_map/unit_product/pallas_call | solution.py:266
  40.9 0.1 collective-permute-start.14
  41.0 1.2 %unit_product.9 = f32[160,128]{1,0:T(8,128)S(1)} custom-call(f32[7,384,128]{2,1,0:T(8,128)S(1)} %pixel_columns.3.pix_ref.refs_0_, bf16[8,80,128]{2,1,0:T(8,128)(2,1)S(1)} %constant_dynamic-update-slice_fusion.refs_0_, bf16[8,80,128]{2,1,0:T(8,128)(2,1)S(1)} %collective-permute-done.13.refs_1_, f32[384,128]{1,0:T(8,128)S(1)} %unit_product.7.refs_2_), custom_call_target="tpu_custom_call" | custom-call | flops 61440000 | bytes 524288 | tf_op jit(solution)/shard_map/unit_product/pallas_call | solution.py:266
  42.2 2.0 %collective-permute-start.16 = (f32[4,40,128]{2,1,0:T(8,128)S(1)}, f32[4,40,128]{2,1,0:T(8,128)S(1)}, u32[]{:S(2)}, u32[]{:S(2)}) collective-permute-start(f32[4,40,128]{2,1,0:T(8,128)S(1)} %bitcast.12), channel_id=1, source_target_pairs={{0,192},{64,128},{128,64},{192,0},{1,193},{65,129},{129,65},{193,1... | collective-permute-start | bytes 245768 | tf_op jit(solution)/shard_map/ppermute | solution.py:392
  44.1 1.5 %collective-permute-done.14.got_ref = f32[4,56,128]{2,1,0:T(8,128)S(1)} collective-permute-done((f32[4,56,128]{2,1,0:T(8,128)S(1)}, f32[4,56,128]{2,1,0:T(8,128)S(1)}, u32[]{:S(2)}, u32[]{:S(2)}) %collective-permute-start.14) | collective-permute-done | bytes 114720 | tf_op jit(solution)/shard_map/ppermute | solution.py:391
  45.7 2.0 %collective-permute-start.15 = (f32[4,56,128]{2,1,0:T(8,128)S(1)}, f32[4,56,128]{2,1,0:T(8,128)S(1)}, u32[]{:S(2)}, u32[]{:S(2)}) collective-permute-start(f32[4,56,128]{2,1,0:T(8,128)S(1)} %exchange_add.2.refs_1_), channel_id=1, source_target_pairs={{0,192},{64,128},{128,64},{192,0},{1,193},{65,129},{129,65},{193,1... | collective-permute-start | bytes 344072 | tf_op jit(solution)/shard_map/ppermute | solution.py:393
  47.7 0.0 collective-permute-done.16.got_ref
  47.7 0.1 collective-permute-start.17
  47.8 3.6 %collective-permute-done.17.refs_4_ = f32[4,40,128]{2,1,0:T(8,128)S(1)} collective-permute-done((f32[4,40,128]{2,1,0:T(8,128)S(1)}, f32[4,40,128]{2,1,0:T(8,128)S(1)}, u32[]{:S(2)}, u32[]{:S(2)}) %collective-permute-start.17) | collective-permute-done | bytes 81952 | tf_op jit(solution)/shard_map/ppermute | solution.py:394
  51.3 0.0 collective-permute-done.15.refs_2_
  51.3 0.1 shard_map.123
  51.4 2.1 %collective-permute-start.18 = (f32[1,128]{1,0:T(1,128)S(1)}, f32[1,128]{1,0:T(1,128)S(1)}, u32[]{:S(2)}, u32[]{:S(2)}) collective-permute-start(f32[1,128]{1,0:T(1,128)S(1)} %shard_map.123), channel_id=1, source_target_pairs={{0,1},{1,0},{2,3},{3,2},{4,5},{5,4},{6,7},{7,6},{8,9},{9,8},{10,11... | collective-permute-start | bytes 1544 | tf_op jit(solution)/shard_map/ppermute | solution.py:399
  53.5 0.8 %collective-permute-done.18 = f32[1,128]{1,0:T(1,128)S(1)} collective-permute-done((f32[1,128]{1,0:T(1,128)S(1)}, f32[1,128]{1,0:T(1,128)S(1)}, u32[]{:S(2)}, u32[]{:S(2)}) %collective-permute-start.18) | collective-permute-done | bytes 544 | tf_op jit(solution)/shard_map/ppermute | solution.py:399
  54.3 0.8 %collective-permute-start.19 = (f32[1,128]{1,0:T(1,128)S(1)}, f32[1,128]{1,0:T(1,128)S(1)}, u32[]{:S(2)}, u32[]{:S(2)}) collective-permute-start(f32[1,128]{1,0:T(1,128)S(1)} %add.18), channel_id=1, source_target_pairs={{2,0},{0,2},{6,4},{4,6},{5,1},{7,3},{1,5},{3,7},{10,8},{8,10},{14,... | collective-permute-start | bytes 1544 | tf_op jit(solution)/shard_map/ppermute | solution.py:401
  55.1 1.6 %collective-permute-start.20 = (f32[1,128]{1,0:T(1,128)S(1)}, f32[1,128]{1,0:T(1,128)S(1)}, u32[]{:S(2)}, u32[]{:S(2)}) collective-permute-start(f32[1,128]{1,0:T(1,128)S(1)} %add.18), channel_id=1, source_target_pairs={{2,0},{0,2},{6,4},{4,6},{7,1},{5,3},{3,5},{1,7},{10,8},{8,10},{14,... | collective-permute-start | bytes 1544 | tf_op jit(solution)/shard_map/ppermute | solution.py:403
  56.7 1.5 %collective-permute-done.19 = f32[1,128]{1,0:T(1,128)S(1)} collective-permute-done((f32[1,128]{1,0:T(1,128)S(1)}, f32[1,128]{1,0:T(1,128)S(1)}, u32[]{:S(2)}, u32[]{:S(2)}) %collective-permute-start.19) | collective-permute-done | bytes 544 | tf_op jit(solution)/shard_map/ppermute | solution.py:401
  58.2 0.5 collective-permute-done.20
  58.7 0.0 collective-permute-start.21
  58.7 1.2 %collective-permute-done.21 = f32[1,128]{1,0:T(1,128)S(1)} collective-permute-done((f32[1,128]{1,0:T(1,128)S(1)}, f32[1,128]{1,0:T(1,128)S(1)}, u32[]{:S(2)}, u32[]{:S(2)}) %collective-permute-start.21) | collective-permute-done | bytes 544 | tf_op jit(solution)/shard_map/ppermute | solution.py:405
  59.9 0.7 collective-permute-start.22
  60.6 1.7 %collective-permute-done.22 = f32[1,128]{1,0:T(1,128)S(1)} collective-permute-done((f32[1,128]{1,0:T(1,128)S(1)}, f32[1,128]{1,0:T(1,128)S(1)}, u32[]{:S(2)}, u32[]{:S(2)}) %collective-permute-start.22) | collective-permute-done | bytes 544 | tf_op jit(solution)/shard_map/ppermute | solution.py:409
  62.3 1.0 %collective-permute-start.23 = (f32[1,128]{1,0:T(1,128)S(1)}, f32[1,128]{1,0:T(1,128)S(1)}, u32[]{:S(2)}, u32[]{:S(2)}) collective-permute-start(f32[1,128]{1,0:T(1,128)S(1)} %add.21), channel_id=1, source_target_pairs={{1,17},{9,25},{17,1},{25,9},{33,49},{41,57},{49,33},{57,41},{0,8},... | collective-permute-start | bytes 1544 | tf_op jit(solution)/shard_map/ppermute | solution.py:409
  63.3 2.3 %collective-permute-done.23 = f32[1,128]{1,0:T(1,128)S(1)} collective-permute-done((f32[1,128]{1,0:T(1,128)S(1)}, f32[1,128]{1,0:T(1,128)S(1)}, u32[]{:S(2)}, u32[]{:S(2)}) %collective-permute-start.23) | collective-permute-done | bytes 544 | tf_op jit(solution)/shard_map/ppermute | solution.py:409
  65.6 2.6 %collective-permute-start.24 = (f32[1,128]{1,0:T(1,128)S(1)}, f32[1,128]{1,0:T(1,128)S(1)}, u32[]{:S(2)}, u32[]{:S(2)}) collective-permute-start(f32[1,128]{1,0:T(1,128)S(1)} %add.22), channel_id=1, source_target_pairs={{1,57},{9,49},{17,41},{25,33},{33,25},{41,17},{49,9},{57,1},{0,8},... | collective-permute-start | bytes 1544 | tf_op jit(solution)/shard_map/ppermute | solution.py:409
  68.2 1.0 %collective-permute-done.24 = f32[1,128]{1,0:T(1,128)S(1)} collective-permute-done((f32[1,128]{1,0:T(1,128)S(1)}, f32[1,128]{1,0:T(1,128)S(1)}, u32[]{:S(2)}, u32[]{:S(2)}) %collective-permute-start.24) | collective-permute-done | bytes 544 | tf_op jit(solution)/shard_map/ppermute | solution.py:409
  69.3 1.5 %collective-permute-start.25 = (f32[1,128]{1,0:T(1,128)S(1)}, f32[1,128]{1,0:T(1,128)S(1)}, u32[]{:S(2)}, u32[]{:S(2)}) collective-permute-start(f32[1,128]{1,0:T(1,128)S(1)} %add.23), channel_id=1, source_target_pairs={{0,1},{1,0},{2,3},{3,2},{4,5},{5,4},{6,7},{7,6},{8,9},{9,8},{10,11... | collective-permute-start | bytes 1544 | tf_op jit(solution)/shard_map/ppermute | solution.py:410
  70.8 0.6 shard_map.122
  71.4 0.2 collective-permute-done.25
  71.6 0.5 fusion.1
  (14 shorter events, 0.1 us)
Async XLA Ops:
  1.6 8.9 %collective-permute-start.2 = (f32[1,8,128]{2,1,0:T(8,128)S(1)}, f32[1,8,128]{2,1,0:T(8,128)S(1)}, u32[]{:S(2)}, u32[]{:S(2)}) collective-permute-start(f32[1,8,128]{2,1,0:T(8,128)S(1)} %get-tuple-element.12), channel_id=1, source_target_pairs={{0,64},{64,0},{128,192},{192,128},{1,65},{65,1},{129,193},{193,129... | collective-permute-start | bytes 12296 | tf_op jit(solution)/shard_map/ppermute | solution.py:353
  3.8 7.9 %collective-permute-start = (bf16[2,80,128]{2,1,0:T(8,128)(2,1)S(1)}, bf16[2,80,128]{2,1,0:T(8,128)(2,1)S(1)}, u32[]{:S(2)}, u32[]{:S(2)}) collective-permute-start(bf16[2,80,128]{2,1,0:T(8,128)(2,1)S(1)} %get-tuple-element.11), channel_id=1, source_target_pairs={{16,0},{24,8},{0,16},{8,24},{48,32},{56,40},{32,48},{40,56},{41,1}... | collective-permute-start | bytes 122888 | tf_op jit(solution)/shard_map/ppermute | solution.py:350
  10.3 5.0 %collective-permute-start.1 = (bf16[2,80,128]{2,1,0:T(8,128)(2,1)S(1)}, bf16[2,80,128]{2,1,0:T(8,128)(2,1)S(1)}, u32[]{:S(2)}, u32[]{:S(2)}) collective-permute-start(bf16[2,80,128]{2,1,0:T(8,128)(2,1)S(1)} %get-tuple-element.11), channel_id=1, source_target_pairs={{8,0},{0,8},{24,16},{16,24},{40,32},{32,40},{56,48},{48,56},{49,1}... | collective-permute-start | bytes 122888 | tf_op jit(solution)/shard_map/ppermute | solution.py:352
  15.3 3.7 %collective-permute-start.6 = (bf16[4,80,128]{2,1,0:T(8,128)(2,1)S(1)}, bf16[4,80,128]{2,1,0:T(8,128)(2,1)S(1)}, u32[]{:S(2)}, u32[]{:S(2)}) collective-permute-start(bf16[4,80,128]{2,1,0:T(8,128)(2,1)S(1)} %maximum_select_fusion.refs_0_), channel_id=1, source_target_pairs={{0,8},{8,0},{16,24},{24,16},{32,40},{40,32},{48,56},{56,48},{1,9},... | collective-permute-start | bytes 245768 | tf_op jit(solution)/shard_map/ppermute | solution.py:356
  16.1 5.4 %collective-permute-start.4 = (bf16[4,80,128]{2,1,0:T(8,128)(2,1)S(1)}, bf16[4,80,128]{2,1,0:T(8,128)(2,1)S(1)}, u32[]{:S(2)}, u32[]{:S(2)}) collective-permute-start(bf16[4,80,128]{2,1,0:T(8,128)(2,1)S(1)} %maximum_select_fusion.refs_0_), channel_id=1, source_target_pairs={{0,6},{2,4},{4,2},{6,0},{1,7},{3,5},{5,3},{7,1},{8,14},{10,12},{12... | collective-permute-start | bytes 245768 | tf_op jit(solution)/shard_map/ppermute | solution.py:357
  18.5 3.6 %collective-permute-start.9 = (bf16[4,80,128]{2,1,0:T(8,128)(2,1)S(1)}, bf16[4,80,128]{2,1,0:T(8,128)(2,1)S(1)}, u32[]{:S(2)}, u32[]{:S(2)}) collective-permute-start(bf16[4,80,128]{2,1,0:T(8,128)(2,1)S(1)} %maximum_select_fusion.refs_0_), channel_id=1, source_target_pairs={{0,2},{2,0},{4,6},{6,4},{1,3},{3,1},{5,7},{7,5},{8,10},{10,8},{12,... | collective-permute-start | bytes 245768 | tf_op jit(solution)/shard_map/ppermute | solution.py:358
  18.9 4.5 %collective-permute-start.7 = (bf16[4,80,128]{2,1,0:T(8,128)(2,1)S(1)}, bf16[4,80,128]{2,1,0:T(8,128)(2,1)S(1)}, u32[]{:S(2)}, u32[]{:S(2)}) collective-permute-start(bf16[4,80,128]{2,1,0:T(8,128)(2,1)S(1)} %collective-permute-done.6.refs_1_), channel_id=1, source_target_pairs={{0,6},{2,4},{4,2},{6,0},{1,7},{3,5},{5,3},{7,1},{8,14},{10,12},{12... | collective-permute-start | bytes 245768 | tf_op jit(solution)/shard_map/ppermute | solution.py:362
  21.4 3.3 %collective-permute-start.10 = (bf16[4,80,128]{2,1,0:T(8,128)(2,1)S(1)}, bf16[4,80,128]{2,1,0:T(8,128)(2,1)S(1)}, u32[]{:S(2)}, u32[]{:S(2)}) collective-permute-start(bf16[4,80,128]{2,1,0:T(8,128)(2,1)S(1)} %collective-permute-done.6.refs_1_), channel_id=1, source_target_pairs={{0,2},{2,0},{4,6},{6,4},{1,3},{3,1},{5,7},{7,5},{8,10},{10,8},{12,... | collective-permute-start | bytes 245768 | tf_op jit(solution)/shard_map/ppermute | solution.py:363
  24.8 8.4 %collective-permute-start.11 = (bf16[16,80,128]{2,1,0:T(8,128)(2,1)S(1)}, bf16[16,80,128]{2,1,0:T(8,128)(2,1)S(1)}, u32[]{:S(2)}, u32[]{:S(2)}) collective-permute-start(bf16[16,80,128]{2,1,0:T(8,128)(2,1)S(1)} %pad_maximum_fusion), channel_id=1, source_target_pairs={{0,1},{1,0},{2,3},{3,2},{4,5},{5,4},{6,7},{7,6},{8,9},{9,8},{10,11... | collective-permute-start | bytes 983048 | tf_op jit(solution)/shard_map/ppermute | solution.py:370
  24.9 6.2 %collective-permute-start.12 = (bf16[8,80,128]{2,1,0:T(8,128)(2,1)S(1)}, bf16[8,80,128]{2,1,0:T(8,128)(2,1)S(1)}, u32[]{:S(2)}, u32[]{:S(2)}) collective-permute-start(bf16[8,80,128]{2,1,0:T(8,128)(2,1)S(1)} %pad_maximum_fusion.1), channel_id=1, source_target_pairs={{0,1},{1,0},{2,3},{3,2},{4,5},{5,4},{6,7},{7,6},{8,9},{9,8},{10,11... | collective-permute-start | bytes 491528 | tf_op jit(solution)/shard_map/ppermute | solution.py:364
  25.5 9.8 %collective-permute-start.5 = (bf16[4,80,128]{2,1,0:T(8,128)(2,1)S(1)}, bf16[4,80,128]{2,1,0:T(8,128)(2,1)S(1)}, u32[]{:S(2)}, u32[]{:S(2)}) collective-permute-start(bf16[4,80,128]{2,1,0:T(8,128)(2,1)S(1)} %collective-permute-done.4.refs_0_), channel_id=1, source_target_pairs={{0,2},{2,0},{4,6},{6,4},{1,3},{3,1},{5,7},{7,5},{8,10},{10,8},{12,... | collective-permute-start | bytes 245768 | tf_op jit(solution)/shard_map/ppermute | solution.py:365
  25.5 9.8 %collective-permute-start.8 = (bf16[4,80,128]{2,1,0:T(8,128)(2,1)S(1)}, bf16[4,80,128]{2,1,0:T(8,128)(2,1)S(1)}, u32[]{:S(2)}, u32[]{:S(2)}) collective-permute-start(bf16[4,80,128]{2,1,0:T(8,128)(2,1)S(1)} %collective-permute-done.7.refs_1_), channel_id=1, source_target_pairs={{0,2},{2,0},{4,6},{6,4},{1,3},{3,1},{5,7},{7,5},{8,10},{10,8},{12,... | collective-permute-start | bytes 245768 | tf_op jit(solution)/shard_map/ppermute | solution.py:369
  26.9 3.7 %collective-permute-start.3 = (f32[2,8,128]{2,1,0:T(8,128)S(1)}, f32[2,8,128]{2,1,0:T(8,128)S(1)}, u32[]{:S(2)}, u32[]{:S(2)}) collective-permute-start(f32[2,8,128]{2,1,0:T(8,128)S(1)} %pad_maximum_fusion.2.sites_ref), channel_id=1, source_target_pairs={{0,192},{64,128},{128,64},{192,0},{1,193},{65,129},{129,65},{193,1... | collective-permute-start | bytes 24584 | tf_op jit(solution)/shard_map/ppermute | solution.py:359
  35.3 4.2 %collective-permute-start.13 = (bf16[8,80,128]{2,1,0:T(8,128)(2,1)S(1)}, bf16[8,80,128]{2,1,0:T(8,128)(2,1)S(1)}, u32[]{:S(2)}, u32[]{:S(2)}) collective-permute-start(bf16[8,80,128]{2,1,0:T(8,128)(2,1)S(1)} %constant_dynamic-update-slice_fusion.refs_0_), channel_id=1, source_target_pairs={{0,1},{1,0},{2,3},{3,2},{4,5},{5,4},{6,7},{7,6},{8,9},{9,8},{10,11... | collective-permute-start | bytes 491528 | tf_op jit(solution)/shard_map/ppermute | solution.py:376
  40.9 4.8 %collective-permute-start.14 = (f32[4,56,128]{2,1,0:T(8,128)S(1)}, f32[4,56,128]{2,1,0:T(8,128)S(1)}, u32[]{:S(2)}, u32[]{:S(2)}) collective-permute-start(f32[4,56,128]{2,1,0:T(8,128)S(1)} %bitcast.10), channel_id=1, source_target_pairs={{0,64},{64,0},{128,192},{192,128},{1,65},{65,1},{129,193},{193,129... | collective-permute-start | bytes 344072 | tf_op jit(solution)/shard_map/ppermute | solution.py:391
  42.2 5.5 %collective-permute-start.16 = (f32[4,40,128]{2,1,0:T(8,128)S(1)}, f32[4,40,128]{2,1,0:T(8,128)S(1)}, u32[]{:S(2)}, u32[]{:S(2)}) collective-permute-start(f32[4,40,128]{2,1,0:T(8,128)S(1)} %bitcast.12), channel_id=1, source_target_pairs={{0,192},{64,128},{128,64},{192,0},{1,193},{65,129},{129,65},{193,1... | collective-permute-start | bytes 245768 | tf_op jit(solution)/shard_map/ppermute | solution.py:392
  45.7 5.7 %collective-permute-start.15 = (f32[4,56,128]{2,1,0:T(8,128)S(1)}, f32[4,56,128]{2,1,0:T(8,128)S(1)}, u32[]{:S(2)}, u32[]{:S(2)}) collective-permute-start(f32[4,56,128]{2,1,0:T(8,128)S(1)} %exchange_add.2.refs_1_), channel_id=1, source_target_pairs={{0,192},{64,128},{128,64},{192,0},{1,193},{65,129},{129,65},{193,1... | collective-permute-start | bytes 344072 | tf_op jit(solution)/shard_map/ppermute | solution.py:393
  47.7 3.7 %collective-permute-start.17 = (f32[4,40,128]{2,1,0:T(8,128)S(1)}, f32[4,40,128]{2,1,0:T(8,128)S(1)}, u32[]{:S(2)}, u32[]{:S(2)}) collective-permute-start(f32[4,40,128]{2,1,0:T(8,128)S(1)} %exchange_add.3.refs_3_), channel_id=1, source_target_pairs={{0,64},{64,0},{128,192},{192,128},{1,65},{65,1},{129,193},{193,129... | collective-permute-start | bytes 245768 | tf_op jit(solution)/shard_map/ppermute | solution.py:394
  51.4 2.9 %collective-permute-start.18 = (f32[1,128]{1,0:T(1,128)S(1)}, f32[1,128]{1,0:T(1,128)S(1)}, u32[]{:S(2)}, u32[]{:S(2)}) collective-permute-start(f32[1,128]{1,0:T(1,128)S(1)} %shard_map.123), channel_id=1, source_target_pairs={{0,1},{1,0},{2,3},{3,2},{4,5},{5,4},{6,7},{7,6},{8,9},{9,8},{10,11... | collective-permute-start | bytes 1544 | tf_op jit(solution)/shard_map/ppermute | solution.py:399
  54.3 3.9 %collective-permute-start.19 = (f32[1,128]{1,0:T(1,128)S(1)}, f32[1,128]{1,0:T(1,128)S(1)}, u32[]{:S(2)}, u32[]{:S(2)}) collective-permute-start(f32[1,128]{1,0:T(1,128)S(1)} %add.18), channel_id=1, source_target_pairs={{2,0},{0,2},{6,4},{4,6},{5,1},{7,3},{1,5},{3,7},{10,8},{8,10},{14,... | collective-permute-start | bytes 1544 | tf_op jit(solution)/shard_map/ppermute | solution.py:401
  55.1 3.6 %collective-permute-start.20 = (f32[1,128]{1,0:T(1,128)S(1)}, f32[1,128]{1,0:T(1,128)S(1)}, u32[]{:S(2)}, u32[]{:S(2)}) collective-permute-start(f32[1,128]{1,0:T(1,128)S(1)} %add.18), channel_id=1, source_target_pairs={{2,0},{0,2},{6,4},{4,6},{7,1},{5,3},{3,5},{1,7},{10,8},{8,10},{14,... | collective-permute-start | bytes 1544 | tf_op jit(solution)/shard_map/ppermute | solution.py:403
  58.7 1.2 %collective-permute-start.21 = (f32[1,128]{1,0:T(1,128)S(1)}, f32[1,128]{1,0:T(1,128)S(1)}, u32[]{:S(2)}, u32[]{:S(2)}) collective-permute-start(f32[1,128]{1,0:T(1,128)S(1)} %fusion.2), channel_id=1, source_target_pairs={{0,1},{1,0},{2,3},{3,2},{4,5},{5,4},{6,7},{7,6},{8,9},{9,8},{10,11... | collective-permute-start | bytes 1544 | tf_op jit(solution)/shard_map/ppermute | solution.py:405
  59.9 2.4 %collective-permute-start.22 = (f32[1,128]{1,0:T(1,128)S(1)}, f32[1,128]{1,0:T(1,128)S(1)}, u32[]{:S(2)}, u32[]{:S(2)}) collective-permute-start(f32[1,128]{1,0:T(1,128)S(1)} %add.20), channel_id=1, source_target_pairs={{1,9},{9,1},{17,25},{25,17},{33,41},{41,33},{49,57},{57,49},{0,8},... | collective-permute-start | bytes 1544 | tf_op jit(solution)/shard_map/ppermute | solution.py:409
  62.3 3.3 %collective-permute-start.23 = (f32[1,128]{1,0:T(1,128)S(1)}, f32[1,128]{1,0:T(1,128)S(1)}, u32[]{:S(2)}, u32[]{:S(2)}) collective-permute-start(f32[1,128]{1,0:T(1,128)S(1)} %add.21), channel_id=1, source_target_pairs={{1,17},{9,25},{17,1},{25,9},{33,49},{41,57},{49,33},{57,41},{0,8},... | collective-permute-start | bytes 1544 | tf_op jit(solution)/shard_map/ppermute | solution.py:409
  65.6 3.6 %collective-permute-start.24 = (f32[1,128]{1,0:T(1,128)S(1)}, f32[1,128]{1,0:T(1,128)S(1)}, u32[]{:S(2)}, u32[]{:S(2)}) collective-permute-start(f32[1,128]{1,0:T(1,128)S(1)} %add.22), channel_id=1, source_target_pairs={{1,57},{9,49},{17,41},{25,33},{33,25},{41,17},{49,9},{57,1},{0,8},... | collective-permute-start | bytes 1544 | tf_op jit(solution)/shard_map/ppermute | solution.py:409
  69.3 2.3 %collective-permute-start.25 = (f32[1,128]{1,0:T(1,128)S(1)}, f32[1,128]{1,0:T(1,128)S(1)}, u32[]{:S(2)}, u32[]{:S(2)}) collective-permute-start(f32[1,128]{1,0:T(1,128)S(1)} %add.23), channel_id=1, source_target_pairs={{0,1},{1,0},{2,3},{3,2},{4,5},{5,4},{6,7},{7,6},{8,9},{9,8},{10,11... | collective-permute-start | bytes 1544 | tf_op jit(solution)/shard_map/ppermute | solution.py:410
